TPU v7x, 512 devices: a whole 4x8x8 slice. The times are simulated.
512 devices in a mesh: views: 32 (over y, z_lo), rows: 16 (over z_hi, x, core).
Axes of the slice: x: 4, y: 8, z: 8 (z_hi: 2, z_lo: 4; z = z_hi * 4 + z_lo), core: 2. Of those that a mesh axis runs over, the one named last changes fastest.
Arguments:
- sinogram: bfloat16 [32, 256, 2048], P(None, 'views'), may hold values from -32 to 6176
- view_shift: int32 [256], P('views'), may hold values from -48 to 48
- conv_one: float32 [9, 32], replicated, may hold values from -2 to 2
- bias_one: float32 [32], replicated, may hold values from -3 to 3
- conv_two: bfloat16 [32, 288], replicated, may hold values from -0.375 to 0.375
- bias_two: float32 [32], replicated, may hold values from -3 to 3
Outputs:
- denoised: bfloat16 [32, 32, 64, 2048], P('views', None, 'rows')
All inputs are finite; a program needn't handle non-finite values.
Results may differ from a plain program's by a relative error of at most 0.008.
Values may be sent and summed in bfloat16 or wider, within the bound.
No kernel may reach another device: no remote copies, remote signals or barrier semaphores. Data moves between devices by JAX's collectives and lax.ppermute only.
A program may use at most 64 MiB of HBM per device.

v0:
```python
import math

import jax
import jax.numpy as jnp
from jax import lax
from jax.experimental import pallas as pl
from jax.experimental.pallas import tpu as pltpu
from jax.sharding import PartitionSpec as P

BINS = 2048
WIDTH = 2048
MARGIN = 384
CHAN = 32
ROW_DEV = 4
GROUP = 4
BLOCK = 256
BLOCKS = BINS // BLOCK
CENTER = (BINS - 1) / 2.0 + MARGIN
FIRST_WIN = 4
WINDOWS = 38
TILES = WIDTH // 128
ROW_SETS = 3
VIEW_STEP = 8


def ramp_kernel(table_ref):
    def one_block(block, carry):
        row = lax.broadcasted_iota(jnp.int32, (BLOCK, BLOCK), 0)
        col = lax.broadcasted_iota(jnp.int32, (BLOCK, BLOCK), 1)
        offset = col - row + (block - (BLOCKS - 1)) * BLOCK
        place = offset.astype(jnp.float32)
        guarded = jnp.maximum(place * place, 1.0)
        odd = (offset & 1) == 1
        values = jnp.where(odd, -1.0 / (math.pi * math.pi * guarded), 0.0)
        values = jnp.where(offset == 0, 0.25, values)
        high = values.astype(jnp.bfloat16)
        low = (values - high.astype(jnp.float32)).astype(jnp.bfloat16)
        where = pl.ds(pl.multiple_of(block * BLOCK, BLOCK), BLOCK)
        table_ref[0:BLOCK, where] = high
        table_ref[BLOCK : 2 * BLOCK, where] = low
        return carry

    lax.fori_loop(0, 2 * BLOCKS - 1, one_block, 0)


def ramp_blocks():
    return pl.pallas_call(
        ramp_kernel,
        out_shape=jax.ShapeDtypeStruct((2 * BLOCK, (2 * BLOCKS - 1) * BLOCK), jnp.bfloat16),
        out_specs=pl.BlockSpec(memory_space=pltpu.VMEM),
        cost_estimate=pl.CostEstimate(flops=20_000_000, bytes_accessed=4_000_000, transcendentals=0),
        name="ramp",
    )()


def backproject_kernel(
    first_ref,
    x_ref,
    cos_ref,
    sin_ref,
    ramp_ref,
    out_ref,
    filt_ref,
    slope_ref,
    level_ref,
    bin_ref,
    center_ref,
    where_ref,
    acc_ref,
    where_smem,
    sem,
):
    views = x_ref.shape[0]
    first_y = first_ref[0]
    lane = lax.broadcasted_iota(jnp.int32, (views, 128), 1)
    lane_f = lane.astype(jnp.float32)

    cosine = cos_ref[...]
    sine = sin_ref[...]
    center = CENTER + x_ref[:, BINS : BINS + 128].astype(jnp.float32)
    center_ref[...] = center
    tile_x = (lane & 15).astype(jnp.float32) * 128.0 - (WIDTH - 1) / 2.0
    set_y = first_y + 8.0 * (lane >> 4).astype(jnp.float32)
    lowest = jnp.minimum(tile_x * cosine, (tile_x + 127.0) * cosine) + set_y * sine + center
    window = ((lowest - 0.25) * (1.0 / 64.0)).astype(jnp.int32) - FIRST_WIN
    window = jnp.clip(window, 0, WINDOWS - 3)
    view = lax.broadcasted_iota(jnp.int32, (views, 128), 0)
    where_ref[...] = window * views + view
    to_smem = pltpu.make_async_copy(where_ref, where_smem, sem)
    to_smem.start()

    for step in range(2 * BLOCKS - 1):
        delta = (step + 1) // 2 * (1 if step % 2 else -1)
        low, high = max(0, -delta), min(BLOCKS, BLOCKS - delta)
        left = jnp.concatenate(
            [x_ref[:, BLOCK * block : BLOCK * block + BLOCK] for block in range(low, high)], axis=0
        )
        left = jnp.concatenate([left, left], axis=1)
        right = ramp_ref[:, BLOCK * (delta + BLOCKS - 1) : BLOCK * (delta + BLOCKS)]
        part = jnp.dot(left, right, preferred_element_type=jnp.float32)
        rows = slice(views * (low + delta), views * (high + delta))
        if delta == 0:
            filt_ref[rows, :] = part
        else:
            filt_ref[rows, :] += part

    zero = jnp.zeros((views, 128), jnp.float32)
    margin = MARGIN // 128

    def filtered(block):
        place = block - margin
        if place < 0 or place >= BINS // 128:
            return zero
        half = 128 * (place % 2)
        piece = filt_ref[views * (place // 2) : views * (place // 2) + views, half : half + 128]
        return piece.astype(jnp.bfloat16).astype(jnp.float32)

    def turned(piece):
        return pltpu.roll(piece, 127, 1)

    def block_tables(block, piece, piece_turned, next_turned):
        after = jnp.where(lane < 127, piece_turned, next_turned)
        slope = after - piece
        bins = lane_f + 128.0 * block
        return slope, piece - bins * slope, bins + 1.0

    first_block = FIRST_WIN // 2
    piece = filtered(first_block)
    piece_turned = turned(piece)
    before = None
    for block in range(first_block, (FIRST_WIN + WINDOWS) // 2 + 1):
        following = filtered(block + 1)
        following_turned = turned(following)
        now = block_tables(block, piece, piece_turned, following_turned)
        for ref, value, old in zip((slope_ref, level_ref, bin_ref), now, before or now):
            row = (2 * block - FIRST_WIN) * views
            if before is not None:
                ref[row - views : row, :] = jnp.where(lane >= 64, old, value)
            if 2 * block < FIRST_WIN + WINDOWS:
                ref[row : row + views, :] = value
        before = now
        piece, piece_turned = following, following_turned

    acc_ref[...] = jnp.zeros_like(acc_ref)
    to_smem.wait()

    lane_one = lax.broadcasted_iota(jnp.int32, (8, 128), 1).astype(jnp.float32)
    sub_one = lax.broadcasted_iota(jnp.int32, (8, 128), 0).astype(jnp.float32)
    per_set = views // VIEW_STEP

    def steps(step, carry):
        row_set = step // per_set
        first_view = (step % per_set) * VIEW_STEP
        rows_y = sub_one + (first_y + 8.0 * row_set.astype(jnp.float32))
        totals = [acc_ref[row_set, :, 128 * tile : 128 * tile + 128] for tile in range(TILES)]
        for view_off in range(VIEW_STEP):
            view = first_view + view_off
            cos_v = jnp.broadcast_to(cos_ref[pl.ds(view, 1), :], (8, 128))
            sin_v = jnp.broadcast_to(sin_ref[pl.ds(view, 1), :], (8, 128))
            base = rows_y * sin_v + jnp.broadcast_to(center_ref[pl.ds(view, 1), :], (8, 128))
            stride = cos_v * 128.0
            middle = (lane_one + 0.5) * cos_v + base
            middle_low = jnp.minimum(0.5 * cos_v, 127.5 * cos_v) + base
            for direction in (1, -1):
                place, place_low = middle, middle_low
                tiles = range(TILES // 2, TILES) if direction == 1 else range(TILES // 2 - 1, -1, -1)
                for tile in tiles:
                    if direction == 1 and tile > TILES // 2:
                        place, place_low = place + stride, place_low + stride
                    elif direction == -1:
                        place, place_low = place - stride, place_low - stride
                    row = where_smem[view, row_set * TILES + tile]
                    near = pl.ds(row, 1)
                    far = pl.ds(row + 2 * views, 1)
                    pick = bin_ref[near, :] > place_low
                    slopes = jnp.where(pick, slope_ref[near, :], slope_ref[far, :])
                    levels = jnp.where(pick, level_ref[near, :], level_ref[far, :])
                    index = place.astype(jnp.int32) & 127
                    slope = jnp.take_along_axis(slopes, index, axis=1, mode="promise_in_bounds")
                    level = jnp.take_along_axis(levels, index, axis=1, mode="promise_in_bounds")
                    totals[tile] = totals[tile] + (level + place * slope)
        for tile in range(TILES):
            acc_ref[row_set, :, 128 * tile : 128 * tile + 128] = totals[tile]
        return carry

    lax.fori_loop(0, ROW_SETS * per_set, steps, 0)

    for member in range(GROUP):
        lower = acc_ref[member // 2]
        if member % 2:
            lower = jnp.concatenate([lower[4:8], acc_ref[member // 2 + 1][0:4]], axis=0)
        out_ref[member] = lower.astype(jnp.bfloat16)


def backproject(first_y, lines, cosine, sine, ramp):
    views = lines.shape[0]
    rows = WINDOWS * views
    vmem = pl.BlockSpec(memory_space=pltpu.VMEM)
    return pl.pallas_call(
        backproject_kernel,
        out_shape=jax.ShapeDtypeStruct((GROUP, 8, WIDTH), jnp.bfloat16),
        in_specs=[pl.BlockSpec(memory_space=pltpu.SMEM), vmem, vmem, vmem, vmem],
        out_specs=vmem,
        scratch_shapes=[
            pltpu.VMEM((BLOCKS * views, BLOCK), jnp.float32),
            pltpu.VMEM((rows, 128), jnp.float32),
            pltpu.VMEM((rows, 128), jnp.float32),
            pltpu.VMEM((rows, 128), jnp.float32),
            pltpu.VMEM((views, 128), jnp.float32),
            pltpu.VMEM((views, 128), jnp.int32),
            pltpu.VMEM((ROW_SETS, 8, WIDTH), jnp.float32),
            pltpu.SMEM((views, 128), jnp.int32),
            pltpu.SemaphoreType.DMA(()),
        ],
        cost_estimate=pl.CostEstimate(flops=1_000_000_000, bytes_accessed=6_000_000, transcendentals=0),
        name="backproject",
    )(first_y, lines, cosine, sine, ramp)


def layers_kernel(
    scale,
    image_rows,
    row_ref,
    parts_ref,
    first_ref,
    bias_one_ref,
    second_ref,
    bias_two_ref,
    out_ref,
    image_ref,
    stack_ref,
):
    row_base = row_ref[0]
    image = parts_ref[0].astype(jnp.float32)
    for member in range(1, GROUP):
        image = image + parts_ref[member].astype(jnp.float32)
    image = (image * scale).astype(jnp.bfloat16).astype(jnp.float32)
    row = lax.broadcasted_iota(jnp.int32, image.shape, 0) + (row_base - 2)
    image = jnp.where((row >= 0) & (row < image_rows), image, 0.0)
    column = lax.broadcasted_iota(jnp.int32, image.shape, 1)
    left = jnp.where(column == 0, 0.0, pltpu.roll(image, 1, 1))
    right = jnp.where(column == WIDTH - 1, 0.0, pltpu.roll(image, WIDTH - 1, 1))
    three = jnp.concatenate([left, image, right], axis=0).astype(jnp.bfloat16)
    image_ref[...] = jnp.concatenate([three, three, three], axis=0)

    weights = first_ref[...]
    high = weights.astype(jnp.bfloat16)
    rest = weights - high.astype(jnp.float32)
    middle = rest.astype(jnp.bfloat16)
    low = (rest - middle.astype(jnp.float32)).astype(jnp.bfloat16)
    weights = jnp.concatenate([high, middle, low], axis=1)

    count = CHAN * (ROW_DEV + 2)
    for tile in range(0, WIDTH, 256):
        hidden = jnp.dot(weights, image_ref[:, tile : tile + 256], preferred_element_type=jnp.float32)
        hidden = jnp.maximum(hidden + bias_one_ref[...], 0.0)
        top = jnp.where(row_base > 0, hidden[0:CHAN], 0.0)
        bottom = jnp.where(row_base + ROW_DEV < image_rows, hidden[count - CHAN : count], 0.0)
        hidden = jnp.concatenate([top, hidden[CHAN : count - CHAN], bottom], axis=0)
        stack_ref[:, tile : tile + 256] = hidden

    middle_rows = stack_ref[...]
    column = lax.broadcasted_iota(jnp.int32, middle_rows.shape, 1)
    before = jnp.where(column == 0, 0.0, pltpu.roll(middle_rows, 1, 1)).astype(jnp.bfloat16)
    after = jnp.where(column == WIDTH - 1, 0.0, pltpu.roll(middle_rows, WIDTH - 1, 1)).astype(jnp.bfloat16)
    stacked = jnp.concatenate([before, middle_rows.astype(jnp.bfloat16), after], axis=0)
    mixed = jnp.dot(second_ref[...], stacked, preferred_element_type=jnp.float32)
    mixed = jnp.maximum(mixed + bias_two_ref[...], 0.0)
    out_ref[...] = mixed.reshape(CHAN, ROW_DEV, WIDTH).astype(jnp.bfloat16)[None]


def layers(row_base, parts, first, bias_one, second, bias_two, scale, image_rows):
    vmem = pl.BlockSpec(memory_space=pltpu.VMEM)

    def body(*refs):
        layers_kernel(scale, image_rows, *refs)

    return pl.pallas_call(
        body,
        out_shape=jax.ShapeDtypeStruct((1, CHAN, ROW_DEV, WIDTH), jnp.bfloat16),
        in_specs=[pl.BlockSpec(memory_space=pltpu.SMEM)] + [vmem] * 5,
        out_specs=vmem,
        scratch_shapes=[
            pltpu.VMEM((72, WIDTH), jnp.bfloat16),
            pltpu.VMEM((CHAN * (ROW_DEV + 2), WIDTH), jnp.float32),
        ],
        cost_estimate=pl.CostEstimate(flops=500_000_000, bytes_accessed=1_000_000, transcendentals=0),
        name="layers",
    )(row_base, parts, first, bias_one, second, bias_two)


def first_matrix(conv_one):
    taps = conv_one.reshape(3, 3, CHAN)
    rows = []
    for row in range(ROW_DEV + 2):
        padded = jnp.pad(taps, ((row, ROW_DEV + 1 - row), (0, 0), (0, 0)))
        rows.append(jnp.transpose(padded, (2, 1, 0)))
    return jnp.stack(rows).reshape(CHAN * (ROW_DEV + 2), 24)


def second_matrix(conv_two):
    taps = conv_two.reshape(CHAN, 3, 3, CHAN)
    rows = []
    for row in range(ROW_DEV):
        padded = jnp.pad(taps, ((0, 0), (row, ROW_DEV - 1 - row), (0, 0), (0, 0)))
        rows.append(jnp.transpose(padded, (0, 2, 1, 3)))
    return jnp.stack(rows, axis=1).reshape(CHAN * ROW_DEV, 3 * (ROW_DEV + 2) * CHAN)


def local(sinogram, view_shift, conv_one, bias_one, conv_two, bias_two):
    sheets, view_count, detector = sinogram.shape
    row_groups = lax.axis_size("rows")
    view_groups = lax.axis_size("views")
    views_total = view_count * view_groups
    image_rows = ROW_DEV * row_groups
    share = view_count // GROUP
    row_index = lax.axis_index("rows")
    member = row_index % GROUP

    mine = lax.dynamic_slice_in_dim(sinogram, member * share, share, 1)
    shift = lax.dynamic_slice_in_dim(view_shift, member * share, share, 0).astype(jnp.bfloat16)
    shift = jnp.broadcast_to(shift[None, :, None], (sheets, share, 128))
    sent = jnp.concatenate([mine, shift], axis=2)
    lines = lax.all_to_all(sent, "views", 0, 0, tiled=True)
    lines = lines.reshape(view_groups * share, detector + 128)

    view = jnp.arange(view_groups * share, dtype=jnp.int32)
    view = view // share * view_count + member * share + view % share
    angle = view.astype(jnp.float32) * (math.pi / views_total)
    cosine = jnp.broadcast_to(jnp.cos(angle)[:, None], (view_groups * share, 128))
    sine = jnp.broadcast_to(jnp.sin(angle)[:, None], (view_groups * share, 128))
    first_row = (row_index - member) * ROW_DEV - 2
    first_y = first_row.astype(jnp.float32) - (image_rows - 1) / 2.0

    partial_rows = backproject(first_y.reshape(1), lines, cosine, sine, ramp_blocks())
    groups = [[GROUP * base + item for item in range(GROUP)] for base in range(row_groups // GROUP)]
    parts = lax.all_to_all(partial_rows, "rows", 0, 0, tiled=True, axis_index_groups=groups)

    row_base = (row_index * ROW_DEV).astype(jnp.int32).reshape(1)
    wide_one = jnp.tile(bias_one, ROW_DEV + 2)[:, None]
    wide_two = jnp.repeat(bias_two, ROW_DEV)[:, None]
    return layers(
        row_base,
        parts,
        first_matrix(conv_one),
        wide_one,
        second_matrix(conv_two),
        wide_two,
        math.pi / views_total,
        image_rows,
    )


def solution(mesh):
    return jax.shard_map(
        local,
        mesh=mesh,
        in_specs=(P(None, "views", None), P("views"), P(), P(), P(), P()),
        out_specs=P("views", None, "rows", None),
        check_vma=False,
    )
```

profile of v0, /device:TPU:1, one launch (start us, length us, event | category | flops | bytes accessed | tf_op | source)
XLA Modules:
  0.0 67.2 jit_solution(1689106418939034967)
XLA Ops:
  0.0 1.2 %copy-done = bf16[32,8,2048]{2,1,0:T(8,128)(2,1)S(1)} copy-done((bf16[32,8,2048]{2,1,0:T(8,128)(2,1)S(1)}, bf16[32,8,2048]{2,1,0:T(8,128)(2,1)}, u32[]{:S(2)}) %copy-start) | copy-done | bytes 1048600
  1.2 0.3 constant_dynamic-slice_fusion
  1.6 0.7 %dynamic-slice_convert_fusion = bf16[2]{0:T(256)(128)(2,1)S(1)} fusion(s32[8]{0:T(128)} %param.7, s32[]{:T(128)S(6)} %select_n.37), kind=kLoop, calls=%fused_computation.16 | loop fusion | flops 2 | bytes 16 | tf_op jit(solution)/shard_map/convert_element_type | solution.py:321
  2.4 0.9 %copy.41 = bf16[32,2,2176]{2,1,0:T(2,128)(2,1)} copy(bf16[32,2,2176]{2,0,1:T(8,128)(2,1)S(1)} %pad_maximum_fusion.1) | data formatting | bytes 557056 | tf_op jit(solution)/shard_map/concatenate | solution.py:323
  3.4 13.5 %all-to-all-start = ((bf16[32,2,2176]{2,1,0:T(2,128)(2,1)}), bf16[32,2,2176]{2,1,0:T(2,128)(2,1)S(1)}, u32[]{:S(2)}, u32[]{:S(2)}) async-start(bf16[32,2,2176]{2,1,0:T(2,128)(2,1)} %copy.41), calls=%async_computation | async-start | bytes 557056 | tf_op jit(solution)/shard_map/all_to_all | solution.py:324
  16.8 0.7 %reshape.55 = f32[3,3,32]{2,1,0:T(4,128)S(1)} reshape(f32[9,32]{1,0:T(8,128)} %param.8) | data formatting | bytes 2304 | tf_op jit(solution)/shard_map/reshape | solution.py:293
  17.6 0.1 stack.42
  17.8 0.7 %copy.49.refs_2_ = f32[192,24]{1,0:T(8,128)} copy(f32[192,24]{0,1:T(8,128)S(1)} %reshape.56) | data formatting | bytes 36864 | tf_op jit(solution)/shard_map/reshape | solution.py:298
  18.5 0.8 %reshape.57 = bf16[32,3,3,32]{3,2,1,0:T(4,128)(2,1)S(1)} reshape(bf16[32,288]{1,0:T(8,128)(2,1)} %param.10) | data formatting | bytes 36864 | tf_op jit(solution)/shard_map/reshape | solution.py:302
  19.4 4.1 %ramp.1.ramp_ref = bf16[512,3840]{1,0:T(8,128)(2,1)} custom-call(), custom_call_target="tpu_custom_call" | custom-call | flops 20000000 | bytes 4000000 | tf_op jit(solution)/shard_map/ramp/pallas_call | solution.py:47
  23.5 0.3 pad_bitcast_fusion.3
  23.8 5.1 %all-to-all-done = bf16[32,2,2176]{2,1,0:T(2,128)(2,1)S(1)} async-done(((bf16[32,2,2176]{2,1,0:T(2,128)(2,1)}), bf16[32,2,2176]{2,1,0:T(2,128)(2,1)S(1)}, u32[]{:S(2)}, u32[]{:S(2)}) %all-to-all-start) | async-done | bytes 278560 | tf_op jit(solution)/shard_map/all_to_all | solution.py:324
  28.9 0.8 %reshape.54.x_ref = bf16[64,2176]{1,0:T(8,128)(2,1)} reshape(bf16[32,2,2176]{2,1,0:T(2,128)(2,1)S(1)} %all-to-all-done) | data formatting | bytes 557056 | tf_op jit(solution)/shard_map/reshape | solution.py:325
  29.7 0.7 %broadcast_in_dim.10.sin_ref = f32[64,128]{1,0:T(8,128)} broadcast(f32[64]{0:T(128)S(1)} %get-tuple-element.15), dimensions={0} | broadcast | bytes 33024 | tf_op jit(solution)/shard_map/broadcast_in_dim | solution.py:331
  30.4 0.7 %broadcast_in_dim.9.cos_ref = f32[64,128]{1,0:T(8,128)} broadcast(f32[64]{0:T(128)S(1)} %get-tuple-element.16), dimensions={0} | broadcast | bytes 33024 | tf_op jit(solution)/shard_map/broadcast_in_dim | solution.py:330
  31.1 22.8 %backproject.1 = bf16[4,8,2048]{2,1,0:T(8,128)(2,1)} custom-call(f32[1]{0:T(128)} %bitcast.1.first_ref, bf16[64,2176]{1,0:T(8,128)(2,1)} %reshape.54.x_ref, f32[64,128]{1,0:T(8,128)} %broadcast_in_dim.9.cos_ref, f32[64,128]{1,0:T(8,128)} %broadcast_in_dim.10.sin_ref, bf16[512,3840]{1,0:T(8,128)(2,1)} %ramp.1.ramp_ref), custom_call_target="tpu_custom_call" | custom-call | flops 1000000000 | bytes 6000000 | tf_op jit(solution)/shard_map/backproject/pallas_call | solution.py:199
  53.9 5.8 %all-to-all-start.1 = ((bf16[4,8,2048]{2,1,0:T(8,128)(2,1)}), bf16[4,8,2048]{2,1,0:T(8,128)(2,1)S(1)}, u32[]{:S(2)}, u32[]{:S(2)}) async-start(bf16[4,8,2048]{2,1,0:T(8,128)(2,1)} %backproject.1), calls=%async_computation.1 | async-start | bytes 262144 | tf_op jit(solution)/shard_map/all_to_all | solution.py:337
  59.7 0.8 %pad_maximum_fusion = bf16[32,4,3,6,32]{4,2,3,0,1:T(4,128)(2,1)S(1)} fusion(bf16[32,1,3,6,32]{4,2,3,0,1:T(4,128)(2,1)S(1)} %get-tuple-element.6, bf16[32,1,3,6,32]{4,2,3,0,1:T(4,128)(2,1)S(1)} %get-tuple-element.7, bf16[32,1,3,6,32]{4,2,3,0,1:T(4,128)(2,1)S(1)} %get-tuple-element.8, bf16[32,1,3,6,32]{4,2,3,0,1:T(4,128)(2,1)S(1)} %get-tuple-element.5), kind=kLoop, calls=%fused_computation | loop fusion | flops 221184 | bytes 294912 | tf_op jit(solution)/shard_map/stack | solution.py:307
  60.5 0.2 copy.48
  60.7 1.1 %reshape.58.refs_4_ = bf16[128,576]{1,0:T(8,128)(2,1)} reshape(bf16[32,4,3,6,32]{4,3,2,1,0:T(8,128)(2,1)S(1)} %copy.48) | data formatting | bytes 294912 | tf_op jit(solution)/shard_map/reshape | solution.py:307
  61.8 0.8 %broadcast_in_dim_tile.4.refs_3_ = f32[192,1]{1,0:T(8,128)} reshape(f32[6,32]{1,0:T(8,128)S(1)} %tile.2) | data formatting | bytes 1536 | tf_op jit(solution)/shard_map/broadcast_in_dim;tile | solution.py:340
  62.6 0.7 %broadcast_in_dim_reshape.4.refs_5_ = f32[128,1]{1,0:T(8,128)} reshape(f32[32,4]{1,0:T(8,128)S(1)} %broadcast_in_dim.11) | data formatting | bytes 1024 | tf_op jit(solution)/shard_map/broadcast_in_dim;reshape | solution.py:341
  63.3 0.6 copy-done.1
  64.0 3.2 %layers.1 = bf16[1,32,4,2048]{3,2,1,0:T(4,128)(2,1)} custom-call(s32[1]{0:T(128)} %bitcast.refs_0_, bf16[4,8,2048]{2,1,0:T(8,128)(2,1)} %copy-done.1, f32[192,24]{1,0:T(8,128)} %copy.49.refs_2_, f32[192,1]{1,0:T(8,128)} %broadcast_in_dim_tile.4.refs_3_, bf16[128,576]{1,0:T(8,128)(2,1)} %reshape.58.refs_4_, f32[128,1]{1,0:T(8,128)} %broadcast_in_dim_reshape.4.refs_5_), custom_call_target="tpu_custom_call" | custom-call | flops 500000000 | bytes 1000000 | tf_op jit(solution)/shard_map/layers/pallas_call | solution.py:278
  (16 shorter events, 0.4 us)
Async XLA Ops:
  0.0 1.2 %copy-start = (bf16[32,8,2048]{2,1,0:T(8,128)(2,1)S(1)}, bf16[32,8,2048]{2,1,0:T(8,128)(2,1)}, u32[]{:S(2)}) copy-start(bf16[32,8,2048]{2,1,0:T(8,128)(2,1)} %param.6) | copy-start | bytes 3145732
  3.4 25.6 %all-to-all-start = ((bf16[32,2,2176]{2,1,0:T(2,128)(2,1)}), bf16[32,2,2176]{2,1,0:T(2,128)(2,1)S(1)}, u32[]{:S(2)}, u32[]{:S(2)}) async-start(bf16[32,2,2176]{2,1,0:T(2,128)(2,1)} %copy.41), calls=%async_computation | async-start | bytes 557056 | tf_op jit(solution)/shard_map/all_to_all | solution.py:324
  31.1 30.7 %copy-start.2 = (f32[32]{0:T(128)S(1)}, f32[32]{0:T(128)}, u32[]{:S(2)}) copy-start(f32[32]{0:T(128)} %param.9) | copy-start | bytes 388
  31.1 31.4 %copy-start.3 = (f32[32]{0:T(128)S(1)}, f32[32]{0:T(128)}, u32[]{:S(2)}) copy-start(f32[32]{0:T(128)} %param.11) | copy-start | bytes 388
  53.9 9.4 %all-to-all-start.1 = ((bf16[4,8,2048]{2,1,0:T(8,128)(2,1)}), bf16[4,8,2048]{2,1,0:T(8,128)(2,1)S(1)}, u32[]{:S(2)}, u32[]{:S(2)}) async-start(bf16[4,8,2048]{2,1,0:T(8,128)(2,1)} %backproject.1), calls=%async_computation.1 | async-start | bytes 262144 | tf_op jit(solution)/shard_map/all_to_all | solution.py:337
  63.3 0.6 copy-start.1
where the time goes:
time: 67.7 us; the launch traced here: 67.2 us
  Pallas kernels  30.2 us (45%)
  starting transfers between devices  19.2 us (28%)
  local copies, waits for them, and re-layouts  11 us (16%)
  waiting for transfers between devices  5.12 us (8%)
  other arithmetic  1.61 us (2%)
    pallas_call x1, Pallas kernels, backproject(): pl.pallas_call(backproject_kernel, out_shape=jax.ShapeDtypeStruct((GROUP,...  22.8 us
    all_to_all x1, starting transfers between devices, local(): lines = lax.all_to_all(sent, 'views', 0, 0, tiled=True)  13.5 us
    all_to_all x1, starting transfers between devices, local(): lax.all_to_all(partial_rows, 'rows', 0, 0, tiled=True, axis_index_groups=...  5.75 us
    all_to_all x1, waiting for transfers between devices, local(): lines = lax.all_to_all(sent, 'views', 0, 0, tiled=True)  5.12 us
    pallas_call x1, Pallas kernels, ramp_blocks(): pl.pallas_call(ramp_kernel, out_shape=jax.ShapeDtypeStruct((2 * BLOCK, (2...  4.13 us
    pallas_call x1, Pallas kernels, layers(): pl.pallas_call(body, out_shape=jax.ShapeDtypeStruct((1, CHAN, ROW_DEV, WI...  3.21 us
    unnamed x9, local copies, waits for them, and re-layouts  1.96 us
  transfers between devices with their start and end apart: 2, of which 1 were waited for; matrix products, arithmetic and copies ran while one was open for 10% of the time, Pallas kernels for 6%

commit v1 on v0

--- a/solution.py
+++ b/solution.py
@@ -23,34 +23,138 @@
 VIEW_STEP = 8
 
 
-def ramp_kernel(table_ref):
-    def one_block(block, carry):
-        row = lax.broadcasted_iota(jnp.int32, (BLOCK, BLOCK), 0)
-        col = lax.broadcasted_iota(jnp.int32, (BLOCK, BLOCK), 1)
-        offset = col - row + (block - (BLOCKS - 1)) * BLOCK
+def selection(shape, test):
+    row = lax.broadcasted_iota(jnp.int32, shape, 0)
+    col = lax.broadcasted_iota(jnp.int32, shape, 1)
+    return jnp.where(test(row, col), 1.0, 0.0)
+
+
+def exact_dot(left, right, contract=(1, 0)):
+    return lax.dot_general(
+        left,
+        right,
+        (((contract[0],), (contract[1],)), ((), ())),
+        precision=lax.Precision.HIGHEST,
+        preferred_element_type=jnp.float32,
+    )
+
+
+def column_of(picker, row):
+    return jnp.sum(picker * row, axis=1, keepdims=True)
+
+
+def prepare_kernel(
+    views_total,
+    share,
+    view_count,
+    member_ref,
+    conv_one_ref,
+    bias_one_ref,
+    conv_two_ref,
+    bias_two_ref,
+    table_ref,
+    cos_ref,
+    sin_ref,
+    first_ref,
+    wide_one_ref,
+    second_ref,
+    wide_two_ref,
+):
+    width = (2 * BLOCKS - 1) * BLOCK
+
+    for turn in range(8):
+        row = lax.broadcasted_iota(jnp.int32, (16, width + 128), 0)
+        col = lax.broadcasted_iota(jnp.int32, (16, width + 128), 1)
+        offset = col - row - (128 + 16 * turn + (BLOCKS - 1) * BLOCK)
         place = offset.astype(jnp.float32)
         guarded = jnp.maximum(place * place, 1.0)
         odd = (offset & 1) == 1
-        values = jnp.where(odd, -1.0 / (math.pi * math.pi * guarded), 0.0)
+        values = jnp.where(odd, (-1.0 / (math.pi * math.pi)) / guarded, 0.0)
         values = jnp.where(offset == 0, 0.25, values)
         high = values.astype(jnp.bfloat16)
         low = (values - high.astype(jnp.float32)).astype(jnp.bfloat16)
-        where = pl.ds(pl.multiple_of(block * BLOCK, BLOCK), BLOCK)
-        table_ref[0:BLOCK, where] = high
-        table_ref[BLOCK : 2 * BLOCK, where] = low
-        return carry
-
-    lax.fori_loop(0, 2 * BLOCKS - 1, one_block, 0)
-
-
-def ramp_blocks():
+        for half in range(2):
+            start = 16 * turn + 128 * half
+            cols = slice(128 - 128 * half, 128 - 128 * half + width)
+            table_ref[start : start + 16, :] = high[:, cols]
+            table_ref[BLOCK + start : BLOCK + start + 16, :] = low[:, cols]
+
+    view = lax.broadcasted_iota(jnp.int32, cos_ref.shape, 0)
+    view = view // share * view_count + member_ref[0] * share + view % share
+    angle = view.astype(jnp.float32) * (math.pi / views_total)
+    cos_ref[...] = jnp.cos(angle)
+    sin_ref[...] = jnp.sin(angle)
+
+    rows_one = CHAN * (ROW_DEV + 2)
+    picker = selection((rows_one, CHAN), lambda row, col: (row & (CHAN - 1)) == col)
+    wide_one_ref[...] = column_of(picker, bias_one_ref[...])
+    taps = exact_dot(picker, conv_one_ref[...], (1, 1))
+    weights = jnp.zeros((rows_one, 24), jnp.float32)
+    for item in range(3):
+        moved = exact_dot(taps, selection((9, 24), lambda row, col: row == 3 * item + (col >> 3)))
+        keep = selection((rows_one, 24), lambda row, col: (col & 7) == (row >> 5) + item)
+        weights = weights + moved * keep
+    high = weights.astype(jnp.bfloat16)
+    rest = weights - high.astype(jnp.float32)
+    middle = rest.astype(jnp.bfloat16)
+    low = (rest - middle.astype(jnp.float32)).astype(jnp.bfloat16)
+    first_ref[...] = jnp.concatenate([high, middle, low], axis=1)
+
+    rows_two = CHAN * ROW_DEV
+    picker = selection((rows_two, CHAN), lambda row, col: (row >> 2) == col)
+    wide_two_ref[...] = column_of(picker, bias_two_ref[...])
+    spread = jnp.dot(
+        picker.astype(jnp.bfloat16), conv_two_ref[...], preferred_element_type=jnp.float32
+    ).astype(jnp.bfloat16)
+    cols_two = CHAN * (ROW_DEV + 2)
+    for tap in range(3):
+        block = jnp.zeros((rows_two, cols_two), jnp.float32)
+        for item in range(3):
+            source = spread[:, (3 * item + tap) * CHAN : (3 * item + tap + 1) * CHAN]
+            place = selection((CHAN, cols_two), lambda row, col: (col & (CHAN - 1)) == row)
+            moved = jnp.dot(source, place.astype(jnp.bfloat16), preferred_element_type=jnp.float32)
+            keep = selection((rows_two, cols_two), lambda row, col: (col >> 5) == (row & 3) + item)
+            block = block + moved * keep
+        second_ref[tap] = block.astype(jnp.bfloat16)
+
+
+def prepare(member, conv_one, bias_one, conv_two, bias_two, views, views_total, share, view_count):
+    vmem = pl.BlockSpec(memory_space=pltpu.VMEM)
+
+    def body(*refs):
+        prepare_kernel(views_total, share, view_count, *refs)
+
+    rows_one, rows_two = CHAN * (ROW_DEV + 2), CHAN * ROW_DEV
     return pl.pallas_call(
-        ramp_kernel,
-        out_shape=jax.ShapeDtypeStruct((2 * BLOCK, (2 * BLOCKS - 1) * BLOCK), jnp.bfloat16),
-        out_specs=pl.BlockSpec(memory_space=pltpu.VMEM),
+        body,
+        out_shape=(
+            jax.ShapeDtypeStruct((2 * BLOCK, (2 * BLOCKS - 1) * BLOCK), jnp.bfloat16),
+            jax.ShapeDtypeStruct((views, 128), jnp.float32),
+            jax.ShapeDtypeStruct((views, 128), jnp.float32),
+            jax.ShapeDtypeStruct((rows_one, 72), jnp.bfloat16),
+            jax.ShapeDtypeStruct((rows_one, 1), jnp.float32),
+            jax.ShapeDtypeStruct((3, rows_two, rows_one), jnp.bfloat16),
+            jax.ShapeDtypeStruct((rows_two, 1), jnp.float32),
+        ),
+        in_specs=[pl.BlockSpec(memory_space=pltpu.SMEM)] + [vmem] * 4,
+        out_specs=(vmem,) * 7,
+        compiler_params=pltpu.CompilerParams(vmem_limit_bytes=16 * 2**20),
         cost_estimate=pl.CostEstimate(flops=20_000_000, bytes_accessed=4_000_000, transcendentals=0),
-        name="ramp",
-    )()
+        name="prepare",
+    )(member, conv_one, bias_one, conv_two, bias_two)
+
+
+def lane_gather(words, index):
+    dims = lax.GatherDimensionNumbers(
+        offset_dims=(),
+        collapsed_slice_dims=(1,),
+        start_index_map=(1,),
+        operand_batching_dims=(0,),
+        start_indices_batching_dims=(0,),
+    )
+    return lax.gather(
+        words, index[:, :, None], dims, (1, 1), mode=lax.GatherScatterMode.PROMISE_IN_BOUNDS
+    )
 
 
 def backproject_kernel(
@@ -61,9 +165,9 @@
     ramp_ref,
     out_ref,
     filt_ref,
-    slope_ref,
-    level_ref,
+    word_ref,
     bin_ref,
+    back_ref,
     center_ref,
     where_ref,
     acc_ref,
@@ -104,25 +208,37 @@
         else:
             filt_ref[rows, :] += part
 
-    zero = jnp.zeros((views, 128), jnp.float32)
     margin = MARGIN // 128
-
-    def filtered(block):
-        place = block - margin
-        if place < 0 or place >= BINS // 128:
-            return zero
+    inner = BINS // 128
+
+    def raw(place):
         half = 128 * (place % 2)
         piece = filt_ref[views * (place // 2) : views * (place // 2) + views, half : half + 128]
         return piece.astype(jnp.bfloat16).astype(jnp.float32)
 
+    largest = jnp.abs(raw(0))
+    for place in range(1, inner):
+        largest = jnp.maximum(largest, jnp.abs(raw(place)))
+    largest = jnp.max(largest, axis=1, keepdims=True)
+    largest = jnp.max(largest.reshape(views // VIEW_STEP, VIEW_STEP, 1), axis=1, keepdims=True)
+    largest = jnp.maximum(jnp.broadcast_to(largest, (views // VIEW_STEP, VIEW_STEP, 128)), 1e-30)
+    largest = largest.reshape(views, 128)
+    back_ref[...] = largest * (1.0 / (16383.0 * 65536.0))
+    scale = 16383.0 / largest
+    zero = jnp.zeros((views, 128), jnp.int32)
+
+    def filtered(block):
+        place = block - margin
+        if place < 0 or place >= inner:
+            return zero
+        return jnp.floor(raw(place) * scale + 0.5).astype(jnp.int32)
+
     def turned(piece):
         return pltpu.roll(piece, 127, 1)
 
     def block_tables(block, piece, piece_turned, next_turned):
-        after = jnp.where(lane < 127, piece_turned, next_turned)
-        slope = after - piece
-        bins = lane_f + 128.0 * block
-        return slope, piece - bins * slope, bins + 1.0
+        step = jnp.where(lane < 127, piece_turned, next_turned) - piece
+        return piece * 65536 + step, lane_f + (128.0 * block + 1.0)
 
     first_block = FIRST_WIN // 2
     piece = filtered(first_block)
@@ -132,7 +248,7 @@
         following = filtered(block + 1)
         following_turned = turned(following)
         now = block_tables(block, piece, piece_turned, following_turned)
-        for ref, value, old in zip((slope_ref, level_ref, bin_ref), now, before or now):
+        for ref, value, old in zip((word_ref, bin_ref), now, before or now):
             row = (2 * block - FIRST_WIN) * views
             if before is not None:
                 ref[row - views : row, :] = jnp.where(lane >= 64, old, value)
@@ -152,7 +268,7 @@
         row_set = step // per_set
         first_view = (step % per_set) * VIEW_STEP
         rows_y = sub_one + (first_y + 8.0 * row_set.astype(jnp.float32))
-        totals = [acc_ref[row_set, :, 128 * tile : 128 * tile + 128] for tile in range(TILES)]
+        totals = [None] * TILES
         for view_off in range(VIEW_STEP):
             view = first_view + view_off
             cos_v = jnp.broadcast_to(cos_ref[pl.ds(view, 1), :], (8, 128))
@@ -173,14 +289,15 @@
                     near = pl.ds(row, 1)
                     far = pl.ds(row + 2 * views, 1)
                     pick = bin_ref[near, :] > place_low
-                    slopes = jnp.where(pick, slope_ref[near, :], slope_ref[far, :])
-                    levels = jnp.where(pick, level_ref[near, :], level_ref[far, :])
-                    index = place.astype(jnp.int32) & 127
-                    slope = jnp.take_along_axis(slopes, index, axis=1, mode="promise_in_bounds")
-                    level = jnp.take_along_axis(levels, index, axis=1, mode="promise_in_bounds")
-                    totals[tile] = totals[tile] + (level + place * slope)
+                    words = jnp.where(pick, word_ref[near, :], word_ref[far, :])
+                    floor = jnp.floor(place)
+                    word = lane_gather(words, floor.astype(jnp.int32) & 127)
+                    value = word.astype(jnp.float32)
+                    value = value + (place - floor) * (word << 16).astype(jnp.float32)
+                    totals[tile] = value if totals[tile] is None else totals[tile] + value
+        back = jnp.broadcast_to(back_ref[pl.ds(first_view, 1), :], (8, 128))
         for tile in range(TILES):
-            acc_ref[row_set, :, 128 * tile : 128 * tile + 128] = totals[tile]
+            acc_ref[row_set, :, 128 * tile : 128 * tile + 128] += totals[tile] * back
         return carry
 
     lax.fori_loop(0, ROW_SETS * per_set, steps, 0)
@@ -203,15 +320,16 @@
         out_specs=vmem,
         scratch_shapes=[
             pltpu.VMEM((BLOCKS * views, BLOCK), jnp.float32),
+            pltpu.VMEM((rows, 128), jnp.int32),
             pltpu.VMEM((rows, 128), jnp.float32),
-            pltpu.VMEM((rows, 128), jnp.float32),
-            pltpu.VMEM((rows, 128), jnp.float32),
+            pltpu.VMEM((views, 128), jnp.float32),
             pltpu.VMEM((views, 128), jnp.float32),
             pltpu.VMEM((views, 128), jnp.int32),
             pltpu.VMEM((ROW_SETS, 8, WIDTH), jnp.float32),
             pltpu.SMEM((views, 128), jnp.int32),
             pltpu.SemaphoreType.DMA(()),
         ],
+        compiler_params=pltpu.CompilerParams(vmem_limit_bytes=16 * 2**20),
         cost_estimate=pl.CostEstimate(flops=1_000_000_000, bytes_accessed=6_000_000, transcendentals=0),
         name="backproject",
     )(first_y, lines, cosine, sine, ramp)
@@ -244,12 +362,6 @@
     image_ref[...] = jnp.concatenate([three, three, three], axis=0)
 
     weights = first_ref[...]
-    high = weights.astype(jnp.bfloat16)
-    rest = weights - high.astype(jnp.float32)
-    middle = rest.astype(jnp.bfloat16)
-    low = (rest - middle.astype(jnp.float32)).astype(jnp.bfloat16)
-    weights = jnp.concatenate([high, middle, low], axis=1)
-
     count = CHAN * (ROW_DEV + 2)
     for tile in range(0, WIDTH, 256):
         hidden = jnp.dot(weights, image_ref[:, tile : tile + 256], preferred_element_type=jnp.float32)
@@ -263,8 +375,9 @@
     column = lax.broadcasted_iota(jnp.int32, middle_rows.shape, 1)
     before = jnp.where(column == 0, 0.0, pltpu.roll(middle_rows, 1, 1)).astype(jnp.bfloat16)
     after = jnp.where(column == WIDTH - 1, 0.0, pltpu.roll(middle_rows, WIDTH - 1, 1)).astype(jnp.bfloat16)
-    stacked = jnp.concatenate([before, middle_rows.astype(jnp.bfloat16), after], axis=0)
-    mixed = jnp.dot(second_ref[...], stacked, preferred_element_type=jnp.float32)
+    mixed = jnp.dot(second_ref[0], before, preferred_element_type=jnp.float32)
+    mixed = mixed + jnp.dot(second_ref[1], middle_rows.astype(jnp.bfloat16), preferred_element_type=jnp.float32)
+    mixed = mixed + jnp.dot(second_ref[2], after, preferred_element_type=jnp.float32)
     mixed = jnp.maximum(mixed + bias_two_ref[...], 0.0)
     out_ref[...] = mixed.reshape(CHAN, ROW_DEV, WIDTH).astype(jnp.bfloat16)[None]
 
@@ -284,27 +397,10 @@
             pltpu.VMEM((72, WIDTH), jnp.bfloat16),
             pltpu.VMEM((CHAN * (ROW_DEV + 2), WIDTH), jnp.float32),
         ],
+        compiler_params=pltpu.CompilerParams(vmem_limit_bytes=16 * 2**20),
         cost_estimate=pl.CostEstimate(flops=500_000_000, bytes_accessed=1_000_000, transcendentals=0),
         name="layers",
     )(row_base, parts, first, bias_one, second, bias_two)
-
-
-def first_matrix(conv_one):
-    taps = conv_one.reshape(3, 3, CHAN)
-    rows = []
-    for row in range(ROW_DEV + 2):
-        padded = jnp.pad(taps, ((row, ROW_DEV + 1 - row), (0, 0), (0, 0)))
-        rows.append(jnp.transpose(padded, (2, 1, 0)))
-    return jnp.stack(rows).reshape(CHAN * (ROW_DEV + 2), 24)
-
-
-def second_matrix(conv_two):
-    taps = conv_two.reshape(CHAN, 3, 3, CHAN)
-    rows = []
-    for row in range(ROW_DEV):
-        padded = jnp.pad(taps, ((0, 0), (row, ROW_DEV - 1 - row), (0, 0), (0, 0)))
-        rows.append(jnp.transpose(padded, (0, 2, 1, 3)))
-    return jnp.stack(rows, axis=1).reshape(CHAN * ROW_DEV, 3 * (ROW_DEV + 2) * CHAN)
 
 
 def local(sinogram, view_shift, conv_one, bias_one, conv_two, bias_two):
@@ -324,27 +420,31 @@
     lines = lax.all_to_all(sent, "views", 0, 0, tiled=True)
     lines = lines.reshape(view_groups * share, detector + 128)
 
-    view = jnp.arange(view_groups * share, dtype=jnp.int32)
-    view = view // share * view_count + member * share + view % share
-    angle = view.astype(jnp.float32) * (math.pi / views_total)
-    cosine = jnp.broadcast_to(jnp.cos(angle)[:, None], (view_groups * share, 128))
-    sine = jnp.broadcast_to(jnp.sin(angle)[:, None], (view_groups * share, 128))
+    ramp, cosine, sine, first, wide_one, second, wide_two = prepare(
+        member.astype(jnp.int32).reshape(1),
+        conv_one,
+        bias_one[None],
+        conv_two,
+        bias_two[None],
+        view_groups * share,
+        views_total,
+        share,
+        view_count,
+    )
     first_row = (row_index - member) * ROW_DEV - 2
     first_y = first_row.astype(jnp.float32) - (image_rows - 1) / 2.0
 
-    partial_rows = backproject(first_y.reshape(1), lines, cosine, sine, ramp_blocks())
+    partial_rows = backproject(first_y.reshape(1), lines, cosine, sine, ramp)
     groups = [[GROUP * base + item for item in range(GROUP)] for base in range(row_groups // GROUP)]
     parts = lax.all_to_all(partial_rows, "rows", 0, 0, tiled=True, axis_index_groups=groups)
 
     row_base = (row_index * ROW_DEV).astype(jnp.int32).reshape(1)
-    wide_one = jnp.tile(bias_one, ROW_DEV + 2)[:, None]
-    wide_two = jnp.repeat(bias_two, ROW_DEV)[:, None]
     return layers(
         row_base,
         parts,
-        first_matrix(conv_one),
+        first,
         wide_one,
-        second_matrix(conv_two),
+        second,
         wide_two,
         math.pi / views_total,
         image_rows,

time: 67.7 us -> 57.1 us (0.84)
  Pallas kernels: 30.2 us -> 19.1 us
  waiting for transfers between devices: 5.12 us -> 8.83 us
  local copies, waits for them, and re-layouts: 11 us -> 8.59 us
  other arithmetic: 1.61 us -> 0.84 us
    pallas_call x1, Pallas kernels: 22.8 us -> 15 us  [backproject(): pl.pallas_call(backproject_kernel, out_shape=jax.ShapeDtypeStruct((GROUP,...]
    unnamed x9 -> x15, local copies, waits for them, and re-layouts: 1.96 us -> 7.21 us
    all_to_all x1, waiting for transfers between devices: 0.01 us -> 3.57 us  [local(): lax.all_to_all(partial_rows, 'rows', 0, 0, tiled=True, axis_index_groups=...]
    reshape x6 -> x0, local copies, waits for them, and re-layouts: 3.47 us -> none  [the longest x1 1.09 us: second_matrix(): jnp.stack(rows, axis=1).reshape(CHAN * ROW_DEV, 3 * (ROW_DEV + 2) * CHAN)]
    another operation x6 -> x0, local copies, waits for them, and re-layouts: 2.04 us -> none  [the longest x2 0.77 us: local(): wide_one = jnp.tile(bias_one, ROW_DEV + 2)[:, None]]
    pallas_call x1, Pallas kernels: 4.13 us -> 2.21 us  [prepare(): pl.pallas_call(body, out_shape=(jax.ShapeDtypeStruct((2 * BLOCK, (2 * BLO...]
    broadcast_in_dim x3 -> x0, local copies, waits for them, and re-layouts: 1.43 us -> none  [the longest x1 0.68 us: local(): sine = jnp.broadcast_to(jnp.sin(angle)[:, None], (view_groups * share, 128))]
    pallas_call x1, Pallas kernels: 3.21 us -> 1.91 us  [layers(): pl.pallas_call(body, out_shape=jax.ShapeDtypeStruct((1, CHAN, ROW_DEV, WI...]
  transfers between devices with their start and end apart: 2 -> 2, of which waited for: 1 -> 2; matrix products, arithmetic and copies ran while one was open for 10% -> 0% of each run, Pallas kernels for 6% -> 4%
where the time goes in v1:
time: 57.1 us; the launch traced here: 56.7 us
  starting transfers between devices  19.2 us (34%)
  Pallas kernels  19.1 us (33%)
  waiting for transfers between devices  8.83 us (15%)
  local copies, waits for them, and re-layouts  8.59 us (15%)
  other arithmetic  0.84 us (1%)
    pallas_call x1, Pallas kernels, backproject(): pl.pallas_call(backproject_kernel, out_shape=jax.ShapeDtypeStruct((GROUP,...  15 us
    all_to_all x1, starting transfers between devices, local(): lines = lax.all_to_all(sent, 'views', 0, 0, tiled=True)  13.5 us
    unnamed x15, local copies, waits for them, and re-layouts  7.21 us
    all_to_all x1, starting transfers between devices, local(): lax.all_to_all(partial_rows, 'rows', 0, 0, tiled=True, axis_index_groups=...  5.75 us
    all_to_all x1, waiting for transfers between devices, local(): lines = lax.all_to_all(sent, 'views', 0, 0, tiled=True)  5.26 us
    all_to_all x1, waiting for transfers between devices, local(): lax.all_to_all(partial_rows, 'rows', 0, 0, tiled=True, axis_index_groups=...  3.57 us
    pallas_call x1, Pallas kernels, prepare(): pl.pallas_call(body, out_shape=(jax.ShapeDtypeStruct((2 * BLOCK, (2 * BLO...  2.21 us
    pallas_call x1, Pallas kernels, layers(): pl.pallas_call(body, out_shape=jax.ShapeDtypeStruct((1, CHAN, ROW_DEV, WI...  1.91 us
  transfers between devices with their start and end apart: 2, of which 2 were waited for; matrix products, arithmetic and copies ran while one was open for 0% of the time, Pallas kernels for 4%

profile of v1, /device:TPU:1, one launch (start us, length us, event | category | flops | bytes accessed | tf_op | source)
XLA Modules:
  0.0 56.7 jit_solution(1247779393809098409)
XLA Ops:
  0.0 0.0 copy-start
  0.0 0.8 %dynamic-slice_convert_fusion = bf16[2]{0:T(256)(128)(2,1)S(1)} fusion(s32[8]{0:T(128)} %param.7, s32[]{:T(128)S(6)} %select_n.12), kind=kLoop, calls=%fused_computation.1 | loop fusion | flops 2 | bytes 16 | tf_op jit(solution)/shard_map/convert_element_type | solution.py:417
  0.8 0.4 copy-done
  1.2 0.3 constant_dynamic-slice_fusion
  1.5 0.1 copy.11
  1.6 0.1 broadcast_in_dim.12
  1.7 0.9 %copy.10 = bf16[32,2,2176]{2,1,0:T(2,128)(2,1)} copy(bf16[32,2,2176]{2,0,1:T(8,128)(2,1)S(1)} %pad_maximum_fusion) | data formatting | bytes 557056 | tf_op jit(solution)/shard_map/concatenate | solution.py:419
  2.6 13.5 %all-to-all-start = ((bf16[32,2,2176]{2,1,0:T(2,128)(2,1)}), bf16[32,2,2176]{2,1,0:T(2,128)(2,1)S(1)}, u32[]{:S(2)}, u32[]{:S(2)}) async-start(bf16[32,2,2176]{2,1,0:T(2,128)(2,1)} %copy.10), calls=%async_computation | async-start | bytes 557056 | tf_op jit(solution)/shard_map/all_to_all | solution.py:420
  16.1 0.0 copy-start.3
  16.1 0.7 %copy-done.3 = bf16[32,288]{1,0:T(8,128)(2,1)S(1)} copy-done((bf16[32,288]{1,0:T(8,128)(2,1)S(1)}, bf16[32,288]{1,0:T(8,128)(2,1)}, u32[]{:S(2)}) %copy-start.3) | copy-done | bytes 18456
  16.8 0.7 %copy-done.4 = f32[9,32]{1,0:T(8,128)S(1)} copy-done((f32[9,32]{1,0:T(8,128)S(1)}, f32[9,32]{1,0:T(8,128)}, u32[]{:S(2)}) %copy-start.4) | copy-done | bytes 1176
  17.5 0.7 %copy-done.5 = f32[32]{0:T(128)S(1)} copy-done((f32[32]{0:T(128)S(1)}, f32[32]{0:T(128)}, u32[]{:S(2)}) %copy-start.5) | copy-done | bytes 152
  18.2 0.7 %copy-done.6 = f32[32]{0:T(128)S(1)} copy-done((f32[32]{0:T(128)S(1)}, f32[32]{0:T(128)}, u32[]{:S(2)}) %copy-start.6) | copy-done | bytes 152
  18.9 2.2 %prepare.1 = (bf16[512,3840]{1,0:T(8,128)(2,1)S(1)}, f32[64,128]{1,0:T(8,128)S(1)}, f32[64,128]{1,0:T(8,128)S(1)}, bf16[192,72]{1,0:T(8,128)(2,1)S(1)}, f32[192,...) custom-call(s32[1]{0:T(128)} %bitcast.2.refs_0_, f32[9,32]{1,0:T(8,128)S(1)} %copy-done.4, ...), custom_call_target="tpu_custom_call" | custom-call | flops 20000000 | bytes 4000000 | tf_op jit(solution)/shard_map/prepare/pallas_call | solution.py:128
  21.1 0.0 copy-start.1
  21.1 1.9 %copy-done.1 = bf16[512,3840]{1,0:T(8,128)(2,1)} copy-done((bf16[512,3840]{1,0:T(8,128)(2,1)}, bf16[512,3840]{1,0:T(8,128)(2,1)S(1)}, u32[]{:S(2)}) %copy-start.1) | copy-done | bytes 3932184
  22.9 5.3 %all-to-all-done = bf16[32,2,2176]{2,1,0:T(2,128)(2,1)S(1)} async-done(((bf16[32,2,2176]{2,1,0:T(2,128)(2,1)}), bf16[32,2,2176]{2,1,0:T(2,128)(2,1)S(1)}, u32[]{:S(2)}, u32[]{:S(2)}) %all-to-all-start) | async-done | bytes 278560 | tf_op jit(solution)/shard_map/all_to_all | solution.py:420
  28.2 0.1 reshape.15.x_ref
  28.3 0.0 copy-start.2
  28.3 2.1 %copy-done.2 = bf16[512,3840]{1,0:T(8,128)(2,1)S(1)} copy-done((bf16[512,3840]{1,0:T(8,128)(2,1)S(1)}, bf16[512,3840]{1,0:T(8,128)(2,1)}, u32[]{:S(2)}) %copy-start.2) | copy-done | bytes 3932184
  30.4 15.0 %backproject.1 = bf16[4,8,2048]{2,1,0:T(8,128)(2,1)} custom-call(f32[1]{0:T(128)} %bitcast.1.first_ref, bf16[64,2176]{1,0:T(8,128)(2,1)S(1)} %reshape.15.x_ref, f32[64,128]{1,0:T(8,128)S(1)} %get-tuple-element.12.cos_ref, f32[64,128]{1,0:T(8,128)S(1)} %get-tuple-element.13.sin_ref, bf16[512,3840]{1,0:T(8,128)(2,1)S(1)} %copy-done.2), custom_call_target="tpu_custom_call" | custom-call | flops 1000000000 | bytes 6000000 | tf_op jit(solution)/shard_map/backproject/pallas_call | solution.py:316
  45.4 5.8 %all-to-all-start.1 = ((bf16[4,8,2048]{2,1,0:T(8,128)(2,1)}), bf16[4,8,2048]{2,1,0:T(8,128)(2,1)S(1)}, u32[]{:S(2)}, u32[]{:S(2)}) async-start(bf16[4,8,2048]{2,1,0:T(8,128)(2,1)} %backproject.1), calls=%async_computation.1 | async-start | bytes 262144 | tf_op jit(solution)/shard_map/all_to_all | solution.py:439
  51.2 3.6 %all-to-all-done.1.refs_1_ = bf16[4,8,2048]{2,1,0:T(8,128)(2,1)S(1)} async-done(((bf16[4,8,2048]{2,1,0:T(8,128)(2,1)}), bf16[4,8,2048]{2,1,0:T(8,128)(2,1)S(1)}, u32[]{:S(2)}, u32[]{:S(2)}) %all-to-all-start.1) | async-done | bytes 131104 | tf_op jit(solution)/shard_map/all_to_all | solution.py:439
  54.8 1.9 %layers.1 = bf16[1,32,4,2048]{3,2,1,0:T(4,128)(2,1)} custom-call(s32[1]{0:T(128)} %bitcast.refs_0_, bf16[4,8,2048]{2,1,0:T(8,128)(2,1)S(1)} %all-to-all-done.1.refs_1_, bf16[192,72]{1,0:T(8,128)(2,1)S(1)} %get-tuple-element.15.refs_2_, f32[192,1]{1,0:T(8,128)S(1)} %get-tuple-element.16.refs_3_, bf16[3,128,192]{2,1,0:T(8,128)(2,1)S(1)} %get-tuple-element.17.refs_4_, ...), custom_call_target="tpu_custom_call" | custom-call | flops 500000000 | bytes 1000000 | tf_op jit(solution)/shard_map/layers/pallas_call | solution.py:391
  (4 shorter events, 0.0 us)
Async XLA Ops:
  0.0 1.2 %copy-start = (bf16[32,8,2048]{2,1,0:T(8,128)(2,1)S(1)}, bf16[32,8,2048]{2,1,0:T(8,128)(2,1)}, u32[]{:S(2)}) copy-start(bf16[32,8,2048]{2,1,0:T(8,128)(2,1)} %param.6) | copy-start | bytes 3145732
  2.6 25.6 %all-to-all-start = ((bf16[32,2,2176]{2,1,0:T(2,128)(2,1)}), bf16[32,2,2176]{2,1,0:T(2,128)(2,1)S(1)}, u32[]{:S(2)}, u32[]{:S(2)}) async-start(bf16[32,2,2176]{2,1,0:T(2,128)(2,1)} %copy.10), calls=%async_computation | async-start | bytes 557056 | tf_op jit(solution)/shard_map/all_to_all | solution.py:420
  16.1 0.7 %copy-start.3 = (bf16[32,288]{1,0:T(8,128)(2,1)S(1)}, bf16[32,288]{1,0:T(8,128)(2,1)}, u32[]{:S(2)}) copy-start(bf16[32,288]{1,0:T(8,128)(2,1)} %refs_3_.1) | copy-start | bytes 55300
  16.8 0.7 %copy-start.4 = (f32[9,32]{1,0:T(8,128)S(1)}, f32[9,32]{1,0:T(8,128)}, u32[]{:S(2)}) copy-start(f32[9,32]{1,0:T(8,128)} %refs_1_.1) | copy-start | bytes 3460
  17.5 0.7 %copy-start.5 = (f32[32]{0:T(128)S(1)}, f32[32]{0:T(128)}, u32[]{:S(2)}) copy-start(f32[32]{0:T(128)} %param.9) | copy-start | bytes 388
  18.2 0.7 %copy-start.6 = (f32[32]{0:T(128)S(1)}, f32[32]{0:T(128)}, u32[]{:S(2)}) copy-start(f32[32]{0:T(128)} %param.11) | copy-start | bytes 388
  21.1 1.9 %copy-start.1 = (bf16[512,3840]{1,0:T(8,128)(2,1)}, bf16[512,3840]{1,0:T(8,128)(2,1)S(1)}, u32[]{:S(2)}) copy-start(bf16[512,3840]{1,0:T(8,128)(2,1)S(1)} %get-tuple-element.14.ramp_ref) | copy-start | bytes 11796484
  28.3 2.1 %copy-start.2 = (bf16[512,3840]{1,0:T(8,128)(2,1)S(1)}, bf16[512,3840]{1,0:T(8,128)(2,1)}, u32[]{:S(2)}) copy-start(bf16[512,3840]{1,0:T(8,128)(2,1)} %copy-done.1) | copy-start | bytes 11796484
  45.4 9.3 %all-to-all-start.1 = ((bf16[4,8,2048]{2,1,0:T(8,128)(2,1)}), bf16[4,8,2048]{2,1,0:T(8,128)(2,1)S(1)}, u32[]{:S(2)}, u32[]{:S(2)}) async-start(bf16[4,8,2048]{2,1,0:T(8,128)(2,1)} %backproject.1), calls=%async_computation.1 | async-start | bytes 262144 | tf_op jit(solution)/shard_map/all_to_all | solution.py:439

commit v2 on v1

--- a/solution.py
+++ b/solution.py
@@ -20,7 +20,10 @@
 WINDOWS = 38
 TILES = WIDTH // 128
 ROW_SETS = 3
-VIEW_STEP = 8
+RAMP_COLS = BLOCKS * BLOCK
+VIEW_STEP = 64
+SCALE_SET = 8
+PARTS = 2
 
 
 def selection(shape, test):
@@ -60,12 +63,12 @@
     second_ref,
     wide_two_ref,
 ):
-    width = (2 * BLOCKS - 1) * BLOCK
+    width = BLOCKS * BLOCK
 
     for turn in range(8):
         row = lax.broadcasted_iota(jnp.int32, (16, width + 128), 0)
         col = lax.broadcasted_iota(jnp.int32, (16, width + 128), 1)
-        offset = col - row - (128 + 16 * turn + (BLOCKS - 1) * BLOCK)
+        offset = col - row - (128 + 16 * turn)
         place = offset.astype(jnp.float32)
         guarded = jnp.maximum(place * place, 1.0)
         odd = (offset & 1) == 1
@@ -128,7 +131,7 @@
     return pl.pallas_call(
         body,
         out_shape=(
-            jax.ShapeDtypeStruct((2 * BLOCK, (2 * BLOCKS - 1) * BLOCK), jnp.bfloat16),
+            jax.ShapeDtypeStruct((2 * BLOCK, BLOCKS * BLOCK), jnp.bfloat16),
             jax.ShapeDtypeStruct((views, 128), jnp.float32),
             jax.ShapeDtypeStruct((views, 128), jnp.float32),
             jax.ShapeDtypeStruct((rows_one, 72), jnp.bfloat16),
@@ -142,6 +145,10 @@
         cost_estimate=pl.CostEstimate(flops=20_000_000, bytes_accessed=4_000_000, transcendentals=0),
         name="prepare",
     )(member, conv_one, bias_one, conv_two, bias_two)
+
+
+def dot_turned(left, right):
+    return lax.dot_general(left, right, (((1,), (1,)), ((), ())), preferred_element_type=jnp.float32)
 
 
 def lane_gather(words, index):
@@ -199,9 +206,12 @@
         left = jnp.concatenate(
             [x_ref[:, BLOCK * block : BLOCK * block + BLOCK] for block in range(low, high)], axis=0
         )
-        left = jnp.concatenate([left, left], axis=1)
-        right = ramp_ref[:, BLOCK * (delta + BLOCKS - 1) : BLOCK * (delta + BLOCKS)]
-        part = jnp.dot(left, right, preferred_element_type=jnp.float32)
+        cols = slice(BLOCK * abs(delta), BLOCK * abs(delta) + BLOCK)
+        if delta >= 0:
+            left = jnp.concatenate([left, left], axis=1)
+            part = jnp.dot(left, ramp_ref[:, cols], preferred_element_type=jnp.float32)
+        else:
+            part = dot_turned(left, ramp_ref[0:BLOCK, cols]) + dot_turned(left, ramp_ref[BLOCK:, cols])
         rows = slice(views * (low + delta), views * (high + delta))
         if delta == 0:
             filt_ref[rows, :] = part
@@ -220,8 +230,8 @@
     for place in range(1, inner):
         largest = jnp.maximum(largest, jnp.abs(raw(place)))
     largest = jnp.max(largest, axis=1, keepdims=True)
-    largest = jnp.max(largest.reshape(views // VIEW_STEP, VIEW_STEP, 1), axis=1, keepdims=True)
-    largest = jnp.maximum(jnp.broadcast_to(largest, (views // VIEW_STEP, VIEW_STEP, 128)), 1e-30)
+    largest = jnp.max(largest.reshape(views // SCALE_SET, SCALE_SET, 1), axis=1, keepdims=True)
+    largest = jnp.maximum(jnp.broadcast_to(largest, (views // SCALE_SET, SCALE_SET, 128)), 1e-30)
     largest = largest.reshape(views, 128)
     back_ref[...] = largest * (1.0 / (16383.0 * 65536.0))
     scale = 16383.0 / largest
@@ -262,50 +272,92 @@
 
     lane_one = lax.broadcasted_iota(jnp.int32, (8, 128), 1).astype(jnp.float32)
     sub_one = lax.broadcasted_iota(jnp.int32, (8, 128), 0).astype(jnp.float32)
+    count = TILES // PARTS
+    span = 128 * count
+    top = lax.broadcasted_iota(jnp.int32, (8, 128), 0) < 4
+
+    def spread(ref, row):
+        return jnp.broadcast_to(ref[pl.ds(row, 1), :], (8, 128))
+
+    def one_view(views_of, row_set, part, rows_y, totals):
+        def both(ref, rows):
+            if len(rows) == 1:
+                return spread(ref, rows[0])
+            return jnp.where(top, spread(ref, rows[0]), spread(ref, rows[1]))
+
+        middle_x = part.astype(jnp.float32) * span + (span // 2 - WIDTH / 2.0 + 0.5)
+        first_tile = row_set * TILES + part * count
+        cos_v = both(cos_ref, views_of)
+        base = rows_y * both(sin_ref, views_of) + both(center_ref, views_of)
+        stride = cos_v * 128.0
+        middle = (lane_one + middle_x) * cos_v + base
+        middle_low = jnp.minimum(middle_x * cos_v, (middle_x + 127.0) * cos_v) + base
+        for direction in (1, -1):
+            place, place_low = middle, middle_low
+            tiles = range(count // 2, count) if direction == 1 else range(count // 2 - 1, -1, -1)
+            for tile in tiles:
+                if direction == 1 and tile > count // 2:
+                    place, place_low = place + stride, place_low + stride
+                elif direction == -1:
+                    place, place_low = place - stride, place_low - stride
+                near = [where_smem[view, first_tile + tile] for view in views_of]
+                far = [row + 2 * views for row in near]
+                pick = both(bin_ref, near) > place_low
+                words = jnp.where(pick, both(word_ref, near), both(word_ref, far))
+                lower = place.astype(jnp.int32)
+                word = lane_gather(words, lower & 127)
+                value = word.astype(jnp.float32)
+                along = place - lower.astype(jnp.float32)
+                value = value + along * (word << 16).astype(jnp.float32)
+                totals[tile] = value if totals[tile] is None else totals[tile] + value
+
+    def add_up(block, first_view, totals):
+        back = spread(back_ref, first_view)
+        for tile in range(count):
+            acc_ref[block, :, 128 * tile : 128 * tile + 128] += totals[tile] * back
+
     per_set = views // VIEW_STEP
 
     def steps(step, carry):
-        row_set = step // per_set
+        block = step // per_set
+        row_set = block // PARTS
         first_view = (step % per_set) * VIEW_STEP
         rows_y = sub_one + (first_y + 8.0 * row_set.astype(jnp.float32))
-        totals = [None] * TILES
-        for view_off in range(VIEW_STEP):
-            view = first_view + view_off
-            cos_v = jnp.broadcast_to(cos_ref[pl.ds(view, 1), :], (8, 128))
-            sin_v = jnp.broadcast_to(sin_ref[pl.ds(view, 1), :], (8, 128))
-            base = rows_y * sin_v + jnp.broadcast_to(center_ref[pl.ds(view, 1), :], (8, 128))
-            stride = cos_v * 128.0
-            middle = (lane_one + 0.5) * cos_v + base
-            middle_low = jnp.minimum(0.5 * cos_v, 127.5 * cos_v) + base
-            for direction in (1, -1):
-                place, place_low = middle, middle_low
-                tiles = range(TILES // 2, TILES) if direction == 1 else range(TILES // 2 - 1, -1, -1)
-                for tile in tiles:
-                    if direction == 1 and tile > TILES // 2:
-                        place, place_low = place + stride, place_low + stride
-                    elif direction == -1:
-                        place, place_low = place - stride, place_low - stride
-                    row = where_smem[view, row_set * TILES + tile]
-                    near = pl.ds(row, 1)
-                    far = pl.ds(row + 2 * views, 1)
-                    pick = bin_ref[near, :] > place_low
-                    words = jnp.where(pick, word_ref[near, :], word_ref[far, :])
-                    floor = jnp.floor(place)
-                    word = lane_gather(words, floor.astype(jnp.int32) & 127)
-                    value = word.astype(jnp.float32)
-                    value = value + (place - floor) * (word << 16).astype(jnp.float32)
-                    totals[tile] = value if totals[tile] is None else totals[tile] + value
-        back = jnp.broadcast_to(back_ref[pl.ds(first_view, 1), :], (8, 128))
-        for tile in range(TILES):
-            acc_ref[row_set, :, 128 * tile : 128 * tile + 128] += totals[tile] * back
+        for set_off in range(0, VIEW_STEP, SCALE_SET):
+            totals = [None] * count
+            for view_off in range(SCALE_SET):
+                view = first_view + (set_off + view_off)
+                one_view((view,), row_set, block % PARTS, rows_y, totals)
+            add_up(block, first_view + set_off, totals)
         return carry
 
-    lax.fori_loop(0, ROW_SETS * per_set, steps, 0)
+    lax.fori_loop(0, 2 * PARTS * per_set, steps, 0)
+
+    def paired_steps(step, carry):
+        part = step // per_set
+        first_view = (step % per_set) * VIEW_STEP
+        rows_y = jnp.where(top, sub_one, sub_one - 4.0) + (first_y + 16.0)
+        for set_off in range(0, VIEW_STEP, SCALE_SET):
+            totals = [None] * count
+            for view_off in range(SCALE_SET // 2):
+                view = first_view + (set_off + view_off)
+                one_view((view, view + SCALE_SET // 2), 2, part, rows_y, totals)
+            add_up(part + 2 * PARTS, first_view + set_off, totals)
+        return carry
+
+    lax.fori_loop(0, PARTS * per_set, paired_steps, 0)
+
+    def rows_of(row_set, low, high):
+        return jnp.concatenate(
+            [acc_ref[row_set * PARTS + part, low:high, :] for part in range(PARTS)], axis=1
+        )
 
     for member in range(GROUP):
-        lower = acc_ref[member // 2]
-        if member % 2:
-            lower = jnp.concatenate([lower[4:8], acc_ref[member // 2 + 1][0:4]], axis=0)
+        lower = rows_of(member // 2, 0, 8)
+        if member == 1:
+            lower = jnp.concatenate([rows_of(0, 4, 8), rows_of(1, 0, 4)], axis=0)
+        elif member == 3:
+            lower = jnp.concatenate([rows_of(1, 4, 8), rows_of(2, 0, 4) + rows_of(2, 4, 8)], axis=0)
         out_ref[member] = lower.astype(jnp.bfloat16)
 
 
@@ -325,7 +377,7 @@
             pltpu.VMEM((views, 128), jnp.float32),
             pltpu.VMEM((views, 128), jnp.float32),
             pltpu.VMEM((views, 128), jnp.int32),
-            pltpu.VMEM((ROW_SETS, 8, WIDTH), jnp.float32),
+            pltpu.VMEM((ROW_SETS * PARTS, 8, WIDTH // PARTS), jnp.float32),
             pltpu.SMEM((views, 128), jnp.int32),
             pltpu.SemaphoreType.DMA(()),
         ],

time: 57.1 us -> 56.7 us (level)
  Pallas kernels: 19.1 us -> 15.8 us
  waiting for transfers between devices: 8.83 us -> 11.5 us
    pallas_call x1, Pallas kernels: 15 us -> 12.3 us  [backproject(): pl.pallas_call(backproject_kernel, out_shape=jax.ShapeDtypeStruct((GROUP,...]
    all_to_all x1, waiting for transfers between devices: 5.26 us -> 7.92 us  [local(): lines = lax.all_to_all(sent, 'views', 0, 0, tiled=True)]
    reshape x1, local copies, waits for them, and re-layouts: 0.1 us -> 1.06 us  [local(): lines = lines.reshape(view_groups * share, detector + 128)]
    unnamed x15 -> x27, local copies, waits for them, and re-layouts: 7.21 us -> 6.3 us
    pallas_call x1, Pallas kernels: 2.21 us -> 1.61 us  [prepare(): pl.pallas_call(body, out_shape=(jax.ShapeDtypeStruct((2 * BLOCK, BLOCKS *...]
  transfers between devices with their start and end apart: 2 -> 2, of which waited for: 2 -> 2; matrix products, arithmetic and copies ran while one was open for 0% -> 0% of each run, Pallas kernels for 4% -> 3%
where the time goes in v2:
time: 56.7 us; the launch traced here: 56.2 us
  starting transfers between devices  19.3 us (34%)
  Pallas kernels  15.8 us (28%)
  waiting for transfers between devices  11.5 us (20%)
  local copies, waits for them, and re-layouts  8.63 us (15%)
  other arithmetic  0.84 us (1%)
    all_to_all x1, starting transfers between devices, local(): lines = lax.all_to_all(sent, 'views', 0, 0, tiled=True)  13.6 us
    pallas_call x1, Pallas kernels, backproject(): pl.pallas_call(backproject_kernel, out_shape=jax.ShapeDtypeStruct((GROUP,...  12.3 us
    all_to_all x1, waiting for transfers between devices, local(): lines = lax.all_to_all(sent, 'views', 0, 0, tiled=True)  7.92 us
    unnamed x27, local copies, waits for them, and re-layouts  6.3 us
    all_to_all x1, starting transfers between devices, local(): lax.all_to_all(partial_rows, 'rows', 0, 0, tiled=True, axis_index_groups=...  5.75 us
    all_to_all x1, waiting for transfers between devices, local(): lax.all_to_all(partial_rows, 'rows', 0, 0, tiled=True, axis_index_groups=...  3.57 us
    pallas_call x1, Pallas kernels, layers(): pl.pallas_call(body, out_shape=jax.ShapeDtypeStruct((1, CHAN, ROW_DEV, WI...  1.91 us
    pallas_call x1, Pallas kernels, prepare(): pl.pallas_call(body, out_shape=(jax.ShapeDtypeStruct((2 * BLOCK, BLOCKS *...  1.61 us
  transfers between devices with their start and end apart: 2, of which 2 were waited for; matrix products, arithmetic and copies ran while one was open for 0% of the time, Pallas kernels for 3%

profile of v2, /device:TPU:1, one launch (start us, length us, event | category | flops | bytes accessed | tf_op | source)
XLA Modules:
  0.0 56.2 jit_solution(15732919602030967583)
XLA Ops:
  0.0 0.8 %dynamic-slice_convert_fusion = bf16[2]{0:T(256)(128)(2,1)S(1)} fusion(s32[8]{0:T(128)} %param.7, s32[]{:T(128)S(6)} %select_n.12), kind=kLoop, calls=%fused_computation.1 | loop fusion | flops 2 | bytes 16 | tf_op jit(solution)/shard_map/convert_element_type | solution.py:469
  0.9 0.4 copy-done
  1.2 0.3 constant_dynamic-slice_fusion
  1.5 0.1 copy.11
  1.6 0.1 broadcast_in_dim.12
  1.7 0.9 %copy.10 = bf16[32,2,2176]{2,1,0:T(2,128)(2,1)} copy(bf16[32,2,2176]{2,0,1:T(8,128)(2,1)S(1)} %pad_maximum_fusion) | data formatting | bytes 557056 | tf_op jit(solution)/shard_map/concatenate | solution.py:471
  2.6 13.6 %all-to-all-start = ((bf16[32,2,2176]{2,1,0:T(2,128)(2,1)}), bf16[32,2,2176]{2,1,0:T(2,128)(2,1)}, u32[]{:S(2)}, u32[]{:S(2)}) async-start(bf16[32,2,2176]{2,1,0:T(2,128)(2,1)} %copy.10), calls=%async_computation | async-start | bytes 557056 | tf_op jit(solution)/shard_map/all_to_all | solution.py:472
  16.2 0.0 copy-done.4
  16.2 0.0 copy-done.1
  16.3 1.6 %prepare.1 = (bf16[512,2048]{1,0:T(8,128)(2,1)S(1)}, f32[64,128]{1,0:T(8,128)S(1)}, f32[64,128]{1,0:T(8,128)S(1)}, bf16[192,72]{1,0:T(8,128)(2,1)S(1)}, f32[192,...) custom-call(s32[1]{0:T(128)} %bitcast.2.refs_0_, f32[9,32]{1,0:T(8,128)S(1)} %copy-done.2, ...), custom_call_target="tpu_custom_call" | custom-call | flops 20000000 | bytes 4000000 | tf_op jit(solution)/shard_map/prepare/pallas_call | solution.py:131
  17.9 0.7 %copy-done.5 = bf16[3,128,192]{2,1,0:T(8,128)(2,1)} copy-done((bf16[3,128,192]{2,1,0:T(8,128)(2,1)}, bf16[3,128,192]{2,1,0:T(8,128)(2,1)S(1)}, u32[]{:S(2)}) %copy-start.5) | copy-done | bytes 147480
  18.6 0.6 %copy-done.7 = f32[128,1]{1,0:T(8,128)} copy-done((f32[128,1]{1,0:T(8,128)}, f32[128,1]{1,0:T(8,128)S(1)}, u32[]{:S(2)}) %copy-start.7) | copy-done | bytes 536
  19.2 0.6 %copy-done.9 = bf16[192,72]{1,0:T(8,128)(2,1)} copy-done((bf16[192,72]{1,0:T(8,128)(2,1)}, bf16[192,72]{1,0:T(8,128)(2,1)S(1)}, u32[]{:S(2)}) %copy-start.9) | copy-done | bytes 27672
  19.8 0.6 %copy-done.11 = f32[64,128]{1,0:T(8,128)} copy-done((f32[64,128]{1,0:T(8,128)}, f32[64,128]{1,0:T(8,128)S(1)}, u32[]{:S(2)}) %copy-start.11) | copy-done | bytes 32792
  20.4 7.9 %all-to-all-done = bf16[32,2,2176]{2,1,0:T(2,128)(2,1)} async-done(((bf16[32,2,2176]{2,1,0:T(2,128)(2,1)}), bf16[32,2,2176]{2,1,0:T(2,128)(2,1)}, u32[]{:S(2)}, u32[]{:S(2)}) %all-to-all-start) | async-done | bytes 278560 | tf_op jit(solution)/shard_map/all_to_all | solution.py:472
  28.3 1.1 %reshape.15.x_ref = bf16[64,2176]{1,0:T(8,128)(2,1)S(1)} reshape(bf16[32,2,2176]{2,1,0:T(2,128)(2,1)} %all-to-all-done) | data formatting | bytes 557056 | tf_op jit(solution)/shard_map/reshape | solution.py:473
  29.4 0.7 %copy-done.12 = f32[64,128]{1,0:T(8,128)S(1)} copy-done((f32[64,128]{1,0:T(8,128)S(1)}, f32[64,128]{1,0:T(8,128)}, u32[]{:S(2)}) %copy-start.12) | copy-done | bytes 32792
  30.1 12.3 %backproject.1 = bf16[4,8,2048]{2,1,0:T(8,128)(2,1)} custom-call(f32[1]{0:T(128)} %bitcast.1.first_ref, bf16[64,2176]{1,0:T(8,128)(2,1)S(1)} %reshape.15.x_ref, f32[64,128]{1,0:T(8,128)S(1)} %get-tuple-element.12.cos_ref, f32[64,128]{1,0:T(8,128)S(1)} %copy-done.12, bf16[512,2048]{1,0:T(8,128)(2,1)S(1)} %get-tuple-element.14.ramp_ref), custom_call_target="tpu_custom_call" | custom-call | flops 1000000000 | bytes 6000000 | tf_op jit(solution)/shard_map/backproject/pallas_call | solution.py:368
  42.4 5.8 %all-to-all-start.1 = ((bf16[4,8,2048]{2,1,0:T(8,128)(2,1)}), bf16[4,8,2048]{2,1,0:T(8,128)(2,1)S(1)}, u32[]{:S(2)}, u32[]{:S(2)}) async-start(bf16[4,8,2048]{2,1,0:T(8,128)(2,1)} %backproject.1), calls=%async_computation.1 | async-start | bytes 262144 | tf_op jit(solution)/shard_map/all_to_all | solution.py:491
  48.2 3.6 %all-to-all-done.1.refs_1_ = bf16[4,8,2048]{2,1,0:T(8,128)(2,1)S(1)} async-done(((bf16[4,8,2048]{2,1,0:T(8,128)(2,1)}), bf16[4,8,2048]{2,1,0:T(8,128)(2,1)S(1)}, u32[]{:S(2)}, u32[]{:S(2)}) %all-to-all-start.1) | async-done | bytes 131104 | tf_op jit(solution)/shard_map/all_to_all | solution.py:491
  51.7 0.9 %copy-done.6 = bf16[3,128,192]{2,1,0:T(8,128)(2,1)S(1)} copy-done((bf16[3,128,192]{2,1,0:T(8,128)(2,1)S(1)}, bf16[3,128,192]{2,1,0:T(8,128)(2,1)}, u32[]{:S(2)}) %copy-start.6) | copy-done | bytes 147480
  52.6 0.8 %copy-done.8 = f32[128,1]{1,0:T(8,128)S(1)} copy-done((f32[128,1]{1,0:T(8,128)S(1)}, f32[128,1]{1,0:T(8,128)}, u32[]{:S(2)}) %copy-start.8) | copy-done | bytes 536
  53.5 0.8 %copy-done.10 = bf16[192,72]{1,0:T(8,128)(2,1)S(1)} copy-done((bf16[192,72]{1,0:T(8,128)(2,1)S(1)}, bf16[192,72]{1,0:T(8,128)(2,1)}, u32[]{:S(2)}) %copy-start.10) | copy-done | bytes 27672
  54.3 1.9 %layers.1 = bf16[1,32,4,2048]{3,2,1,0:T(4,128)(2,1)} custom-call(s32[1]{0:T(128)} %bitcast.refs_0_, bf16[4,8,2048]{2,1,0:T(8,128)(2,1)S(1)} %all-to-all-done.1.refs_1_, bf16[192,72]{1,0:T(8,128)(2,1)S(1)} %copy-done.10, f32[192,1]{1,0:T(8,128)S(1)} %get-tuple-element.16.refs_3_, bf16[3,128,192]{2,1,0:T(8,128)(2,1)S(1)} %copy-done.6, f32[128,1]{1,0:T(8,128)S(1)} %copy-done.8), custom_call_target="tpu_custom_call" | custom-call | flops 500000000 | bytes 1000000 | tf_op jit(solution)/shard_map/layers/pallas_call | solution.py:443
  (16 shorter events, 0.1 us)
Async XLA Ops:
  0.0 1.2 %copy-start = (bf16[32,8,2048]{2,1,0:T(8,128)(2,1)S(1)}, bf16[32,8,2048]{2,1,0:T(8,128)(2,1)}, u32[]{:S(2)}) copy-start(bf16[32,8,2048]{2,1,0:T(8,128)(2,1)} %param.6) | copy-start | bytes 3145732
  0.0 16.2 %copy-start.4 = (f32[32]{0:T(128)S(1)}, f32[32]{0:T(128)}, u32[]{:S(2)}) copy-start(f32[32]{0:T(128)} %param.11) | copy-start | bytes 388
  0.0 16.2 %copy-start.1 = (bf16[32,288]{1,0:T(8,128)(2,1)S(1)}, bf16[32,288]{1,0:T(8,128)(2,1)}, u32[]{:S(2)}) copy-start(bf16[32,288]{1,0:T(8,128)(2,1)} %refs_3_.1) | copy-start | bytes 55300
  0.0 16.2 %copy-start.3 = (f32[32]{0:T(128)S(1)}, f32[32]{0:T(128)}, u32[]{:S(2)}) copy-start(f32[32]{0:T(128)} %param.9) | copy-start | bytes 388
  0.0 16.2 %copy-start.2 = (f32[9,32]{1,0:T(8,128)S(1)}, f32[9,32]{1,0:T(8,128)}, u32[]{:S(2)}) copy-start(f32[9,32]{1,0:T(8,128)} %refs_1_.1) | copy-start | bytes 3460
  2.6 25.7 %all-to-all-start = ((bf16[32,2,2176]{2,1,0:T(2,128)(2,1)}), bf16[32,2,2176]{2,1,0:T(2,128)(2,1)}, u32[]{:S(2)}, u32[]{:S(2)}) async-start(bf16[32,2,2176]{2,1,0:T(2,128)(2,1)} %copy.10), calls=%async_computation | async-start | bytes 557056 | tf_op jit(solution)/shard_map/all_to_all | solution.py:472
  17.9 0.7 %copy-start.5 = (bf16[3,128,192]{2,1,0:T(8,128)(2,1)}, bf16[3,128,192]{2,1,0:T(8,128)(2,1)S(1)}, u32[]{:S(2)}) copy-start(bf16[3,128,192]{2,1,0:T(8,128)(2,1)S(1)} %get-tuple-element.17.refs_4_) | copy-start | bytes 442372
  18.6 0.6 %copy-start.7 = (f32[128,1]{1,0:T(8,128)}, f32[128,1]{1,0:T(8,128)S(1)}, u32[]{:S(2)}) copy-start(f32[128,1]{1,0:T(8,128)S(1)} %get-tuple-element.18.refs_5_) | copy-start | bytes 1540
  19.2 0.6 %copy-start.9 = (bf16[192,72]{1,0:T(8,128)(2,1)}, bf16[192,72]{1,0:T(8,128)(2,1)S(1)}, u32[]{:S(2)}) copy-start(bf16[192,72]{1,0:T(8,128)(2,1)S(1)} %get-tuple-element.15.refs_2_) | copy-start | bytes 82948
  19.8 0.6 %copy-start.11 = (f32[64,128]{1,0:T(8,128)}, f32[64,128]{1,0:T(8,128)S(1)}, u32[]{:S(2)}) copy-start(f32[64,128]{1,0:T(8,128)S(1)} %get-tuple-element.13.sin_ref) | copy-start | bytes 98308
  29.4 0.8 %copy-start.12 = (f32[64,128]{1,0:T(8,128)S(1)}, f32[64,128]{1,0:T(8,128)}, u32[]{:S(2)}) copy-start(f32[64,128]{1,0:T(8,128)} %copy-done.11) | copy-start | bytes 98308
  42.4 9.3 %all-to-all-start.1 = ((bf16[4,8,2048]{2,1,0:T(8,128)(2,1)}), bf16[4,8,2048]{2,1,0:T(8,128)(2,1)S(1)}, u32[]{:S(2)}, u32[]{:S(2)}) async-start(bf16[4,8,2048]{2,1,0:T(8,128)(2,1)} %backproject.1), calls=%async_computation.1 | async-start | bytes 262144 | tf_op jit(solution)/shard_map/all_to_all | solution.py:491
  51.7 0.9 %copy-start.6 = (bf16[3,128,192]{2,1,0:T(8,128)(2,1)S(1)}, bf16[3,128,192]{2,1,0:T(8,128)(2,1)}, u32[]{:S(2)}) copy-start(bf16[3,128,192]{2,1,0:T(8,128)(2,1)} %copy-done.5) | copy-start | bytes 442372
  52.6 0.8 %copy-start.8 = (f32[128,1]{1,0:T(8,128)S(1)}, f32[128,1]{1,0:T(8,128)}, u32[]{:S(2)}) copy-start(f32[128,1]{1,0:T(8,128)} %copy-done.7) | copy-start | bytes 1540
  53.5 0.8 %copy-start.10 = (bf16[192,72]{1,0:T(8,128)(2,1)S(1)}, bf16[192,72]{1,0:T(8,128)(2,1)}, u32[]{:S(2)}) copy-start(bf16[192,72]{1,0:T(8,128)(2,1)} %copy-done.9) | copy-start | bytes 82948

commit v3 on v2

--- a/solution.py
+++ b/solution.py
@@ -46,22 +46,45 @@
     return jnp.sum(picker * row, axis=1, keepdims=True)
 
 
+def pack_kernel(member_ref, shift_ref, x_ref, out_ref):
+    sheets, views, bins = x_ref.shape
+    share = out_ref.shape[1]
+    for member in range(views // share):
+
+        @pl.when(member_ref[0] == member)
+        def copy_rows():
+            out_ref[:, :, 0:bins] = x_ref[:, member * share : member * share + share, :]
+
+    lane = lax.broadcasted_iota(jnp.int32, (1, share, 128), 2)
+    shifts = jnp.zeros((1, share, 128), jnp.float32)
+    for view in range(views):
+        shifts = jnp.where(lane == view, shift_ref[view].astype(jnp.float32), shifts)
+    shifts = jnp.broadcast_to(shifts.astype(jnp.bfloat16), (sheets, share, 128))
+    out_ref[:, :, bins : bins + 128] = shifts
+
+
+def pack(member, view_shift, sinogram, share):
+    sheets, views, bins = sinogram.shape
+    smem = pl.BlockSpec(memory_space=pltpu.SMEM)
+    vmem = pl.BlockSpec(memory_space=pltpu.VMEM)
+    return pl.pallas_call(
+        pack_kernel,
+        out_shape=jax.ShapeDtypeStruct((sheets, share, bins + 128), jnp.bfloat16),
+        in_specs=[smem, smem, vmem],
+        out_specs=vmem,
+        compiler_params=pltpu.CompilerParams(vmem_limit_bytes=8 * 2**20),
+        cost_estimate=pl.CostEstimate(flops=1_000_000, bytes_accessed=1_500_000, transcendentals=0),
+        name="pack",
+    )(member, view_shift, sinogram)
+
+
 def prepare_kernel(
     views_total,
     share,
     view_count,
     member_ref,
-    conv_one_ref,
-    bias_one_ref,
-    conv_two_ref,
-    bias_two_ref,
     table_ref,
-    cos_ref,
-    sin_ref,
-    first_ref,
-    wide_one_ref,
-    second_ref,
-    wide_two_ref,
+    trig_ref,
 ):
     width = BLOCKS * BLOCK
 
@@ -82,12 +105,26 @@
             table_ref[start : start + 16, :] = high[:, cols]
             table_ref[BLOCK + start : BLOCK + start + 16, :] = low[:, cols]
 
-    view = lax.broadcasted_iota(jnp.int32, cos_ref.shape, 0)
+    views = trig_ref.shape[0] // 2
+    view = lax.broadcasted_iota(jnp.int32, (views, 128), 0)
     view = view // share * view_count + member_ref[0] * share + view % share
     angle = view.astype(jnp.float32) * (math.pi / views_total)
-    cos_ref[...] = jnp.cos(angle)
-    sin_ref[...] = jnp.sin(angle)
-
+    trig_ref[0:views, :] = jnp.cos(angle)
+    trig_ref[views : 2 * views, :] = jnp.sin(angle)
+
+
+def weights_kernel(
+    after_ref,
+    conv_one_ref,
+    bias_one_ref,
+    conv_two_ref,
+    bias_two_ref,
+    first_ref,
+    wide_one_ref,
+    second_ref,
+    wide_two_ref,
+):
+    del after_ref
     rows_one = CHAN * (ROW_DEV + 2)
     picker = selection((rows_one, CHAN), lambda row, col: (row & (CHAN - 1)) == col)
     wide_one_ref[...] = column_of(picker, bias_one_ref[...])
@@ -121,30 +158,43 @@
         second_ref[tap] = block.astype(jnp.bfloat16)
 
 
-def prepare(member, conv_one, bias_one, conv_two, bias_two, views, views_total, share, view_count):
+def prepare(member, views, views_total, share, view_count):
     vmem = pl.BlockSpec(memory_space=pltpu.VMEM)
 
     def body(*refs):
         prepare_kernel(views_total, share, view_count, *refs)
 
-    rows_one, rows_two = CHAN * (ROW_DEV + 2), CHAN * ROW_DEV
     return pl.pallas_call(
         body,
         out_shape=(
             jax.ShapeDtypeStruct((2 * BLOCK, BLOCKS * BLOCK), jnp.bfloat16),
-            jax.ShapeDtypeStruct((views, 128), jnp.float32),
-            jax.ShapeDtypeStruct((views, 128), jnp.float32),
+            jax.ShapeDtypeStruct((2 * views, 128), jnp.float32),
+        ),
+        in_specs=[pl.BlockSpec(memory_space=pltpu.SMEM)],
+        out_specs=(vmem,) * 2,
+        compiler_params=pltpu.CompilerParams(vmem_limit_bytes=8 * 2**20),
+        cost_estimate=pl.CostEstimate(flops=20_000_000, bytes_accessed=4_000_000, transcendentals=0),
+        name="prepare",
+    )(member)
+
+
+def spread_weights(after, conv_one, bias_one, conv_two, bias_two):
+    vmem = pl.BlockSpec(memory_space=pltpu.VMEM)
+    rows_one, rows_two = CHAN * (ROW_DEV + 2), CHAN * ROW_DEV
+    return pl.pallas_call(
+        weights_kernel,
+        out_shape=(
             jax.ShapeDtypeStruct((rows_one, 72), jnp.bfloat16),
             jax.ShapeDtypeStruct((rows_one, 1), jnp.float32),
             jax.ShapeDtypeStruct((3, rows_two, rows_one), jnp.bfloat16),
             jax.ShapeDtypeStruct((rows_two, 1), jnp.float32),
         ),
-        in_specs=[pl.BlockSpec(memory_space=pltpu.SMEM)] + [vmem] * 4,
-        out_specs=(vmem,) * 7,
-        compiler_params=pltpu.CompilerParams(vmem_limit_bytes=16 * 2**20),
-        cost_estimate=pl.CostEstimate(flops=20_000_000, bytes_accessed=4_000_000, transcendentals=0),
-        name="prepare",
-    )(member, conv_one, bias_one, conv_two, bias_two)
+        in_specs=[pl.BlockSpec(memory_space=pl.ANY)] + [vmem] * 4,
+        out_specs=(vmem,) * 4,
+        compiler_params=pltpu.CompilerParams(vmem_limit_bytes=8 * 2**20),
+        cost_estimate=pl.CostEstimate(flops=20_000_000, bytes_accessed=1_000_000, transcendentals=0),
+        name="weights",
+    )(after, conv_one, bias_one, conv_two, bias_two)
 
 
 def dot_turned(left, right):
@@ -166,9 +216,9 @@
 
 def backproject_kernel(
     first_ref,
+    member_ref,
     x_ref,
-    cos_ref,
-    sin_ref,
+    trig_ref,
     ramp_ref,
     out_ref,
     filt_ref,
@@ -181,91 +231,101 @@
     where_smem,
     sem,
 ):
-    views = x_ref.shape[0]
+    share = x_ref.shape[1]
+    views = x_ref.shape[0] * share
     first_y = first_ref[0]
     lane = lax.broadcasted_iota(jnp.int32, (views, 128), 1)
     lane_f = lane.astype(jnp.float32)
 
-    cosine = cos_ref[...]
-    sine = sin_ref[...]
-    center = CENTER + x_ref[:, BINS : BINS + 128].astype(jnp.float32)
+    cosine = trig_ref[0:views, :]
+    sine = trig_ref[views : 2 * views, :]
+    view = lax.broadcasted_iota(jnp.int32, (views, 128), 0)
+    shifts = x_ref[:, :, BINS : BINS + 128].reshape(views, 128).astype(jnp.float32)
+    own = lane == member_ref[0] * 2 + (view & 1)
+    center = CENTER + jnp.sum(jnp.where(own, shifts, 0.0), axis=1, keepdims=True)
+    center = jnp.broadcast_to(center, (views, 128))
     center_ref[...] = center
     tile_x = (lane & 15).astype(jnp.float32) * 128.0 - (WIDTH - 1) / 2.0
     set_y = first_y + 8.0 * (lane >> 4).astype(jnp.float32)
     lowest = jnp.minimum(tile_x * cosine, (tile_x + 127.0) * cosine) + set_y * sine + center
     window = ((lowest - 0.25) * (1.0 / 64.0)).astype(jnp.int32) - FIRST_WIN
     window = jnp.clip(window, 0, WINDOWS - 3)
-    view = lax.broadcasted_iota(jnp.int32, (views, 128), 0)
     where_ref[...] = window * views + view
     to_smem = pltpu.make_async_copy(where_ref, where_smem, sem)
     to_smem.start()
 
-    for step in range(2 * BLOCKS - 1):
-        delta = (step + 1) // 2 * (1 if step % 2 else -1)
-        low, high = max(0, -delta), min(BLOCKS, BLOCKS - delta)
-        left = jnp.concatenate(
-            [x_ref[:, BLOCK * block : BLOCK * block + BLOCK] for block in range(low, high)], axis=0
-        )
-        cols = slice(BLOCK * abs(delta), BLOCK * abs(delta) + BLOCK)
-        if delta >= 0:
-            left = jnp.concatenate([left, left], axis=1)
-            part = jnp.dot(left, ramp_ref[:, cols], preferred_element_type=jnp.float32)
-        else:
-            part = dot_turned(left, ramp_ref[0:BLOCK, cols]) + dot_turned(left, ramp_ref[BLOCK:, cols])
-        rows = slice(views * (low + delta), views * (high + delta))
-        if delta == 0:
-            filt_ref[rows, :] = part
-        else:
-            filt_ref[rows, :] += part
-
-    margin = MARGIN // 128
-    inner = BINS // 128
-
-    def raw(place):
-        half = 128 * (place % 2)
-        piece = filt_ref[views * (place // 2) : views * (place // 2) + views, half : half + 128]
-        return piece.astype(jnp.bfloat16).astype(jnp.float32)
-
-    largest = jnp.abs(raw(0))
-    for place in range(1, inner):
-        largest = jnp.maximum(largest, jnp.abs(raw(place)))
-    largest = jnp.max(largest, axis=1, keepdims=True)
-    largest = jnp.max(largest.reshape(views // SCALE_SET, SCALE_SET, 1), axis=1, keepdims=True)
-    largest = jnp.maximum(jnp.broadcast_to(largest, (views // SCALE_SET, SCALE_SET, 128)), 1e-30)
-    largest = largest.reshape(views, 128)
-    back_ref[...] = largest * (1.0 / (16383.0 * 65536.0))
-    scale = 16383.0 / largest
-    zero = jnp.zeros((views, 128), jnp.int32)
-
-    def filtered(block):
-        place = block - margin
-        if place < 0 or place >= inner:
-            return zero
-        return jnp.floor(raw(place) * scale + 0.5).astype(jnp.int32)
-
-    def turned(piece):
-        return pltpu.roll(piece, 127, 1)
-
-    def block_tables(block, piece, piece_turned, next_turned):
-        step = jnp.where(lane < 127, piece_turned, next_turned) - piece
-        return piece * 65536 + step, lane_f + (128.0 * block + 1.0)
-
-    first_block = FIRST_WIN // 2
-    piece = filtered(first_block)
-    piece_turned = turned(piece)
-    before = None
-    for block in range(first_block, (FIRST_WIN + WINDOWS) // 2 + 1):
-        following = filtered(block + 1)
-        following_turned = turned(following)
-        now = block_tables(block, piece, piece_turned, following_turned)
-        for ref, value, old in zip((word_ref, bin_ref), now, before or now):
-            row = (2 * block - FIRST_WIN) * views
-            if before is not None:
-                ref[row - views : row, :] = jnp.where(lane >= 64, old, value)
-            if 2 * block < FIRST_WIN + WINDOWS:
-                ref[row : row + views, :] = value
-        before = now
-        piece, piece_turned = following, following_turned
+    @pl.when(member_ref[0] >= 0)
+    def filter_and_tables():
+        pieces = [
+            x_ref[:, :, BLOCK * block : BLOCK * block + BLOCK].reshape(views, BLOCK)
+            for block in range(BLOCKS)
+        ]
+        for step in range(2 * BLOCKS - 1):
+            delta = (step + 1) // 2 * (1 if step % 2 else -1)
+            low, high = max(0, -delta), min(BLOCKS, BLOCKS - delta)
+            left = jnp.concatenate(
+                [pieces[block] for block in range(low, high)], axis=0
+            )
+            cols = slice(BLOCK * abs(delta), BLOCK * abs(delta) + BLOCK)
+            if delta >= 0:
+                left = jnp.concatenate([left, left], axis=1)
+                part = jnp.dot(left, ramp_ref[:, cols], preferred_element_type=jnp.float32)
+            else:
+                part = dot_turned(left, ramp_ref[0:BLOCK, cols]) + dot_turned(left, ramp_ref[BLOCK:, cols])
+            rows = slice(views * (low + delta), views * (high + delta))
+            if delta == 0:
+                filt_ref[rows, :] = part
+            else:
+                filt_ref[rows, :] += part
+
+        margin = MARGIN // 128
+        inner = BINS // 128
+
+        def raw(place):
+            half = 128 * (place % 2)
+            piece = filt_ref[views * (place // 2) : views * (place // 2) + views, half : half + 128]
+            return piece.astype(jnp.bfloat16).astype(jnp.float32)
+
+        largest = jnp.abs(raw(0))
+        for place in range(1, inner):
+            largest = jnp.maximum(largest, jnp.abs(raw(place)))
+        largest = jnp.max(largest, axis=1, keepdims=True)
+        largest = jnp.max(largest.reshape(views // SCALE_SET, SCALE_SET, 1), axis=1, keepdims=True)
+        largest = jnp.maximum(jnp.broadcast_to(largest, (views // SCALE_SET, SCALE_SET, 128)), 1e-30)
+        largest = largest.reshape(views, 128)
+        back_ref[...] = largest * (1.0 / (16383.0 * 65536.0))
+        scale = 16383.0 / largest
+        zero = jnp.zeros((views, 128), jnp.int32)
+
+        def filtered(block):
+            place = block - margin
+            if place < 0 or place >= inner:
+                return zero
+            return jnp.floor(raw(place) * scale + 0.5).astype(jnp.int32)
+
+        def turned(piece):
+            return pltpu.roll(piece, 127, 1)
+
+        def block_tables(block, piece, piece_turned, next_turned):
+            step = jnp.where(lane < 127, piece_turned, next_turned) - piece
+            return piece * 65536 + step, lane_f + (128.0 * block + 1.0)
+
+        first_block = FIRST_WIN // 2
+        piece = filtered(first_block)
+        piece_turned = turned(piece)
+        before = None
+        for block in range(first_block, (FIRST_WIN + WINDOWS) // 2 + 1):
+            following = filtered(block + 1)
+            following_turned = turned(following)
+            now = block_tables(block, piece, piece_turned, following_turned)
+            for ref, value, old in zip((word_ref, bin_ref), now, before or now):
+                row = (2 * block - FIRST_WIN) * views
+                if before is not None:
+                    ref[row - views : row, :] = jnp.where(lane >= 64, old, value)
+                if 2 * block < FIRST_WIN + WINDOWS:
+                    ref[row : row + views, :] = value
+            before = now
+            piece, piece_turned = following, following_turned
 
     acc_ref[...] = jnp.zeros_like(acc_ref)
     to_smem.wait()
@@ -287,8 +347,8 @@
 
         middle_x = part.astype(jnp.float32) * span + (span // 2 - WIDTH / 2.0 + 0.5)
         first_tile = row_set * TILES + part * count
-        cos_v = both(cos_ref, views_of)
-        base = rows_y * both(sin_ref, views_of) + both(center_ref, views_of)
+        cos_v = both(trig_ref, views_of)
+        base = rows_y * both(trig_ref, [views + view for view in views_of]) + both(center_ref, views_of)
         stride = cos_v * 128.0
         middle = (lane_one + middle_x) * cos_v + base
         middle_low = jnp.minimum(middle_x * cos_v, (middle_x + 127.0) * cos_v) + base
@@ -361,14 +421,14 @@
         out_ref[member] = lower.astype(jnp.bfloat16)
 
 
-def backproject(first_y, lines, cosine, sine, ramp):
-    views = lines.shape[0]
+def backproject(first_y, member, lines, trig, ramp):
+    views = lines.shape[0] * lines.shape[1]
     rows = WINDOWS * views
     vmem = pl.BlockSpec(memory_space=pltpu.VMEM)
     return pl.pallas_call(
         backproject_kernel,
         out_shape=jax.ShapeDtypeStruct((GROUP, 8, WIDTH), jnp.bfloat16),
-        in_specs=[pl.BlockSpec(memory_space=pltpu.SMEM), vmem, vmem, vmem, vmem],
+        in_specs=[pl.BlockSpec(memory_space=pltpu.SMEM)] * 2 + [vmem] * 3,
         out_specs=vmem,
         scratch_shapes=[
             pltpu.VMEM((BLOCKS * views, BLOCK), jnp.float32),
@@ -384,7 +444,7 @@
         compiler_params=pltpu.CompilerParams(vmem_limit_bytes=16 * 2**20),
         cost_estimate=pl.CostEstimate(flops=1_000_000_000, bytes_accessed=6_000_000, transcendentals=0),
         name="backproject",
-    )(first_y, lines, cosine, sine, ramp)
+    )(first_y, member, lines, trig, ramp)
 
 
 def layers_kernel(
@@ -465,31 +525,21 @@
     row_index = lax.axis_index("rows")
     member = row_index % GROUP
 
-    mine = lax.dynamic_slice_in_dim(sinogram, member * share, share, 1)
-    shift = lax.dynamic_slice_in_dim(view_shift, member * share, share, 0).astype(jnp.bfloat16)
-    shift = jnp.broadcast_to(shift[None, :, None], (sheets, share, 128))
-    sent = jnp.concatenate([mine, shift], axis=2)
+    member_one = member.astype(jnp.int32).reshape(1)
+    sent = pack(member_one, view_shift, sinogram, share)
     lines = lax.all_to_all(sent, "views", 0, 0, tiled=True)
-    lines = lines.reshape(view_groups * share, detector + 128)
-
-    ramp, cosine, sine, first, wide_one, second, wide_two = prepare(
-        member.astype(jnp.int32).reshape(1),
-        conv_one,
-        bias_one[None],
-        conv_two,
-        bias_two[None],
-        view_groups * share,
-        views_total,
-        share,
-        view_count,
-    )
+
+    ramp, trig = prepare(member_one, view_groups * share, views_total, share, view_count)
     first_row = (row_index - member) * ROW_DEV - 2
     first_y = first_row.astype(jnp.float32) - (image_rows - 1) / 2.0
 
-    partial_rows = backproject(first_y.reshape(1), lines, cosine, sine, ramp)
+    partial_rows = backproject(first_y.reshape(1), member_one, lines, trig, ramp)
     groups = [[GROUP * base + item for item in range(GROUP)] for base in range(row_groups // GROUP)]
     parts = lax.all_to_all(partial_rows, "rows", 0, 0, tiled=True, axis_index_groups=groups)
 
+    first, wide_one, second, wide_two = spread_weights(
+        partial_rows, conv_one, bias_one[None], conv_two, bias_two[None]
+    )
     row_base = (row_index * ROW_DEV).astype(jnp.int32).reshape(1)
     return layers(
         row_base,

time: 56.7 us -> 51.8 us (0.914)
  local copies, waits for them, and re-layouts: 8.63 us -> 1.9 us
  waiting for transfers between devices: 11.5 us -> 13.9 us
  other arithmetic: 0.84 us -> 0 us
  Pallas kernels: 15.8 us -> 16.4 us
    unnamed x27 -> x12, local copies, waits for them, and re-layouts: 6.3 us -> 1.9 us
    all_to_all x1, waiting for transfers between devices: 7.92 us -> 11.4 us  [local(): lines = lax.all_to_all(sent, 'views', 0, 0, tiled=True)]
    pallas_call x0 -> x2, Pallas kernels: none -> 2.49 us  [the longest x1 1.43 us: pack(): pl.pallas_call(pack_kernel, out_shape=jax.ShapeDtypeStruct((sheets, share...]
    all_to_all x1, waiting for transfers between devices: 3.57 us -> 2.48 us  [local(): lax.all_to_all(partial_rows, 'rows', 0, 0, tiled=True, axis_index_groups=...]
    reshape x1 -> x0, local copies, waits for them, and re-layouts: 1.06 us -> none  [local(): lines = lines.reshape(view_groups * share, detector + 128)]
    pallas_call x1, Pallas kernels: 1.61 us -> 0.63 us  [prepare(): pl.pallas_call(body, out_shape=(jax.ShapeDtypeStruct((2 * BLOCK, BLOCKS *...]
    pallas_call x1, Pallas kernels: 12.3 us -> 11.3 us  [backproject(): pl.pallas_call(backproject_kernel, out_shape=jax.ShapeDtypeStruct((GROUP,...]
    concatenate x1 -> x0, local copies, waits for them, and re-layouts: 0.92 us -> none  [local(): sent = jnp.concatenate([mine, shift], axis=2)]
where the time goes in v3:
time: 51.8 us; the launch traced here: 51.5 us
  starting transfers between devices  19.2 us (37%)
  Pallas kernels  16.4 us (32%)
  waiting for transfers between devices  13.9 us (27%)
  local copies, waits for them, and re-layouts  1.9 us (4%)
    all_to_all x1, starting transfers between devices, local(): lines = lax.all_to_all(sent, 'views', 0, 0, tiled=True)  13.5 us
    all_to_all x1, waiting for transfers between devices, local(): lines = lax.all_to_all(sent, 'views', 0, 0, tiled=True)  11.4 us
    pallas_call x1, Pallas kernels, backproject(): pl.pallas_call(backproject_kernel, out_shape=jax.ShapeDtypeStruct((GROUP,...  11.3 us
    all_to_all x1, starting transfers between devices, local(): lax.all_to_all(partial_rows, 'rows', 0, 0, tiled=True, axis_index_groups=...  5.76 us
    all_to_all x1, waiting for transfers between devices, local(): lax.all_to_all(partial_rows, 'rows', 0, 0, tiled=True, axis_index_groups=...  2.48 us
    pallas_call x1, Pallas kernels, layers(): pl.pallas_call(body, out_shape=jax.ShapeDtypeStruct((1, CHAN, ROW_DEV, WI...  1.93 us
    unnamed x12, local copies, waits for them, and re-layouts  1.9 us
    pallas_call x1, Pallas kernels, pack(): pl.pallas_call(pack_kernel, out_shape=jax.ShapeDtypeStruct((sheets, share...  1.43 us
  transfers between devices with their start and end apart: 2, of which 2 were waited for; matrix products, arithmetic and copies ran while one was open for 0% of the time, Pallas kernels for 3%

profile of v3, /device:TPU:1, one launch (start us, length us, event | category | flops | bytes accessed | tf_op | source)
XLA Modules:
  0.0 51.5 jit_solution(4129673339341179411)
XLA Ops:
  0.0 0.0 copy-start
  0.0 1.2 %copy-done = bf16[32,8,2048]{2,1,0:T(8,128)(2,1)S(1)} copy-done((bf16[32,8,2048]{2,1,0:T(8,128)(2,1)S(1)}, bf16[32,8,2048]{2,1,0:T(8,128)(2,1)}, u32[]{:S(2)}) %copy-start) | copy-done | bytes 1048600
  1.2 0.0 copy-start.3
  1.2 0.7 %copy-done.3 = s32[8]{0:T(128)S(1)} copy-done((s32[8]{0:T(128)S(1)}, s32[8]{0:T(128)}, u32[]{:S(2)}) %copy-start.3) | copy-done | bytes 56
  1.9 1.4 %pack.1 = bf16[32,2,2176]{2,1,0:T(2,128)(2,1)} custom-call(s32[1]{0:T(128)} %bitcast.2.member_ref.refs_0_, s32[8]{0:T(128)S(1)} %copy-done.3, bf16[32,8,2048]{2,1,0:T(8,128)(2,1)S(1)} %copy-done), custom_call_target="tpu_custom_call" | custom-call | flops 1000000 | bytes 1500000 | tf_op jit(solution)/shard_map/pack/pallas_call | solution.py:70
  3.3 13.5 %all-to-all-start = ((bf16[32,2,2176]{2,1,0:T(2,128)(2,1)}), bf16[32,2,2176]{2,1,0:T(2,128)(2,1)S(1)}, u32[]{:S(2)}, u32[]{:S(2)}) async-start(bf16[32,2,2176]{2,1,0:T(2,128)(2,1)} %pack.1), calls=%async_computation | async-start | bytes 557056 | tf_op jit(solution)/shard_map/all_to_all | solution.py:530
  16.8 0.0 copy-start.1
  16.8 0.0 copy-start.2
  16.8 0.0 copy-start.4
  16.8 0.0 copy-start.5
  16.8 0.6 %prepare.1 = (bf16[512,2048]{1,0:T(8,128)(2,1)S(1)}, f32[128,128]{1,0:T(8,128)S(1)}) custom-call(s32[1]{0:T(128)} %bitcast.2.member_ref.refs_0_), custom_call_target="tpu_custom_call" | custom-call | flops 20000000 | bytes 4000000 | tf_op jit(solution)/shard_map/prepare/pallas_call | solution.py:167
  17.5 11.4 %all-to-all-done.x_ref = bf16[32,2,2176]{2,1,0:T(2,128)(2,1)S(1)} async-done(((bf16[32,2,2176]{2,1,0:T(2,128)(2,1)}), bf16[32,2,2176]{2,1,0:T(2,128)(2,1)S(1)}, u32[]{:S(2)}, u32[]{:S(2)}) %all-to-all-start) | async-done | bytes 278560 | tf_op jit(solution)/shard_map/all_to_all | solution.py:530
  28.9 11.3 %backproject.1.after_ref = bf16[4,8,2048]{2,1,0:T(8,128)(2,1)} custom-call(f32[1]{0:T(128)} %bitcast.1.first_ref, s32[1]{0:T(128)} %bitcast.2.member_ref.refs_0_, bf16[32,2,2176]{2,1,0:T(2,128)(2,1)S(1)} %all-to-all-done.x_ref, f32[128,128]{1,0:T(8,128)S(1)} %get-tuple-element.11.trig_ref, bf16[512,2048]{1,0:T(8,128)(2,1)S(1)} %get-tuple-element.12.ramp_ref), custom_call_target="tpu_custom_call" | custom-call | flops 1000000000 | bytes 6000000 | tf_op jit(solution)/shard_map/backproject/pallas_call | solution.py:428
  40.2 5.8 %all-to-all-start.1 = ((bf16[4,8,2048]{2,1,0:T(8,128)(2,1)}), bf16[4,8,2048]{2,1,0:T(8,128)(2,1)S(1)}, u32[]{:S(2)}, u32[]{:S(2)}) async-start(bf16[4,8,2048]{2,1,0:T(8,128)(2,1)} %backproject.1.after_ref), calls=%async_computation.1 | async-start | bytes 262144 | tf_op jit(solution)/shard_map/all_to_all | solution.py:538
  46.0 0.0 copy-done.1
  46.0 0.0 copy-done.2
  46.0 0.0 copy-done.4
  46.0 0.0 copy-done.5
  46.0 1.1 %weights.1 = (bf16[192,72]{1,0:T(8,128)(2,1)S(1)}, f32[192,1]{1,0:T(8,128)S(1)}, bf16[3,128,192]{2,1,0:T(8,128)(2,1)S(1)}, f32[128,1]{1,0:T(8,128)S(1)}) custom-call(bf16[4,8,2048]{2,1,0:T(8,128)(2,1)} %backproject.1.after_ref, f32[9,32]{1,0:T(8,128)S(1)} %copy-done.2, f32[1,32]{1,0:T(1,128)S(1)} %bitcast.5, bf16[32,288]{1,0:T(8,128)(2,1)S(1)} %copy-done.1, ...), custom_call_target="tpu_custom_call" | custom-call | flops 20000000 | bytes 1000000 | tf_op jit(solution)/shard_map/weights/pallas_call | solution.py:184
  47.0 2.5 %all-to-all-done.1.refs_1_ = bf16[4,8,2048]{2,1,0:T(8,128)(2,1)S(1)} async-done(((bf16[4,8,2048]{2,1,0:T(8,128)(2,1)}), bf16[4,8,2048]{2,1,0:T(8,128)(2,1)S(1)}, u32[]{:S(2)}, u32[]{:S(2)}) %all-to-all-start.1) | async-done | bytes 131104 | tf_op jit(solution)/shard_map/all_to_all | solution.py:538
  49.5 1.9 %layers.1 = bf16[1,32,4,2048]{3,2,1,0:T(4,128)(2,1)} custom-call(s32[1]{0:T(128)} %bitcast.refs_0_, bf16[4,8,2048]{2,1,0:T(8,128)(2,1)S(1)} %all-to-all-done.1.refs_1_, bf16[192,72]{1,0:T(8,128)(2,1)S(1)} %get-tuple-element.13.refs_2_, f32[192,1]{1,0:T(8,128)S(1)} %get-tuple-element.14.refs_3_, bf16[3,128,192]{2,1,0:T(8,128)(2,1)S(1)} %get-tuple-element.15.refs_4_, ...), custom_call_target="tpu_custom_call" | custom-call | flops 500000000 | bytes 1000000 | tf_op jit(solution)/shard_map/layers/pallas_call | solution.py:503
Async XLA Ops:
  0.0 1.2 %copy-start = (bf16[32,8,2048]{2,1,0:T(8,128)(2,1)S(1)}, bf16[32,8,2048]{2,1,0:T(8,128)(2,1)}, u32[]{:S(2)}) copy-start(bf16[32,8,2048]{2,1,0:T(8,128)(2,1)} %x_ref.1) | copy-start | bytes 3145732
  1.2 0.7 %copy-start.3 = (s32[8]{0:T(128)S(1)}, s32[8]{0:T(128)}, u32[]{:S(2)}) copy-start(s32[8]{0:T(128)} %shift_ref.1) | copy-start | bytes 100
  3.3 25.6 %all-to-all-start = ((bf16[32,2,2176]{2,1,0:T(2,128)(2,1)}), bf16[32,2,2176]{2,1,0:T(2,128)(2,1)S(1)}, u32[]{:S(2)}, u32[]{:S(2)}) async-start(bf16[32,2,2176]{2,1,0:T(2,128)(2,1)} %pack.1), calls=%async_computation | async-start | bytes 557056 | tf_op jit(solution)/shard_map/all_to_all | solution.py:530
  16.8 29.2 %copy-start.1 = (bf16[32,288]{1,0:T(8,128)(2,1)S(1)}, bf16[32,288]{1,0:T(8,128)(2,1)}, u32[]{:S(2)}) copy-start(bf16[32,288]{1,0:T(8,128)(2,1)} %conv_two_ref.1) | copy-start | bytes 55300
  16.8 29.2 %copy-start.2 = (f32[9,32]{1,0:T(8,128)S(1)}, f32[9,32]{1,0:T(8,128)}, u32[]{:S(2)}) copy-start(f32[9,32]{1,0:T(8,128)} %conv_one_ref.1) | copy-start | bytes 3460
  16.8 29.2 %copy-start.4 = (f32[32]{0:T(128)S(1)}, f32[32]{0:T(128)}, u32[]{:S(2)}) copy-start(f32[32]{0:T(128)} %param.9) | copy-start | bytes 388
  16.8 29.2 %copy-start.5 = (f32[32]{0:T(128)S(1)}, f32[32]{0:T(128)}, u32[]{:S(2)}) copy-start(f32[32]{0:T(128)} %param.11) | copy-start | bytes 388
  40.2 9.3 %all-to-all-start.1 = ((bf16[4,8,2048]{2,1,0:T(8,128)(2,1)}), bf16[4,8,2048]{2,1,0:T(8,128)(2,1)S(1)}, u32[]{:S(2)}, u32[]{:S(2)}) async-start(bf16[4,8,2048]{2,1,0:T(8,128)(2,1)} %backproject.1.after_ref), calls=%async_computation.1 | async-start | bytes 262144 | tf_op jit(solution)/shard_map/all_to_all | solution.py:538

commit v4 on v3

--- a/solution.py
+++ b/solution.py
@@ -44,38 +44,6 @@
 
 def column_of(picker, row):
     return jnp.sum(picker * row, axis=1, keepdims=True)
-
-
-def pack_kernel(member_ref, shift_ref, x_ref, out_ref):
-    sheets, views, bins = x_ref.shape
-    share = out_ref.shape[1]
-    for member in range(views // share):
-
-        @pl.when(member_ref[0] == member)
-        def copy_rows():
-            out_ref[:, :, 0:bins] = x_ref[:, member * share : member * share + share, :]
-
-    lane = lax.broadcasted_iota(jnp.int32, (1, share, 128), 2)
-    shifts = jnp.zeros((1, share, 128), jnp.float32)
-    for view in range(views):
-        shifts = jnp.where(lane == view, shift_ref[view].astype(jnp.float32), shifts)
-    shifts = jnp.broadcast_to(shifts.astype(jnp.bfloat16), (sheets, share, 128))
-    out_ref[:, :, bins : bins + 128] = shifts
-
-
-def pack(member, view_shift, sinogram, share):
-    sheets, views, bins = sinogram.shape
-    smem = pl.BlockSpec(memory_space=pltpu.SMEM)
-    vmem = pl.BlockSpec(memory_space=pltpu.VMEM)
-    return pl.pallas_call(
-        pack_kernel,
-        out_shape=jax.ShapeDtypeStruct((sheets, share, bins + 128), jnp.bfloat16),
-        in_specs=[smem, smem, vmem],
-        out_specs=vmem,
-        compiler_params=pltpu.CompilerParams(vmem_limit_bytes=8 * 2**20),
-        cost_estimate=pl.CostEstimate(flops=1_000_000, bytes_accessed=1_500_000, transcendentals=0),
-        name="pack",
-    )(member, view_shift, sinogram)
 
 
 def prepare_kernel(
@@ -525,10 +493,12 @@
     row_index = lax.axis_index("rows")
     member = row_index % GROUP
 
+    mine = lax.dynamic_slice_in_dim(sinogram, member * share, share, 1)
+    shift = jnp.pad(view_shift.astype(jnp.bfloat16), (0, 128 - view_count))
+    sent = jnp.concatenate([mine, jnp.broadcast_to(shift, (sheets, share, 128))], axis=2)
+    lines = lax.all_to_all(sent, "views", 0, 0, tiled=True)
+
     member_one = member.astype(jnp.int32).reshape(1)
-    sent = pack(member_one, view_shift, sinogram, share)
-    lines = lax.all_to_all(sent, "views", 0, 0, tiled=True)
-
     ramp, trig = prepare(member_one, view_groups * share, views_total, share, view_count)
     first_row = (row_index - member) * ROW_DEV - 2
     first_y = first_row.astype(jnp.float32) - (image_rows - 1) / 2.0

time: 51.8 us -> 50.9 us (0.983)
  other arithmetic: 0 us -> 1.75 us
  Pallas kernels: 16.4 us -> 14.9 us
  local copies, waits for them, and re-layouts: 1.9 us -> 0.79 us
    pallas_call x1 -> x0, Pallas kernels: 1.43 us -> none  [pack(): pl.pallas_call(pack_kernel, out_shape=jax.ShapeDtypeStruct((sheets, share...]
    unnamed x12 -> x10, local copies, waits for them, and re-layouts: 1.9 us -> 0.51 us
    concatenate x0 -> x2, other arithmetic: none -> 1 us  [local(): jnp.concatenate([mine, jnp.broadcast_to(shift, (sheets, share, 128))], ax...]
    convert_element_type x0 -> x1, other arithmetic: none -> 0.75 us  [local(): shift = jnp.pad(view_shift.astype(jnp.bfloat16), (0, 128 - view_count))]
where the time goes in v4:
time: 50.9 us; the launch traced here: 50.6 us
  starting transfers between devices  19.2 us (38%)
  Pallas kernels  14.9 us (29%)
  waiting for transfers between devices  13.9 us (27%)
  other arithmetic  1.75 us (3%)
  local copies, waits for them, and re-layouts  0.79 us (2%)
    all_to_all x1, starting transfers between devices, local(): lines = lax.all_to_all(sent, 'views', 0, 0, tiled=True)  13.5 us
    all_to_all x1, waiting for transfers between devices, local(): lines = lax.all_to_all(sent, 'views', 0, 0, tiled=True)  11.4 us
    pallas_call x1, Pallas kernels, backproject(): pl.pallas_call(backproject_kernel, out_shape=jax.ShapeDtypeStruct((GROUP,...  11.3 us
    all_to_all x1, starting transfers between devices, local(): lax.all_to_all(partial_rows, 'rows', 0, 0, tiled=True, axis_index_groups=...  5.76 us
    all_to_all x1, waiting for transfers between devices, local(): lax.all_to_all(partial_rows, 'rows', 0, 0, tiled=True, axis_index_groups=...  2.48 us
    pallas_call x1, Pallas kernels, layers(): pl.pallas_call(body, out_shape=jax.ShapeDtypeStruct((1, CHAN, ROW_DEV, WI...  1.93 us
    pallas_call x1, Pallas kernels, spread_weights(): pl.pallas_call(weights_kernel, out_shape=(jax.ShapeDtypeStruct((rows_one,...  1.06 us
  transfers between devices with their start and end apart: 2, of which 2 were waited for; matrix products, arithmetic and copies ran while one was open for 0% of the time, Pallas kernels for 3%

profile of v4, /device:TPU:1, one launch (start us, length us, event | category | flops | bytes accessed | tf_op | source)
XLA Modules:
  0.0 50.6 jit_solution(6995530283384113738)
XLA Ops:
  0.0 0.0 copy-start
  0.0 0.7 %convert_element_type.9 = bf16[8]{0:T(256)(128)(2,1)S(1)} convert(s32[8]{0:T(128)} %param.7) | non-fusion elementwise | flops 8 | bytes 48 | tf_op jit(solution)/shard_map/convert_element_type | solution.py:497
  0.8 0.5 copy-done
  1.2 0.3 constant_dynamic-slice_fusion
  1.5 1.0 %pad_maximum_fusion = bf16[32,2,2176]{2,1,0:T(2,128)(2,1)} fusion(bf16[32,2,2048]{2,1,0:T(2,128)(2,1)S(1)} %constant_dynamic-slice_fusion, bf16[2176]{0:T(1024)(128)(2,1)S(1)} %fusion), kind=kLoop, calls=%fused_computation | loop fusion | flops 557056 | bytes 545024 | tf_op jit(solution)/shard_map/concatenate | solution.py:498
  2.5 13.5 %all-to-all-start = ((bf16[32,2,2176]{2,1,0:T(2,128)(2,1)}), bf16[32,2,2176]{2,1,0:T(2,128)(2,1)S(1)}, u32[]{:S(2)}, u32[]{:S(2)}) async-start(bf16[32,2,2176]{2,1,0:T(2,128)(2,1)} %pad_maximum_fusion), calls=%async_computation | async-start | bytes 557056 | tf_op jit(solution)/shard_map/all_to_all | solution.py:499
  16.0 0.0 copy-start.1
  16.0 0.0 copy-start.2
  16.0 0.0 copy-start.3
  16.0 0.0 copy-start.4
  16.0 0.6 %prepare.1 = (bf16[512,2048]{1,0:T(8,128)(2,1)S(1)}, f32[128,128]{1,0:T(8,128)S(1)}) custom-call(s32[1]{0:T(128)} %bitcast.2.refs_0_.member_ref), custom_call_target="tpu_custom_call" | custom-call | flops 20000000 | bytes 4000000 | tf_op jit(solution)/shard_map/prepare/pallas_call | solution.py:135
  16.7 11.4 %all-to-all-done.x_ref = bf16[32,2,2176]{2,1,0:T(2,128)(2,1)S(1)} async-done(((bf16[32,2,2176]{2,1,0:T(2,128)(2,1)}), bf16[32,2,2176]{2,1,0:T(2,128)(2,1)S(1)}, u32[]{:S(2)}, u32[]{:S(2)}) %all-to-all-start) | async-done | bytes 278560 | tf_op jit(solution)/shard_map/all_to_all | solution.py:499
  28.1 11.3 %backproject.1.after_ref = bf16[4,8,2048]{2,1,0:T(8,128)(2,1)} custom-call(f32[1]{0:T(128)} %bitcast.1.first_ref, s32[1]{0:T(128)} %bitcast.2.refs_0_.member_ref, bf16[32,2,2176]{2,1,0:T(2,128)(2,1)S(1)} %all-to-all-done.x_ref, f32[128,128]{1,0:T(8,128)S(1)} %get-tuple-element.11.trig_ref, bf16[512,2048]{1,0:T(8,128)(2,1)S(1)} %get-tuple-element.12.ramp_ref), custom_call_target="tpu_custom_call" | custom-call | flops 1000000000 | bytes 6000000 | tf_op jit(solution)/shard_map/backproject/pallas_call | solution.py:396
  39.4 5.8 %all-to-all-start.1 = ((bf16[4,8,2048]{2,1,0:T(8,128)(2,1)}), bf16[4,8,2048]{2,1,0:T(8,128)(2,1)S(1)}, u32[]{:S(2)}, u32[]{:S(2)}) async-start(bf16[4,8,2048]{2,1,0:T(8,128)(2,1)} %backproject.1.after_ref), calls=%async_computation.1 | async-start | bytes 262144 | tf_op jit(solution)/shard_map/all_to_all | solution.py:508
  45.2 0.0 copy-done.1
  45.2 0.0 copy-done.2
  45.2 0.0 copy-done.3
  45.2 0.0 copy-done.4
  45.2 1.1 %weights.1 = (bf16[192,72]{1,0:T(8,128)(2,1)S(1)}, f32[192,1]{1,0:T(8,128)S(1)}, bf16[3,128,192]{2,1,0:T(8,128)(2,1)S(1)}, f32[128,1]{1,0:T(8,128)S(1)}) custom-call(bf16[4,8,2048]{2,1,0:T(8,128)(2,1)} %backproject.1.after_ref, f32[9,32]{1,0:T(8,128)S(1)} %copy-done.2, f32[1,32]{1,0:T(1,128)S(1)} %bitcast.5, bf16[32,288]{1,0:T(8,128)(2,1)S(1)} %copy-done.1, ...), custom_call_target="tpu_custom_call" | custom-call | flops 20000000 | bytes 1000000 | tf_op jit(solution)/shard_map/weights/pallas_call | solution.py:152
  46.2 2.5 %all-to-all-done.1.refs_1_ = bf16[4,8,2048]{2,1,0:T(8,128)(2,1)S(1)} async-done(((bf16[4,8,2048]{2,1,0:T(8,128)(2,1)}), bf16[4,8,2048]{2,1,0:T(8,128)(2,1)S(1)}, u32[]{:S(2)}, u32[]{:S(2)}) %all-to-all-start.1) | async-done | bytes 131104 | tf_op jit(solution)/shard_map/all_to_all | solution.py:508
  48.7 1.9 %layers.1 = bf16[1,32,4,2048]{3,2,1,0:T(4,128)(2,1)} custom-call(s32[1]{0:T(128)} %bitcast.refs_0_, bf16[4,8,2048]{2,1,0:T(8,128)(2,1)S(1)} %all-to-all-done.1.refs_1_, bf16[192,72]{1,0:T(8,128)(2,1)S(1)} %get-tuple-element.13.refs_2_, f32[192,1]{1,0:T(8,128)S(1)} %get-tuple-element.14.refs_3_, bf16[3,128,192]{2,1,0:T(8,128)(2,1)S(1)} %get-tuple-element.15.refs_4_, ...), custom_call_target="tpu_custom_call" | custom-call | flops 500000000 | bytes 1000000 | tf_op jit(solution)/shard_map/layers/pallas_call | solution.py:471
  (1 shorter events, 0.0 us)
Async XLA Ops:
  0.0 1.2 %copy-start = (bf16[32,8,2048]{2,1,0:T(8,128)(2,1)S(1)}, bf16[32,8,2048]{2,1,0:T(8,128)(2,1)}, u32[]{:S(2)}) copy-start(bf16[32,8,2048]{2,1,0:T(8,128)(2,1)} %param.6) | copy-start | bytes 3145732
  2.5 25.6 %all-to-all-start = ((bf16[32,2,2176]{2,1,0:T(2,128)(2,1)}), bf16[32,2,2176]{2,1,0:T(2,128)(2,1)S(1)}, u32[]{:S(2)}, u32[]{:S(2)}) async-start(bf16[32,2,2176]{2,1,0:T(2,128)(2,1)} %pad_maximum_fusion), calls=%async_computation | async-start | bytes 557056 | tf_op jit(solution)/shard_map/all_to_all | solution.py:499
  16.0 29.2 %copy-start.1 = (bf16[32,288]{1,0:T(8,128)(2,1)S(1)}, bf16[32,288]{1,0:T(8,128)(2,1)}, u32[]{:S(2)}) copy-start(bf16[32,288]{1,0:T(8,128)(2,1)} %conv_two_ref.1) | copy-start | bytes 55300
  16.0 29.2 %copy-start.2 = (f32[9,32]{1,0:T(8,128)S(1)}, f32[9,32]{1,0:T(8,128)}, u32[]{:S(2)}) copy-start(f32[9,32]{1,0:T(8,128)} %conv_one_ref.1) | copy-start | bytes 3460
  16.0 29.2 %copy-start.3 = (f32[32]{0:T(128)S(1)}, f32[32]{0:T(128)}, u32[]{:S(2)}) copy-start(f32[32]{0:T(128)} %param.9) | copy-start | bytes 388
  16.0 29.2 %copy-start.4 = (f32[32]{0:T(128)S(1)}, f32[32]{0:T(128)}, u32[]{:S(2)}) copy-start(f32[32]{0:T(128)} %param.11) | copy-start | bytes 388
  39.4 9.3 %all-to-all-start.1 = ((bf16[4,8,2048]{2,1,0:T(8,128)(2,1)}), bf16[4,8,2048]{2,1,0:T(8,128)(2,1)S(1)}, u32[]{:S(2)}, u32[]{:S(2)}) async-start(bf16[4,8,2048]{2,1,0:T(8,128)(2,1)} %backproject.1.after_ref), calls=%async_computation.1 | async-start | bytes 262144 | tf_op jit(solution)/shard_map/all_to_all | solution.py:508

commit v5 on v4

--- a/solution.py
+++ b/solution.py
@@ -15,13 +15,15 @@
 GROUP = 4
 BLOCK = 256
 BLOCKS = BINS // BLOCK
-CENTER = (BINS - 1) / 2.0 + MARGIN
 FIRST_WIN = 4
-WINDOWS = 38
+WINDOWS = 36
+HALF_TURN = 64
+PAIRS = 32
+SLOTS = 40
+CENTER = (BINS - 1) / 2.0 + MARGIN - HALF_TURN
 TILES = WIDTH // 128
 ROW_SETS = 3
 RAMP_COLS = BLOCKS * BLOCK
-VIEW_STEP = 64
 SCALE_SET = 8
 PARTS = 2
 
@@ -46,9 +48,28 @@
     return jnp.sum(picker * row, axis=1, keepdims=True)
 
 
+def source_of(row, member):
+    slot = row & (PAIRS - 1)
+    mirror = row >> 5
+    turned = jnp.where(mirror == 1, PAIRS - 1 - slot, slot)
+    zero_even = jnp.where(mirror == 1, PAIRS + 15 - slot, slot - 15)
+    zero_last = jnp.where(mirror == 1, PAIRS // 2, 0)
+    zero_group = jnp.where(slot == PAIRS - 1, zero_last, zero_even)
+    zero_group = jnp.where(slot < PAIRS // 2, turned, zero_group)
+    zero_which = jnp.where(slot < PAIRS // 2, 1, 0)
+    group = jnp.where(member == 0, zero_group, turned)
+    which = jnp.where(member == 0, zero_which, mirror)
+    return group, which
+
+
+def residue_of(which, member, view_count):
+    return jnp.where(
+        which == 0, member, jnp.where(member == 0, view_count // 2, view_count - member)
+    )
+
+
 def prepare_kernel(
     views_total,
-    share,
     view_count,
     member_ref,
     table_ref,
@@ -73,12 +94,14 @@
             table_ref[start : start + 16, :] = high[:, cols]
             table_ref[BLOCK + start : BLOCK + start + 16, :] = low[:, cols]
 
-    views = trig_ref.shape[0] // 2
-    view = lax.broadcasted_iota(jnp.int32, (views, 128), 0)
-    view = view // share * view_count + member_ref[0] * share + view % share
+    slot = lax.broadcasted_iota(jnp.int32, (SLOTS, 128), 0)
+    member = jnp.full((SLOTS, 128), member_ref[0], jnp.int32)
+    group, which = source_of(slot & (PAIRS - 1), member)
+    view = group * view_count + residue_of(which, member, view_count)
+    view = jnp.where(slot < PAIRS, view, views_total // 2)
     angle = view.astype(jnp.float32) * (math.pi / views_total)
-    trig_ref[0:views, :] = jnp.cos(angle)
-    trig_ref[views : 2 * views, :] = jnp.sin(angle)
+    trig_ref[0:SLOTS, :] = jnp.cos(angle)
+    trig_ref[SLOTS : 2 * SLOTS, :] = jnp.sin(angle)
 
 
 def weights_kernel(
@@ -126,17 +149,17 @@
         second_ref[tap] = block.astype(jnp.bfloat16)
 
 
-def prepare(member, views, views_total, share, view_count):
+def prepare(member, views_total, view_count):
     vmem = pl.BlockSpec(memory_space=pltpu.VMEM)
 
     def body(*refs):
-        prepare_kernel(views_total, share, view_count, *refs)
+        prepare_kernel(views_total, view_count, *refs)
 
     return pl.pallas_call(
         body,
         out_shape=(
             jax.ShapeDtypeStruct((2 * BLOCK, BLOCKS * BLOCK), jnp.bfloat16),
-            jax.ShapeDtypeStruct((2 * views, 128), jnp.float32),
+            jax.ShapeDtypeStruct((2 * SLOTS, 128), jnp.float32),
         ),
         in_specs=[pl.BlockSpec(memory_space=pltpu.SMEM)],
         out_specs=(vmem,) * 2,
@@ -193,7 +216,6 @@
     word_ref,
     bin_ref,
     back_ref,
-    center_ref,
     where_ref,
     acc_ref,
     where_smem,
@@ -202,32 +224,48 @@
     share = x_ref.shape[1]
     views = x_ref.shape[0] * share
     first_y = first_ref[0]
+    member = member_ref[0]
     lane = lax.broadcasted_iota(jnp.int32, (views, 128), 1)
-    lane_f = lane.astype(jnp.float32)
-
-    cosine = trig_ref[0:views, :]
-    sine = trig_ref[views : 2 * views, :]
-    view = lax.broadcasted_iota(jnp.int32, (views, 128), 0)
-    shifts = x_ref[:, :, BINS : BINS + 128].reshape(views, 128).astype(jnp.float32)
-    own = lane == member_ref[0] * 2 + (view & 1)
-    center = CENTER + jnp.sum(jnp.where(own, shifts, 0.0), axis=1, keepdims=True)
-    center = jnp.broadcast_to(center, (views, 128))
-    center_ref[...] = center
-    tile_x = (lane & 15).astype(jnp.float32) * 128.0 - (WIDTH - 1) / 2.0
-    set_y = first_y + 8.0 * (lane >> 4).astype(jnp.float32)
-    lowest = jnp.minimum(tile_x * cosine, (tile_x + 127.0) * cosine) + set_y * sine + center
+
+    slot_lane = lax.broadcasted_iota(jnp.int32, (SLOTS, 128), 1)
+    slot_row = lax.broadcasted_iota(jnp.int32, (SLOTS, 128), 0)
+    cosine = trig_ref[0:SLOTS, :]
+    sine = trig_ref[SLOTS : 2 * SLOTS, :]
+    tile_x = (slot_lane & 15).astype(jnp.float32) * 128.0 - (WIDTH - 1) / 2.0
+    set_y = first_y + 8.0 * (slot_lane >> 4).astype(jnp.float32)
+    lowest = jnp.minimum(tile_x * cosine, (tile_x + 127.0) * cosine) + set_y * sine + CENTER
     window = ((lowest - 0.25) * (1.0 / 64.0)).astype(jnp.int32) - FIRST_WIN
-    window = jnp.clip(window, 0, WINDOWS - 3)
-    where_ref[...] = window * views + view
+    where_ref[...] = jnp.clip(window, 0, WINDOWS - 3) * views
+    first_bin = (slot_row + FIRST_WIN) * 64 + slot_lane
+    halves = jnp.where(slot_lane >= 64, -64, 64)
+    bin_ref[...] = (first_bin + 1 + jnp.where((slot_row & 1) == 1, halves, 0)).astype(jnp.float32)
     to_smem = pltpu.make_async_copy(where_ref, where_smem, sem)
     to_smem.start()
 
     @pl.when(member_ref[0] >= 0)
     def filter_and_tables():
+        row = lax.broadcasted_iota(jnp.int32, (views, views), 0)
+        col = lax.broadcasted_iota(jnp.int32, (views, views), 1)
+        group, which = source_of(row, jnp.full((views, views), member, jnp.int32))
+        order = jnp.where(col == group * share + which, 1.0, 0.0).astype(jnp.bfloat16)
+
+        def in_order(low, high):
+            part = x_ref[:, :, low:high].reshape(views, high - low)
+            return jnp.dot(order, part, preferred_element_type=jnp.float32)
+
         pieces = [
-            x_ref[:, :, BLOCK * block : BLOCK * block + BLOCK].reshape(views, BLOCK)
+            in_order(BLOCK * block, BLOCK * block + BLOCK).astype(jnp.bfloat16)
             for block in range(BLOCKS)
         ]
+        row = lax.broadcasted_iota(jnp.int32, (views, 128), 0)
+        everyone = jnp.full((views, 128), member, jnp.int32)
+        group, which = source_of(row, everyone)
+        own = lane == residue_of(which, everyone, 8)
+        turn = jnp.sum(jnp.where(own, in_order(BINS, BINS + 128), 0.0), axis=1, keepdims=True)
+        turn = jnp.broadcast_to(turn, (views, 128)).astype(jnp.int32) + HALF_TURN
+        turn_index = (lane + turn) & 127
+        turn_near = lane >= turn
+
         for step in range(2 * BLOCKS - 1):
             delta = (step + 1) // 2 * (1 if step % 2 else -1)
             low, high = max(0, -delta), min(BLOCKS, BLOCKS - delta)
@@ -274,25 +312,31 @@
         def turned(piece):
             return pltpu.roll(piece, 127, 1)
 
-        def block_tables(block, piece, piece_turned, next_turned):
-            step = jnp.where(lane < 127, piece_turned, next_turned) - piece
-            return piece * 65536 + step, lane_f + (128.0 * block + 1.0)
+        def shifted(block):
+            return lane_gather(jnp.where(turn_near, filtered_at(block), filtered_at(block + 1)), turn_index)
+
+        known = {}
+
+        def filtered_at(block):
+            if block not in known:
+                known[block] = filtered(block)
+            return known[block]
 
         first_block = FIRST_WIN // 2
-        piece = filtered(first_block)
+        piece = shifted(first_block)
         piece_turned = turned(piece)
         before = None
         for block in range(first_block, (FIRST_WIN + WINDOWS) // 2 + 1):
-            following = filtered(block + 1)
+            following = shifted(block + 1)
             following_turned = turned(following)
-            now = block_tables(block, piece, piece_turned, following_turned)
-            for ref, value, old in zip((word_ref, bin_ref), now, before or now):
-                row = (2 * block - FIRST_WIN) * views
-                if before is not None:
-                    ref[row - views : row, :] = jnp.where(lane >= 64, old, value)
-                if 2 * block < FIRST_WIN + WINDOWS:
-                    ref[row : row + views, :] = value
-            before = now
+            step = jnp.where(lane < 127, piece_turned, following_turned) - piece
+            word = piece * 65536 + step
+            row = (2 * block - FIRST_WIN) * views
+            if before is not None:
+                word_ref[row - views : row, :] = jnp.where(lane >= 64, before, word)
+            if 2 * block < FIRST_WIN + WINDOWS:
+                word_ref[row : row + views, :] = word
+            before = word
             piece, piece_turned = following, following_turned
 
     acc_ref[...] = jnp.zeros_like(acc_ref)
@@ -307,19 +351,29 @@
     def spread(ref, row):
         return jnp.broadcast_to(ref[pl.ds(row, 1), :], (8, 128))
 
-    def one_view(views_of, row_set, part, rows_y, totals):
+    member_vec = jnp.full((8, 128), member, jnp.int32)
+    is_zero = member_vec == 0
+    not_zero = member_vec > 0
+
+    def one_slot(slots, row_set, part, rows_y, straight, mirrored):
         def both(ref, rows):
             if len(rows) == 1:
                 return spread(ref, rows[0])
             return jnp.where(top, spread(ref, rows[0]), spread(ref, rows[1]))
 
+        alone = slots[0] == PAIRS
         middle_x = part.astype(jnp.float32) * span + (span // 2 - WIDTH / 2.0 + 0.5)
         first_tile = row_set * TILES + part * count
-        cos_v = both(trig_ref, views_of)
-        base = rows_y * both(trig_ref, [views + view for view in views_of]) + both(center_ref, views_of)
+        cos_v = both(trig_ref, slots)
+        base = rows_y * both(trig_ref, [SLOTS + slot for slot in slots]) + CENTER
         stride = cos_v * 128.0
         middle = (lane_one + middle_x) * cos_v + base
         middle_low = jnp.minimum(middle_x * cos_v, (middle_x + 127.0) * cos_v) + base
+
+        def value_of(words, index, along):
+            word = lane_gather(words, index)
+            return word.astype(jnp.float32) + along * (word << 16).astype(jnp.float32)
+
         for direction in (1, -1):
             place, place_low = middle, middle_low
             tiles = range(count // 2, count) if direction == 1 else range(count // 2 - 1, -1, -1)
@@ -328,56 +382,86 @@
                     place, place_low = place + stride, place_low + stride
                 elif direction == -1:
                     place, place_low = place - stride, place_low - stride
-                near = [where_smem[view, first_tile + tile] for view in views_of]
-                far = [row + 2 * views for row in near]
-                pick = both(bin_ref, near) > place_low
-                words = jnp.where(pick, both(word_ref, near), both(word_ref, far))
+                starts = [where_smem[slot, first_tile + tile] for slot in slots]
+                pick = both(bin_ref, [start >> 6 for start in starts]) > place_low
                 lower = place.astype(jnp.int32)
-                word = lane_gather(words, lower & 127)
-                value = word.astype(jnp.float32)
+                index = lower & 127
                 along = place - lower.astype(jnp.float32)
-                value = value + along * (word << 16).astype(jnp.float32)
-                totals[tile] = value if totals[tile] is None else totals[tile] + value
-
-    def add_up(block, first_view, totals):
-        back = spread(back_ref, first_view)
+
+                def words_of(lines):
+                    near = [start + line for start, line in zip(starts, lines)]
+                    far = [start + (line + 2 * views) for start, line in zip(starts, lines)]
+                    return jnp.where(pick, both(word_ref, near), both(word_ref, far))
+
+                if alone:
+                    words = words_of([views - 1 for slot in slots])
+                    words = jnp.where(is_zero if len(slots) == 1 else top & is_zero, words, 0)
+                else:
+                    words = words_of(slots)
+                    other = words_of([PAIRS + slot for slot in slots])
+                    if slots[-1] == PAIRS - 1:
+                        other = jnp.where(not_zero if len(slots) == 1 else top | not_zero, other, 0)
+                    value = value_of(other, index, along)
+                    mirrored[tile] = value if mirrored[tile] is None else mirrored[tile] + value
+                value = value_of(words, index, along)
+                straight[tile] = value if straight[tile] is None else straight[tile] + value
+
+    def add_up(side, block, line, totals):
+        back = spread(back_ref, line)
         for tile in range(count):
-            acc_ref[block, :, 128 * tile : 128 * tile + 128] += totals[tile] * back
-
-    per_set = views // VIEW_STEP
-
-    def steps(step, carry):
-        block = step // per_set
+            acc_ref[side, block, :, 128 * tile : 128 * tile + 128] += totals[tile] * back
+
+    def all_slots(row_set, part, block, rows_y, slot_sets):
+        for first, group in slot_sets:
+            straight, mirrored = [None] * count, [None] * count
+            for slots in group:
+                one_slot(slots, row_set, part, rows_y, straight, mirrored)
+            if first == PAIRS:
+                add_up(0, block, views - SCALE_SET, straight)
+            else:
+                add_up(0, block, first, straight)
+                add_up(1, block, PAIRS + first, mirrored)
+
+    singles = [
+        (first, [(first + item,) for item in range(SCALE_SET)])
+        for first in range(0, PAIRS, SCALE_SET)
+    ]
+    doubles = [
+        (first, [(first + item, first + item + 4) for item in range(SCALE_SET // 2)])
+        for first in range(0, PAIRS, SCALE_SET)
+    ]
+
+    def steps(block, carry):
         row_set = block // PARTS
-        first_view = (step % per_set) * VIEW_STEP
         rows_y = sub_one + (first_y + 8.0 * row_set.astype(jnp.float32))
-        for set_off in range(0, VIEW_STEP, SCALE_SET):
-            totals = [None] * count
-            for view_off in range(SCALE_SET):
-                view = first_view + (set_off + view_off)
-                one_view((view,), row_set, block % PARTS, rows_y, totals)
-            add_up(block, first_view + set_off, totals)
+        all_slots(row_set, block % PARTS, block, rows_y, singles + [(PAIRS, [(PAIRS,)])])
         return carry
 
-    lax.fori_loop(0, 2 * PARTS * per_set, steps, 0)
-
-    def paired_steps(step, carry):
-        part = step // per_set
-        first_view = (step % per_set) * VIEW_STEP
+    lax.fori_loop(0, 2 * PARTS, steps, 0)
+
+    def paired_steps(part, carry):
         rows_y = jnp.where(top, sub_one, sub_one - 4.0) + (first_y + 16.0)
-        for set_off in range(0, VIEW_STEP, SCALE_SET):
-            totals = [None] * count
-            for view_off in range(SCALE_SET // 2):
-                view = first_view + (set_off + view_off)
-                one_view((view, view + SCALE_SET // 2), 2, part, rows_y, totals)
-            add_up(part + 2 * PARTS, first_view + set_off, totals)
+        all_slots(2, part, 2 * PARTS + part, rows_y, doubles + [(PAIRS, [(PAIRS, PAIRS)])])
         return carry
 
-    lax.fori_loop(0, PARTS * per_set, paired_steps, 0)
+    lax.fori_loop(0, PARTS, paired_steps, 0)
+
+    back_index = 127 - lax.broadcasted_iota(jnp.int32, (8, 128), 1)
+    for row_set in range(ROW_SETS):
+        for tile in range(TILES):
+            block, spot = row_set * PARTS + tile // count, tile % count
+            turn_tile = TILES - 1 - tile
+            other = acc_ref[
+                1,
+                row_set * PARTS + turn_tile // count,
+                :,
+                128 * (turn_tile % count) : 128 * (turn_tile % count) + 128,
+            ]
+            acc_ref[0, block, :, 128 * spot : 128 * spot + 128] += lane_gather(other, back_index)
 
     def rows_of(row_set, low, high):
         return jnp.concatenate(
-            [acc_ref[row_set * PARTS + part, low:high, :] for part in range(PARTS)], axis=1
+            [acc_ref[0, row_set * PARTS + part, low:high, :] for part in range(PARTS)], axis=1
         )
 
     for member in range(GROUP):
@@ -401,12 +485,11 @@
         scratch_shapes=[
             pltpu.VMEM((BLOCKS * views, BLOCK), jnp.float32),
             pltpu.VMEM((rows, 128), jnp.int32),
-            pltpu.VMEM((rows, 128), jnp.float32),
+            pltpu.VMEM((SLOTS, 128), jnp.float32),
             pltpu.VMEM((views, 128), jnp.float32),
-            pltpu.VMEM((views, 128), jnp.float32),
-            pltpu.VMEM((views, 128), jnp.int32),
-            pltpu.VMEM((ROW_SETS * PARTS, 8, WIDTH // PARTS), jnp.float32),
-            pltpu.SMEM((views, 128), jnp.int32),
+            pltpu.VMEM((SLOTS, 128), jnp.int32),
+            pltpu.VMEM((2, ROW_SETS * PARTS, 8, WIDTH // PARTS), jnp.float32),
+            pltpu.SMEM((SLOTS, 128), jnp.int32),
             pltpu.SemaphoreType.DMA(()),
         ],
         compiler_params=pltpu.CompilerParams(vmem_limit_bytes=16 * 2**20),
@@ -493,13 +576,20 @@
     row_index = lax.axis_index("rows")
     member = row_index % GROUP
 
-    mine = lax.dynamic_slice_in_dim(sinogram, member * share, share, 1)
+    second_row = jnp.where(member == 0, view_count // 2, view_count - member)
+    mine = jnp.concatenate(
+        [
+            lax.dynamic_slice_in_dim(sinogram, member, 1, 1),
+            lax.dynamic_slice_in_dim(sinogram, second_row, 1, 1),
+        ],
+        axis=1,
+    )
     shift = jnp.pad(view_shift.astype(jnp.bfloat16), (0, 128 - view_count))
     sent = jnp.concatenate([mine, jnp.broadcast_to(shift, (sheets, share, 128))], axis=2)
     lines = lax.all_to_all(sent, "views", 0, 0, tiled=True)
 
     member_one = member.astype(jnp.int32).reshape(1)
-    ramp, trig = prepare(member_one, view_groups * share, views_total, share, view_count)
+    ramp, trig = prepare(member_one, views_total, view_count)
     first_row = (row_index - member) * ROW_DEV - 2
     first_y = first_row.astype(jnp.float32) - (image_rows - 1) / 2.0
 

time: 50.9 us -> 51.5 us (1.012)
  local copies, waits for them, and re-layouts: 0.79 us -> 2.22 us
  Pallas kernels: 14.9 us -> 13.8 us
    dynamic_slice x1, local copies, waits for them, and re-layouts: 0.28 us -> 2.19 us  [local(): lax.dynamic_slice_in_dim(sinogram, member, 1, 1)]
    pallas_call x1, Pallas kernels: 11.3 us -> 10.2 us  [backproject(): pl.pallas_call(backproject_kernel, out_shape=jax.ShapeDtypeStruct((GROUP,...]
where the time goes in v5:
time: 51.5 us; the launch traced here: 51.2 us
  starting transfers between devices  19.2 us (37%)
  waiting for transfers between devices  14 us (27%)
  Pallas kernels  13.8 us (27%)
  local copies, waits for them, and re-layouts  2.22 us (4%)
  other arithmetic  1.99 us (4%)
    all_to_all x1, starting transfers between devices, local(): lines = lax.all_to_all(sent, 'views', 0, 0, tiled=True)  13.5 us
    all_to_all x1, waiting for transfers between devices, local(): lines = lax.all_to_all(sent, 'views', 0, 0, tiled=True)  11.5 us
    pallas_call x1, Pallas kernels, backproject(): pl.pallas_call(backproject_kernel, out_shape=jax.ShapeDtypeStruct((GROUP,...  10.2 us
    all_to_all x1, starting transfers between devices, local(): lax.all_to_all(partial_rows, 'rows', 0, 0, tiled=True, axis_index_groups=...  5.73 us
    all_to_all x1, waiting for transfers between devices, local(): lax.all_to_all(partial_rows, 'rows', 0, 0, tiled=True, axis_index_groups=...  2.49 us
    dynamic_slice x1, local copies, waits for them, and re-layouts, local(): lax.dynamic_slice_in_dim(sinogram, member, 1, 1)  2.19 us
    pallas_call x1, Pallas kernels, layers(): pl.pallas_call(body, out_shape=jax.ShapeDtypeStruct((1, CHAN, ROW_DEV, WI...  1.93 us
    concatenate x2, other arithmetic, local(): jnp.concatenate([mine, jnp.broadcast_to(shift, (sheets, share, 128))], ax...  1.34 us
  transfers between devices with their start and end apart: 2, of which 2 were waited for; matrix products, arithmetic and copies ran while one was open for 0% of the time, Pallas kernels for 3%

profile of v5, /device:TPU:1, one launch (start us, length us, event | category | flops | bytes accessed | tf_op | source)
XLA Modules:
  0.0 51.2 jit_solution(9283543326843221732)
XLA Ops:
  0.0 0.7 %convert_element_type.9 = bf16[8]{0:T(256)(128)(2,1)S(1)} convert(s32[8]{0:T(128)} %param.7) | non-fusion elementwise | flops 8 | bytes 48 | tf_op jit(solution)/shard_map/convert_element_type | solution.py:587
  0.7 2.2 %constant_dynamic-slice_fusion.1 = (bf16[32,1,2048]{2,1,0:T(2,128)(2,1)S(1)}, bf16[32,1,2048]{2,1,0:T(2,128)(2,1)S(1)}) fusion(bf16[32,8,2048]{2,1,0:T(8,128)(2,1)} %param.6, s32[]{:T(128)S(6)} %select_n.18, s32[]{:T(128)S(6)} %select_n.20), kind=kLoop, calls=%fused_computation.4 | loop fusion | bytes 524296 | tf_op jit(solution)/shard_map/dynamic_slice | solution.py:582
  2.9 1.3 %maximum_maximum_fusion = bf16[32,2,2176]{2,1,0:T(2,128)(2,1)} fusion(bf16[32,1,2048]{2,1,0:T(2,128)(2,1)S(1)} %get-tuple-element.18, bf16[32,1,2048]{2,1,0:T(2,128)(2,1)S(1)} %get-tuple-element.17, bf16[2176]{0:T(1024)(128)(2,1)S(1)} %fusion), kind=kLoop, calls=%fused_computation | loop fusion | flops 835584 | bytes 545024 | tf_op jit(solution)/shard_map/concatenate | solution.py:588
  4.2 13.5 %all-to-all-start = ((bf16[32,2,2176]{2,1,0:T(2,128)(2,1)}), bf16[32,2,2176]{2,1,0:T(2,128)(2,1)S(1)}, u32[]{:S(2)}, u32[]{:S(2)}) async-start(bf16[32,2,2176]{2,1,0:T(2,128)(2,1)} %maximum_maximum_fusion), calls=%async_computation | async-start | bytes 557056 | tf_op jit(solution)/shard_map/all_to_all | solution.py:589
  17.7 0.0 copy-start
  17.7 0.0 copy-start.1
  17.7 0.0 copy-start.2
  17.7 0.0 copy-start.3
  17.7 0.6 %prepare.1 = (bf16[512,2048]{1,0:T(8,128)(2,1)S(1)}, f32[80,128]{1,0:T(8,128)S(1)}) custom-call(s32[1]{0:T(128)} %bitcast.2.refs_0_.member_ref), custom_call_target="tpu_custom_call" | custom-call | flops 20000000 | bytes 4000000 | tf_op jit(solution)/shard_map/prepare/pallas_call | solution.py:158
  18.3 11.5 %all-to-all-done.x_ref = bf16[32,2,2176]{2,1,0:T(2,128)(2,1)S(1)} async-done(((bf16[32,2,2176]{2,1,0:T(2,128)(2,1)}), bf16[32,2,2176]{2,1,0:T(2,128)(2,1)S(1)}, u32[]{:S(2)}, u32[]{:S(2)}) %all-to-all-start) | async-done | bytes 278560 | tf_op jit(solution)/shard_map/all_to_all | solution.py:589
  29.8 10.2 %backproject.1.after_ref = bf16[4,8,2048]{2,1,0:T(8,128)(2,1)} custom-call(f32[1]{0:T(128)} %bitcast.1.first_ref, s32[1]{0:T(128)} %bitcast.2.refs_0_.member_ref, bf16[32,2,2176]{2,1,0:T(2,128)(2,1)S(1)} %all-to-all-done.x_ref, f32[80,128]{1,0:T(8,128)S(1)} %get-tuple-element.11.trig_ref, bf16[512,2048]{1,0:T(8,128)(2,1)S(1)} %get-tuple-element.12.ramp_ref), custom_call_target="tpu_custom_call" | custom-call | flops 1000000000 | bytes 6000000 | tf_op jit(solution)/shard_map/backproject/pallas_call | solution.py:480
  40.0 5.7 %all-to-all-start.1 = ((bf16[4,8,2048]{2,1,0:T(8,128)(2,1)}), bf16[4,8,2048]{2,1,0:T(8,128)(2,1)S(1)}, u32[]{:S(2)}, u32[]{:S(2)}) async-start(bf16[4,8,2048]{2,1,0:T(8,128)(2,1)} %backproject.1.after_ref), calls=%async_computation.1 | async-start | bytes 262144 | tf_op jit(solution)/shard_map/all_to_all | solution.py:598
  45.7 0.0 copy-done
  45.7 0.0 copy-done.1
  45.7 0.0 copy-done.2
  45.7 0.0 copy-done.3
  45.7 1.1 %weights.1 = (bf16[192,72]{1,0:T(8,128)(2,1)S(1)}, f32[192,1]{1,0:T(8,128)S(1)}, bf16[3,128,192]{2,1,0:T(8,128)(2,1)S(1)}, f32[128,1]{1,0:T(8,128)S(1)}) custom-call(bf16[4,8,2048]{2,1,0:T(8,128)(2,1)} %backproject.1.after_ref, f32[9,32]{1,0:T(8,128)S(1)} %copy-done.1, f32[1,32]{1,0:T(1,128)S(1)} %bitcast.5, bf16[32,288]{1,0:T(8,128)(2,1)S(1)} %copy-done, ...), custom_call_target="tpu_custom_call" | custom-call | flops 20000000 | bytes 1000000 | tf_op jit(solution)/shard_map/weights/pallas_call | solution.py:175
  46.8 2.5 %all-to-all-done.1.refs_1_ = bf16[4,8,2048]{2,1,0:T(8,128)(2,1)S(1)} async-done(((bf16[4,8,2048]{2,1,0:T(8,128)(2,1)}), bf16[4,8,2048]{2,1,0:T(8,128)(2,1)S(1)}, u32[]{:S(2)}, u32[]{:S(2)}) %all-to-all-start.1) | async-done | bytes 131104 | tf_op jit(solution)/shard_map/all_to_all | solution.py:598
  49.3 1.9 %layers.1 = bf16[1,32,4,2048]{3,2,1,0:T(4,128)(2,1)} custom-call(s32[1]{0:T(128)} %bitcast.refs_0_, bf16[4,8,2048]{2,1,0:T(8,128)(2,1)S(1)} %all-to-all-done.1.refs_1_, bf16[192,72]{1,0:T(8,128)(2,1)S(1)} %get-tuple-element.13.refs_2_, f32[192,1]{1,0:T(8,128)S(1)} %get-tuple-element.14.refs_3_, bf16[3,128,192]{2,1,0:T(8,128)(2,1)S(1)} %get-tuple-element.15.refs_4_, ...), custom_call_target="tpu_custom_call" | custom-call | flops 500000000 | bytes 1000000 | tf_op jit(solution)/shard_map/layers/pallas_call | solution.py:554
  (1 shorter events, 0.0 us)
Async XLA Ops:
  4.2 25.6 %all-to-all-start = ((bf16[32,2,2176]{2,1,0:T(2,128)(2,1)}), bf16[32,2,2176]{2,1,0:T(2,128)(2,1)S(1)}, u32[]{:S(2)}, u32[]{:S(2)}) async-start(bf16[32,2,2176]{2,1,0:T(2,128)(2,1)} %maximum_maximum_fusion), calls=%async_computation | async-start | bytes 557056 | tf_op jit(solution)/shard_map/all_to_all | solution.py:589
  17.7 28.1 %copy-start = (bf16[32,288]{1,0:T(8,128)(2,1)S(1)}, bf16[32,288]{1,0:T(8,128)(2,1)}, u32[]{:S(2)}) copy-start(bf16[32,288]{1,0:T(8,128)(2,1)} %conv_two_ref.1) | copy-start | bytes 55300
  17.7 28.1 %copy-start.1 = (f32[9,32]{1,0:T(8,128)S(1)}, f32[9,32]{1,0:T(8,128)}, u32[]{:S(2)}) copy-start(f32[9,32]{1,0:T(8,128)} %conv_one_ref.1) | copy-start | bytes 3460
  17.7 28.1 %copy-start.2 = (f32[32]{0:T(128)S(1)}, f32[32]{0:T(128)}, u32[]{:S(2)}) copy-start(f32[32]{0:T(128)} %param.9) | copy-start | bytes 388
  17.7 28.0 %copy-start.3 = (f32[32]{0:T(128)S(1)}, f32[32]{0:T(128)}, u32[]{:S(2)}) copy-start(f32[32]{0:T(128)} %param.11) | copy-start | bytes 388
  40.0 9.3 %all-to-all-start.1 = ((bf16[4,8,2048]{2,1,0:T(8,128)(2,1)}), bf16[4,8,2048]{2,1,0:T(8,128)(2,1)S(1)}, u32[]{:S(2)}, u32[]{:S(2)}) async-start(bf16[4,8,2048]{2,1,0:T(8,128)(2,1)} %backproject.1.after_ref), calls=%async_computation.1 | async-start | bytes 262144 | tf_op jit(solution)/shard_map/all_to_all | solution.py:598

commit v6 on v5

--- a/solution.py
+++ b/solution.py
@@ -19,6 +19,8 @@
 WINDOWS = 36
 HALF_TURN = 64
 PAIRS = 32
+PACK_STEPS = 2
+PACK_LIMIT = 66_500_000
 SLOTS = 40
 CENTER = (BINS - 1) / 2.0 + MARGIN - HALF_TURN
 TILES = WIDTH // 128
@@ -66,6 +68,45 @@
     return jnp.where(
         which == 0, member, jnp.where(member == 0, view_count // 2, view_count - member)
     )
+
+
+def pack_kernel(member_ref, shift_ref, x_ref, out_ref):
+    sheets, views, width = x_ref.shape
+    share = out_ref.shape[1]
+    row = lax.broadcasted_iota(jnp.int32, (sheets * share, sheets * views), 0)
+    col = lax.broadcasted_iota(jnp.int32, (sheets * share, sheets * views), 1)
+    member = jnp.full(row.shape, member_ref[0], jnp.int32)
+    wanted = (row >> 1) * views + residue_of(row & 1, member, views)
+    order = jnp.where(col == wanted, 1.0, 0.0).astype(jnp.bfloat16)
+    lines = x_ref[...].reshape(sheets * views, width)
+    picked = jnp.dot(order, lines, preferred_element_type=jnp.float32).astype(jnp.bfloat16)
+    start = pl.multiple_of(pl.program_id(0) * width, width)
+    out_ref[:, :, pl.ds(start, width)] = picked.reshape(sheets, share, width)
+
+    @pl.when(pl.program_id(0) == 0)
+    def shifts_of_views():
+        lane = lax.broadcasted_iota(jnp.int32, (1, share, 128), 2)
+        shifts = jnp.zeros((1, share, 128), jnp.float32)
+        for view in range(views):
+            shifts = jnp.where(lane == view, shift_ref[view].astype(jnp.float32), shifts)
+        shifts = jnp.broadcast_to(shifts.astype(jnp.bfloat16), (sheets, share, 128))
+        out_ref[:, :, BINS : BINS + 128] = shifts
+
+
+def pack(member, view_shift, sinogram, share):
+    sheets, views, bins = sinogram.shape
+    smem = pl.BlockSpec(memory_space=pltpu.SMEM)
+    width = bins // PACK_STEPS
+    return pl.pallas_call(
+        pack_kernel,
+        grid=(PACK_STEPS,),
+        out_shape=jax.ShapeDtypeStruct((sheets, share, bins + 128), jnp.bfloat16),
+        in_specs=[smem, smem, pl.BlockSpec((sheets, views, width), lambda step: (0, 0, step))],
+        out_specs=pl.BlockSpec((sheets, share, bins + 128), lambda step: (0, 0, 0)),
+        compiler_params=pltpu.CompilerParams(vmem_limit_bytes=PACK_LIMIT),
+        cost_estimate=pl.CostEstimate(flops=70_000_000, bytes_accessed=1_500_000, transcendentals=0),
+        name="pack",
+    )(member, view_shift, sinogram)
 
 
 def prepare_kernel(
@@ -576,19 +617,10 @@
     row_index = lax.axis_index("rows")
     member = row_index % GROUP
 
-    second_row = jnp.where(member == 0, view_count // 2, view_count - member)
-    mine = jnp.concatenate(
-        [
-            lax.dynamic_slice_in_dim(sinogram, member, 1, 1),
-            lax.dynamic_slice_in_dim(sinogram, second_row, 1, 1),
-        ],
-        axis=1,
-    )
-    shift = jnp.pad(view_shift.astype(jnp.bfloat16), (0, 128 - view_count))
-    sent = jnp.concatenate([mine, jnp.broadcast_to(shift, (sheets, share, 128))], axis=2)
+    member_one = member.astype(jnp.int32).reshape(1)
+    sent = pack(member_one, view_shift, sinogram, share)
     lines = lax.all_to_all(sent, "views", 0, 0, tiled=True)
 
-    member_one = member.astype(jnp.int32).reshape(1)
     ramp, trig = prepare(member_one, views_total, view_count)
     first_row = (row_index - member) * ROW_DEV - 2
     first_y = first_row.astype(jnp.float32) - (image_rows - 1) / 2.0

time: 51.5 us -> 49.5 us (0.961)
  Pallas kernels: 13.8 us -> 16 us
  local copies, waits for them, and re-layouts: 2.22 us -> 0.03 us
  other arithmetic: 1.99 us -> 0 us
    pallas_call x0 -> x1, Pallas kernels: none -> 2.23 us  [pack(): pl.pallas_call(pack_kernel, grid=(PACK_STEPS,), out_shape=jax.ShapeDtypeS...]
    dynamic_slice x1 -> x0, local copies, waits for them, and re-layouts: 2.19 us -> none  [local(): lax.dynamic_slice_in_dim(sinogram, member, 1, 1)]
    concatenate x2 -> x0, other arithmetic: 1.34 us -> none  [local(): jnp.concatenate([mine, jnp.broadcast_to(shift, (sheets, share, 128))], ax...]
    convert_element_type x1 -> x0, other arithmetic: 0.66 us -> none  [local(): shift = jnp.pad(view_shift.astype(jnp.bfloat16), (0, 128 - view_count))]
where the time goes in v6:
time: 49.5 us; the launch traced here: 49.3 us
  starting transfers between devices  19.2 us (39%)
  Pallas kernels  16 us (32%)
  waiting for transfers between devices  14 us (28%)
    all_to_all x1, starting transfers between devices, local(): lines = lax.all_to_all(sent, 'views', 0, 0, tiled=True)  13.5 us
    all_to_all x1, waiting for transfers between devices, local(): lines = lax.all_to_all(sent, 'views', 0, 0, tiled=True)  11.5 us
    pallas_call x1, Pallas kernels, backproject(): pl.pallas_call(backproject_kernel, out_shape=jax.ShapeDtypeStruct((GROUP,...  10.2 us
    all_to_all x1, starting transfers between devices, local(): lax.all_to_all(partial_rows, 'rows', 0, 0, tiled=True, axis_index_groups=...  5.73 us
    all_to_all x1, waiting for transfers between devices, local(): lax.all_to_all(partial_rows, 'rows', 0, 0, tiled=True, axis_index_groups=...  2.49 us
    pallas_call x1, Pallas kernels, pack(): pl.pallas_call(pack_kernel, grid=(PACK_STEPS,), out_shape=jax.ShapeDtypeS...  2.23 us
    pallas_call x1, Pallas kernels, layers(): pl.pallas_call(body, out_shape=jax.ShapeDtypeStruct((1, CHAN, ROW_DEV, WI...  1.93 us
    pallas_call x1, Pallas kernels, spread_weights(): pl.pallas_call(weights_kernel, out_shape=(jax.ShapeDtypeStruct((rows_one,...  1.05 us
  transfers between devices with their start and end apart: 2, of which 2 were waited for; matrix products, arithmetic and copies ran while one was open for 0% of the time, Pallas kernels for 3%

profile of v6, /device:TPU:1, one launch (start us, length us, event | category | flops | bytes accessed | tf_op | source)
XLA Modules:
  0.0 49.3 jit_solution(8915498229887269002)
XLA Ops:
  0.0 2.2 %pack.1 = bf16[32,2,2176]{2,1,0:T(2,128)(2,1)} custom-call(s32[1]{0:T(128)} %bitcast.2.member_ref.refs_0_, s32[8]{0:T(128)} %shift_ref.1, bf16[32,8,2048]{2,1,0:T(8,128)(2,1)} %x_ref.1), custom_call_target="tpu_custom_call" | custom-call | flops 70000000 | bytes 1500000 | tf_op jit(solution)/shard_map/pack/pallas_call | solution.py:100
  2.2 13.5 %all-to-all-start = ((bf16[32,2,2176]{2,1,0:T(2,128)(2,1)}), bf16[32,2,2176]{2,1,0:T(2,128)(2,1)S(1)}, u32[]{:S(2)}, u32[]{:S(2)}) async-start(bf16[32,2,2176]{2,1,0:T(2,128)(2,1)} %pack.1), calls=%async_computation | async-start | bytes 557056 | tf_op jit(solution)/shard_map/all_to_all | solution.py:622
  15.7 0.0 copy-start
  15.7 0.0 copy-start.1
  15.7 0.0 copy-start.2
  15.7 0.0 copy-start.3
  15.7 0.6 %prepare.1 = (bf16[512,2048]{1,0:T(8,128)(2,1)S(1)}, f32[80,128]{1,0:T(8,128)S(1)}) custom-call(s32[1]{0:T(128)} %bitcast.2.member_ref.refs_0_), custom_call_target="tpu_custom_call" | custom-call | flops 20000000 | bytes 4000000 | tf_op jit(solution)/shard_map/prepare/pallas_call | solution.py:199
  16.3 11.5 %all-to-all-done.x_ref = bf16[32,2,2176]{2,1,0:T(2,128)(2,1)S(1)} async-done(((bf16[32,2,2176]{2,1,0:T(2,128)(2,1)}), bf16[32,2,2176]{2,1,0:T(2,128)(2,1)S(1)}, u32[]{:S(2)}, u32[]{:S(2)}) %all-to-all-start) | async-done | bytes 278560 | tf_op jit(solution)/shard_map/all_to_all | solution.py:622
  27.8 10.2 %backproject.1.after_ref = bf16[4,8,2048]{2,1,0:T(8,128)(2,1)} custom-call(f32[1]{0:T(128)} %bitcast.1.first_ref, s32[1]{0:T(128)} %bitcast.2.member_ref.refs_0_, bf16[32,2,2176]{2,1,0:T(2,128)(2,1)S(1)} %all-to-all-done.x_ref, f32[80,128]{1,0:T(8,128)S(1)} %get-tuple-element.11.trig_ref, bf16[512,2048]{1,0:T(8,128)(2,1)S(1)} %get-tuple-element.12.ramp_ref), custom_call_target="tpu_custom_call" | custom-call | flops 1000000000 | bytes 6000000 | tf_op jit(solution)/shard_map/backproject/pallas_call | solution.py:521
  38.0 5.7 %all-to-all-start.1 = ((bf16[4,8,2048]{2,1,0:T(8,128)(2,1)}), bf16[4,8,2048]{2,1,0:T(8,128)(2,1)S(1)}, u32[]{:S(2)}, u32[]{:S(2)}) async-start(bf16[4,8,2048]{2,1,0:T(8,128)(2,1)} %backproject.1.after_ref), calls=%async_computation.1 | async-start | bytes 262144 | tf_op jit(solution)/shard_map/all_to_all | solution.py:630
  43.8 0.0 copy-done
  43.8 0.0 copy-done.1
  43.8 0.0 copy-done.2
  43.8 0.0 copy-done.3
  43.8 1.0 %weights.1 = (bf16[192,72]{1,0:T(8,128)(2,1)S(1)}, f32[192,1]{1,0:T(8,128)S(1)}, bf16[3,128,192]{2,1,0:T(8,128)(2,1)S(1)}, f32[128,1]{1,0:T(8,128)S(1)}) custom-call(bf16[4,8,2048]{2,1,0:T(8,128)(2,1)} %backproject.1.after_ref, f32[9,32]{1,0:T(8,128)S(1)} %copy-done.1, f32[1,32]{1,0:T(1,128)S(1)} %bitcast.5, bf16[32,288]{1,0:T(8,128)(2,1)S(1)} %copy-done, ...), custom_call_target="tpu_custom_call" | custom-call | flops 20000000 | bytes 1000000 | tf_op jit(solution)/shard_map/weights/pallas_call | solution.py:216
  44.8 2.5 %all-to-all-done.1.refs_1_ = bf16[4,8,2048]{2,1,0:T(8,128)(2,1)S(1)} async-done(((bf16[4,8,2048]{2,1,0:T(8,128)(2,1)}), bf16[4,8,2048]{2,1,0:T(8,128)(2,1)S(1)}, u32[]{:S(2)}, u32[]{:S(2)}) %all-to-all-start.1) | async-done | bytes 131104 | tf_op jit(solution)/shard_map/all_to_all | solution.py:630
  47.3 1.9 %layers.1 = bf16[1,32,4,2048]{3,2,1,0:T(4,128)(2,1)} custom-call(s32[1]{0:T(128)} %bitcast.refs_0_, bf16[4,8,2048]{2,1,0:T(8,128)(2,1)S(1)} %all-to-all-done.1.refs_1_, bf16[192,72]{1,0:T(8,128)(2,1)S(1)} %get-tuple-element.13.refs_2_, f32[192,1]{1,0:T(8,128)S(1)} %get-tuple-element.14.refs_3_, bf16[3,128,192]{2,1,0:T(8,128)(2,1)S(1)} %get-tuple-element.15.refs_4_, ...), custom_call_target="tpu_custom_call" | custom-call | flops 500000000 | bytes 1000000 | tf_op jit(solution)/shard_map/layers/pallas_call | solution.py:595
Async XLA Ops:
  2.2 25.6 %all-to-all-start = ((bf16[32,2,2176]{2,1,0:T(2,128)(2,1)}), bf16[32,2,2176]{2,1,0:T(2,128)(2,1)S(1)}, u32[]{:S(2)}, u32[]{:S(2)}) async-start(bf16[32,2,2176]{2,1,0:T(2,128)(2,1)} %pack.1), calls=%async_computation | async-start | bytes 557056 | tf_op jit(solution)/shard_map/all_to_all | solution.py:622
  15.7 28.1 %copy-start = (bf16[32,288]{1,0:T(8,128)(2,1)S(1)}, bf16[32,288]{1,0:T(8,128)(2,1)}, u32[]{:S(2)}) copy-start(bf16[32,288]{1,0:T(8,128)(2,1)} %conv_two_ref.1) | copy-start | bytes 55300
  15.7 28.1 %copy-start.1 = (f32[9,32]{1,0:T(8,128)S(1)}, f32[9,32]{1,0:T(8,128)}, u32[]{:S(2)}) copy-start(f32[9,32]{1,0:T(8,128)} %conv_one_ref.1) | copy-start | bytes 3460
  15.7 28.1 %copy-start.2 = (f32[32]{0:T(128)S(1)}, f32[32]{0:T(128)}, u32[]{:S(2)}) copy-start(f32[32]{0:T(128)} %param.9) | copy-start | bytes 388
  15.7 28.0 %copy-start.3 = (f32[32]{0:T(128)S(1)}, f32[32]{0:T(128)}, u32[]{:S(2)}) copy-start(f32[32]{0:T(128)} %param.11) | copy-start | bytes 388
  38.0 9.3 %all-to-all-start.1 = ((bf16[4,8,2048]{2,1,0:T(8,128)(2,1)}), bf16[4,8,2048]{2,1,0:T(8,128)(2,1)S(1)}, u32[]{:S(2)}, u32[]{:S(2)}) async-start(bf16[4,8,2048]{2,1,0:T(8,128)(2,1)} %backproject.1.after_ref), calls=%async_computation.1 | async-start | bytes 262144 | tf_op jit(solution)/shard_map/all_to_all | solution.py:630

commit v7 on v6

--- a/solution.py
+++ b/solution.py
@@ -70,12 +70,16 @@
     )
 
 
-def pack_kernel(member_ref, shift_ref, x_ref, out_ref):
+def own_member():
+    return lax.rem(lax.axis_index("rows"), GROUP)
+
+
+def pack_kernel(shift_ref, x_ref, out_ref):
     sheets, views, width = x_ref.shape
     share = out_ref.shape[1]
     row = lax.broadcasted_iota(jnp.int32, (sheets * share, sheets * views), 0)
     col = lax.broadcasted_iota(jnp.int32, (sheets * share, sheets * views), 1)
-    member = jnp.full(row.shape, member_ref[0], jnp.int32)
+    member = jnp.full(row.shape, own_member(), jnp.int32)
     wanted = (row >> 1) * views + residue_of(row & 1, member, views)
     order = jnp.where(col == wanted, 1.0, 0.0).astype(jnp.bfloat16)
     lines = x_ref[...].reshape(sheets * views, width)
@@ -93,7 +97,7 @@
         out_ref[:, :, BINS : BINS + 128] = shifts
 
 
-def pack(member, view_shift, sinogram, share):
+def pack(view_shift, sinogram, share):
     sheets, views, bins = sinogram.shape
     smem = pl.BlockSpec(memory_space=pltpu.SMEM)
     width = bins // PACK_STEPS
@@ -101,18 +105,17 @@
         pack_kernel,
         grid=(PACK_STEPS,),
         out_shape=jax.ShapeDtypeStruct((sheets, share, bins + 128), jnp.bfloat16),
-        in_specs=[smem, smem, pl.BlockSpec((sheets, views, width), lambda step: (0, 0, step))],
+        in_specs=[smem, pl.BlockSpec((sheets, views, width), lambda step: (0, 0, step))],
         out_specs=pl.BlockSpec((sheets, share, bins + 128), lambda step: (0, 0, 0)),
         compiler_params=pltpu.CompilerParams(vmem_limit_bytes=PACK_LIMIT),
         cost_estimate=pl.CostEstimate(flops=70_000_000, bytes_accessed=1_500_000, transcendentals=0),
         name="pack",
-    )(member, view_shift, sinogram)
+    )(view_shift, sinogram)
 
 
 def prepare_kernel(
     views_total,
     view_count,
-    member_ref,
     table_ref,
     trig_ref,
 ):
@@ -136,7 +139,7 @@
             table_ref[BLOCK + start : BLOCK + start + 16, :] = low[:, cols]
 
     slot = lax.broadcasted_iota(jnp.int32, (SLOTS, 128), 0)
-    member = jnp.full((SLOTS, 128), member_ref[0], jnp.int32)
+    member = jnp.full((SLOTS, 128), own_member(), jnp.int32)
     group, which = source_of(slot & (PAIRS - 1), member)
     view = group * view_count + residue_of(which, member, view_count)
     view = jnp.where(slot < PAIRS, view, views_total // 2)
@@ -190,7 +193,7 @@
         second_ref[tap] = block.astype(jnp.bfloat16)
 
 
-def prepare(member, views_total, view_count):
+def prepare(views_total, view_count):
     vmem = pl.BlockSpec(memory_space=pltpu.VMEM)
 
     def body(*refs):
@@ -202,12 +205,11 @@
             jax.ShapeDtypeStruct((2 * BLOCK, BLOCKS * BLOCK), jnp.bfloat16),
             jax.ShapeDtypeStruct((2 * SLOTS, 128), jnp.float32),
         ),
-        in_specs=[pl.BlockSpec(memory_space=pltpu.SMEM)],
         out_specs=(vmem,) * 2,
         compiler_params=pltpu.CompilerParams(vmem_limit_bytes=8 * 2**20),
         cost_estimate=pl.CostEstimate(flops=20_000_000, bytes_accessed=4_000_000, transcendentals=0),
         name="prepare",
-    )(member)
+    )()
 
 
 def spread_weights(after, conv_one, bias_one, conv_two, bias_two):
@@ -247,8 +249,7 @@
 
 
 def backproject_kernel(
-    first_ref,
-    member_ref,
+    image_rows,
     x_ref,
     trig_ref,
     ramp_ref,
@@ -264,8 +265,9 @@
 ):
     share = x_ref.shape[1]
     views = x_ref.shape[0] * share
-    first_y = first_ref[0]
-    member = member_ref[0]
+    member = own_member()
+    first_row = (lax.axis_index("rows") - member) * ROW_DEV - 2
+    first_y = first_row.astype(jnp.float32) - (image_rows - 1) / 2.0
     lane = lax.broadcasted_iota(jnp.int32, (views, 128), 1)
 
     slot_lane = lax.broadcasted_iota(jnp.int32, (SLOTS, 128), 1)
@@ -283,7 +285,7 @@
     to_smem = pltpu.make_async_copy(where_ref, where_smem, sem)
     to_smem.start()
 
-    @pl.when(member_ref[0] >= 0)
+    @pl.when(member >= 0)
     def filter_and_tables():
         row = lax.broadcasted_iota(jnp.int32, (views, views), 0)
         col = lax.broadcasted_iota(jnp.int32, (views, views), 1)
@@ -342,43 +344,44 @@
         largest = largest.reshape(views, 128)
         back_ref[...] = largest * (1.0 / (16383.0 * 65536.0))
         scale = 16383.0 / largest
-        zero = jnp.zeros((views, 128), jnp.int32)
-
-        def filtered(block):
-            place = block - margin
-            if place < 0 or place >= inner:
-                return zero
-            return jnp.floor(raw(place) * scale + 0.5).astype(jnp.int32)
-
-        def turned(piece):
-            return pltpu.roll(piece, 127, 1)
-
-        def shifted(block):
-            return lane_gather(jnp.where(turn_near, filtered_at(block), filtered_at(block + 1)), turn_index)
-
-        known = {}
-
-        def filtered_at(block):
-            if block not in known:
-                known[block] = filtered(block)
-            return known[block]
-
-        first_block = FIRST_WIN // 2
-        piece = shifted(first_block)
-        piece_turned = turned(piece)
-        before = None
-        for block in range(first_block, (FIRST_WIN + WINDOWS) // 2 + 1):
-            following = shifted(block + 1)
-            following_turned = turned(following)
-            step = jnp.where(lane < 127, piece_turned, following_turned) - piece
-            word = piece * 65536 + step
-            row = (2 * block - FIRST_WIN) * views
-            if before is not None:
-                word_ref[row - views : row, :] = jnp.where(lane >= 64, before, word)
-            if 2 * block < FIRST_WIN + WINDOWS:
-                word_ref[row : row + views, :] = word
-            before = word
-            piece, piece_turned = following, following_turned
+        zero = jnp.zeros((8, 128), jnp.int32)
+        lane_row = lax.broadcasted_iota(jnp.int32, (8, 128), 1)
+
+        def group_tables(first):
+            here = slice(first, first + 8)
+            scale_here, near_here, index_here = scale[here], turn_near[here], turn_index[here]
+
+            def filtered(block):
+                place = block - margin
+                if place < 0 or place >= inner:
+                    return zero
+                line = views * (place // 2) + first
+                half = 128 * (place % 2)
+                piece = filt_ref[line : line + 8, half : half + 128]
+                piece = piece.astype(jnp.bfloat16).astype(jnp.float32)
+                return jnp.floor(piece * scale_here + 0.5).astype(jnp.int32)
+
+            first_block = FIRST_WIN // 2
+            last_block = (FIRST_WIN + WINDOWS) // 2 + 1
+            bins = [filtered(block) for block in range(first_block, last_block + 2)]
+            pieces = [
+                lane_gather(jnp.where(near_here, low, high), index_here)
+                for low, high in zip(bins[:-1], bins[1:])
+            ]
+            rolled = [pltpu.roll(piece, 127, 1) for piece in pieces]
+            before = None
+            for item in range(last_block - first_block):
+                after = jnp.where(lane_row < 127, rolled[item], rolled[item + 1])
+                word = pieces[item] * 65536 + (after - pieces[item])
+                row = 2 * item * views + first
+                if before is not None:
+                    word_ref[row - views : row - views + 8, :] = jnp.where(lane_row >= 64, before, word)
+                if 2 * item < WINDOWS:
+                    word_ref[row : row + 8, :] = word
+                before = word
+
+        for first in range(0, views, 8):
+            group_tables(first)
 
     acc_ref[...] = jnp.zeros_like(acc_ref)
     to_smem.wait()
@@ -514,14 +517,17 @@
         out_ref[member] = lower.astype(jnp.bfloat16)
 
 
-def backproject(first_y, member, lines, trig, ramp):
+def backproject(lines, trig, ramp, image_rows):
     views = lines.shape[0] * lines.shape[1]
     rows = WINDOWS * views
     vmem = pl.BlockSpec(memory_space=pltpu.VMEM)
+    def body(*refs):
+        backproject_kernel(image_rows, *refs)
+
     return pl.pallas_call(
-        backproject_kernel,
+        body,
         out_shape=jax.ShapeDtypeStruct((GROUP, 8, WIDTH), jnp.bfloat16),
-        in_specs=[pl.BlockSpec(memory_space=pltpu.SMEM)] * 2 + [vmem] * 3,
+        in_specs=[vmem] * 3,
         out_specs=vmem,
         scratch_shapes=[
             pltpu.VMEM((BLOCKS * views, BLOCK), jnp.float32),
@@ -536,13 +542,12 @@
         compiler_params=pltpu.CompilerParams(vmem_limit_bytes=16 * 2**20),
         cost_estimate=pl.CostEstimate(flops=1_000_000_000, bytes_accessed=6_000_000, transcendentals=0),
         name="backproject",
-    )(first_y, member, lines, trig, ramp)
+    )(lines, trig, ramp)
 
 
 def layers_kernel(
     scale,
     image_rows,
-    row_ref,
     parts_ref,
     first_ref,
     bias_one_ref,
@@ -552,7 +557,7 @@
     image_ref,
     stack_ref,
 ):
-    row_base = row_ref[0]
+    row_base = lax.axis_index("rows") * ROW_DEV
     image = parts_ref[0].astype(jnp.float32)
     for member in range(1, GROUP):
         image = image + parts_ref[member].astype(jnp.float32)
@@ -586,7 +591,7 @@
     out_ref[...] = mixed.reshape(CHAN, ROW_DEV, WIDTH).astype(jnp.bfloat16)[None]
 
 
-def layers(row_base, parts, first, bias_one, second, bias_two, scale, image_rows):
+def layers(parts, first, bias_one, second, bias_two, scale, image_rows):
     vmem = pl.BlockSpec(memory_space=pltpu.VMEM)
 
     def body(*refs):
@@ -595,7 +600,7 @@
     return pl.pallas_call(
         body,
         out_shape=jax.ShapeDtypeStruct((1, CHAN, ROW_DEV, WIDTH), jnp.bfloat16),
-        in_specs=[pl.BlockSpec(memory_space=pltpu.SMEM)] + [vmem] * 5,
+        in_specs=[vmem] * 5,
         out_specs=vmem,
         scratch_shapes=[
             pltpu.VMEM((72, WIDTH), jnp.bfloat16),
@@ -604,7 +609,7 @@
         compiler_params=pltpu.CompilerParams(vmem_limit_bytes=16 * 2**20),
         cost_estimate=pl.CostEstimate(flops=500_000_000, bytes_accessed=1_000_000, transcendentals=0),
         name="layers",
-    )(row_base, parts, first, bias_one, second, bias_two)
+    )(parts, first, bias_one, second, bias_two)
 
 
 def local(sinogram, view_shift, conv_one, bias_one, conv_two, bias_two):
@@ -614,27 +619,18 @@
     views_total = view_count * view_groups
     image_rows = ROW_DEV * row_groups
     share = view_count // GROUP
-    row_index = lax.axis_index("rows")
-    member = row_index % GROUP
-
-    member_one = member.astype(jnp.int32).reshape(1)
-    sent = pack(member_one, view_shift, sinogram, share)
+    sent = pack(view_shift, sinogram, share)
     lines = lax.all_to_all(sent, "views", 0, 0, tiled=True)
 
-    ramp, trig = prepare(member_one, views_total, view_count)
-    first_row = (row_index - member) * ROW_DEV - 2
-    first_y = first_row.astype(jnp.float32) - (image_rows - 1) / 2.0
-
-    partial_rows = backproject(first_y.reshape(1), member_one, lines, trig, ramp)
+    ramp, trig = prepare(views_total, view_count)
+    partial_rows = backproject(lines, trig, ramp, image_rows)
     groups = [[GROUP * base + item for item in range(GROUP)] for base in range(row_groups // GROUP)]
     parts = lax.all_to_all(partial_rows, "rows", 0, 0, tiled=True, axis_index_groups=groups)
 
     first, wide_one, second, wide_two = spread_weights(
         partial_rows, conv_one, bias_one[None], conv_two, bias_two[None]
     )
-    row_base = (row_index * ROW_DEV).astype(jnp.int32).reshape(1)
     return layers(
-        row_base,
         parts,
         first,
         wide_one,

time: 49.5 us -> 49.4 us (level)
  no operation moved by 1% of the time
where the time goes in v7:
time: 49.4 us; the launch traced here: 49.1 us
  starting transfers between devices  19.2 us (39%)
  Pallas kernels  15.9 us (32%)
  waiting for transfers between devices  13.9 us (28%)
    all_to_all x1, starting transfers between devices, local(): lines = lax.all_to_all(sent, 'views', 0, 0, tiled=True)  13.5 us
    all_to_all x1, waiting for transfers between devices, local(): lines = lax.all_to_all(sent, 'views', 0, 0, tiled=True)  11.5 us
    pallas_call x1, Pallas kernels, backproject(): pl.pallas_call(body, out_shape=jax.ShapeDtypeStruct((GROUP, 8, WIDTH), jn...  10.1 us
    all_to_all x1, starting transfers between devices, local(): lax.all_to_all(partial_rows, 'rows', 0, 0, tiled=True, axis_index_groups=...  5.72 us
    all_to_all x1, waiting for transfers between devices, local(): lax.all_to_all(partial_rows, 'rows', 0, 0, tiled=True, axis_index_groups=...  2.48 us
    pallas_call x1, Pallas kernels, pack(): pl.pallas_call(pack_kernel, grid=(PACK_STEPS,), out_shape=jax.ShapeDtypeS...  2.23 us
    pallas_call x1, Pallas kernels, layers(): pl.pallas_call(body, out_shape=jax.ShapeDtypeStruct((1, CHAN, ROW_DEV, WI...  1.92 us
    pallas_call x1, Pallas kernels, spread_weights(): pl.pallas_call(weights_kernel, out_shape=(jax.ShapeDtypeStruct((rows_one,...  1.06 us
  transfers between devices with their start and end apart: 2, of which 2 were waited for; matrix products, arithmetic and copies ran while one was open for 0% of the time, Pallas kernels for 3%

profile of v7, /device:TPU:1, one launch (start us, length us, event | category | flops | bytes accessed | tf_op | source)
XLA Modules:
  0.0 49.1 jit_solution(11824669709585326858)
XLA Ops:
  0.0 2.2 %pack.1 = bf16[32,2,2176]{2,1,0:T(2,128)(2,1)} custom-call(s32[8]{0:T(128)} %shift_ref.1, bf16[32,8,2048]{2,1,0:T(8,128)(2,1)} %x_ref.1), custom_call_target="tpu_custom_call" | custom-call | flops 70000000 | bytes 1500000 | tf_op jit(solution)/shard_map/pack/pallas_call | solution.py:104
  2.2 13.5 %all-to-all-start = ((bf16[32,2,2176]{2,1,0:T(2,128)(2,1)}), bf16[32,2,2176]{2,1,0:T(2,128)(2,1)S(1)}, u32[]{:S(2)}, u32[]{:S(2)}) async-start(bf16[32,2,2176]{2,1,0:T(2,128)(2,1)} %pack.1), calls=%async_computation | async-start | bytes 557056 | tf_op jit(solution)/shard_map/all_to_all | solution.py:623
  15.7 0.0 copy-start
  15.7 0.0 copy-start.1
  15.7 0.0 copy-start.2
  15.7 0.0 copy-start.3
  15.7 0.6 %prepare.1 = (bf16[512,2048]{1,0:T(8,128)(2,1)S(1)}, f32[80,128]{1,0:T(8,128)S(1)}) custom-call(), custom_call_target="tpu_custom_call" | custom-call | flops 20000000 | bytes 4000000 | tf_op jit(solution)/shard_map/prepare/pallas_call | solution.py:202
  16.3 11.5 %all-to-all-done.refs_0_ = bf16[32,2,2176]{2,1,0:T(2,128)(2,1)S(1)} async-done(((bf16[32,2,2176]{2,1,0:T(2,128)(2,1)}), bf16[32,2,2176]{2,1,0:T(2,128)(2,1)S(1)}, u32[]{:S(2)}, u32[]{:S(2)}) %all-to-all-start) | async-done | bytes 278560 | tf_op jit(solution)/shard_map/all_to_all | solution.py:623
  27.8 10.1 %backproject.1.after_ref = bf16[4,8,2048]{2,1,0:T(8,128)(2,1)} custom-call(bf16[32,2,2176]{2,1,0:T(2,128)(2,1)S(1)} %all-to-all-done.refs_0_, f32[80,128]{1,0:T(8,128)S(1)} %get-tuple-element.11.refs_1_, bf16[512,2048]{1,0:T(8,128)(2,1)S(1)} %get-tuple-element.12.refs_2_), custom_call_target="tpu_custom_call" | custom-call | flops 1000000000 | bytes 6000000 | tf_op jit(solution)/shard_map/backproject/pallas_call | solution.py:527
  37.9 5.7 %all-to-all-start.1 = ((bf16[4,8,2048]{2,1,0:T(8,128)(2,1)}), bf16[4,8,2048]{2,1,0:T(8,128)(2,1)S(1)}, u32[]{:S(2)}, u32[]{:S(2)}) async-start(bf16[4,8,2048]{2,1,0:T(8,128)(2,1)} %backproject.1.after_ref), calls=%async_computation.1 | async-start | bytes 262144 | tf_op jit(solution)/shard_map/all_to_all | solution.py:628
  43.6 0.0 copy-done
  43.6 0.0 copy-done.1
  43.6 0.0 copy-done.2
  43.6 0.0 copy-done.3
  43.6 1.1 %weights.1 = (bf16[192,72]{1,0:T(8,128)(2,1)S(1)}, f32[192,1]{1,0:T(8,128)S(1)}, bf16[3,128,192]{2,1,0:T(8,128)(2,1)S(1)}, f32[128,1]{1,0:T(8,128)S(1)}) custom-call(bf16[4,8,2048]{2,1,0:T(8,128)(2,1)} %backproject.1.after_ref, f32[9,32]{1,0:T(8,128)S(1)} %copy-done.1, f32[1,32]{1,0:T(1,128)S(1)} %bitcast.2, bf16[32,288]{1,0:T(8,128)(2,1)S(1)} %copy-done, ...), custom_call_target="tpu_custom_call" | custom-call | flops 20000000 | bytes 1000000 | tf_op jit(solution)/shard_map/weights/pallas_call | solution.py:218
  44.7 2.5 %all-to-all-done.1.refs_0_ = bf16[4,8,2048]{2,1,0:T(8,128)(2,1)S(1)} async-done(((bf16[4,8,2048]{2,1,0:T(8,128)(2,1)}), bf16[4,8,2048]{2,1,0:T(8,128)(2,1)S(1)}, u32[]{:S(2)}, u32[]{:S(2)}) %all-to-all-start.1) | async-done | bytes 131104 | tf_op jit(solution)/shard_map/all_to_all | solution.py:628
  47.2 1.9 %layers.1 = bf16[1,32,4,2048]{3,2,1,0:T(4,128)(2,1)} custom-call(bf16[4,8,2048]{2,1,0:T(8,128)(2,1)S(1)} %all-to-all-done.1.refs_0_, bf16[192,72]{1,0:T(8,128)(2,1)S(1)} %get-tuple-element.13.refs_1_, f32[192,1]{1,0:T(8,128)S(1)} %get-tuple-element.14.refs_2_, bf16[3,128,192]{2,1,0:T(8,128)(2,1)S(1)} %get-tuple-element.15.refs_3_, ...), custom_call_target="tpu_custom_call" | custom-call | flops 500000000 | bytes 1000000 | tf_op jit(solution)/shard_map/layers/pallas_call | solution.py:600
Async XLA Ops:
  2.2 25.6 %all-to-all-start = ((bf16[32,2,2176]{2,1,0:T(2,128)(2,1)}), bf16[32,2,2176]{2,1,0:T(2,128)(2,1)S(1)}, u32[]{:S(2)}, u32[]{:S(2)}) async-start(bf16[32,2,2176]{2,1,0:T(2,128)(2,1)} %pack.1), calls=%async_computation | async-start | bytes 557056 | tf_op jit(solution)/shard_map/all_to_all | solution.py:623
  15.7 27.9 %copy-start = (bf16[32,288]{1,0:T(8,128)(2,1)S(1)}, bf16[32,288]{1,0:T(8,128)(2,1)}, u32[]{:S(2)}) copy-start(bf16[32,288]{1,0:T(8,128)(2,1)} %conv_two_ref.1) | copy-start | bytes 55300
  15.7 27.9 %copy-start.1 = (f32[9,32]{1,0:T(8,128)S(1)}, f32[9,32]{1,0:T(8,128)}, u32[]{:S(2)}) copy-start(f32[9,32]{1,0:T(8,128)} %conv_one_ref.1) | copy-start | bytes 3460
  15.7 27.9 %copy-start.2 = (f32[32]{0:T(128)S(1)}, f32[32]{0:T(128)}, u32[]{:S(2)}) copy-start(f32[32]{0:T(128)} %param.9) | copy-start | bytes 388
  15.7 27.9 %copy-start.3 = (f32[32]{0:T(128)S(1)}, f32[32]{0:T(128)}, u32[]{:S(2)}) copy-start(f32[32]{0:T(128)} %param.11) | copy-start | bytes 388
  37.9 9.3 %all-to-all-start.1 = ((bf16[4,8,2048]{2,1,0:T(8,128)(2,1)}), bf16[4,8,2048]{2,1,0:T(8,128)(2,1)S(1)}, u32[]{:S(2)}, u32[]{:S(2)}) async-start(bf16[4,8,2048]{2,1,0:T(8,128)(2,1)} %backproject.1.after_ref), calls=%async_computation.1 | async-start | bytes 262144 | tf_op jit(solution)/shard_map/all_to_all | solution.py:628
